TPU v7x, 1024 devices: a whole 4x8x16 slice. The times are simulated.
1024 devices in a mesh: node: 32 (over z, core), local: 32 (over y, x).
Axes of the slice: x: 4, y: 8, z: 16, core: 2. Of those that a mesh axis runs over, the one named last changes fastest.
Arguments:
- tokens: bfloat16 [8192, 3584], P(('node', 'local')), may hold values from -6 to 6
- expert_ids: int32 [8192, 4], P(('node', 'local')), may hold values from 0 to 127, as said below
- combine_codes: int32 [8192, 4], P(('node', 'local')), may hold values from 1 to 16
- gate_weight: bfloat16 [1024, 3584, 128], P(('node', 'local')), may hold values from -0.09375 to 0.09375
- up_weight: bfloat16 [1024, 3584, 128], P(('node', 'local')), may hold values from -0.09375 to 0.09375
- down_weight: bfloat16 [1024, 128, 3584], P(('node', 'local')), may hold values from -0.1875 to 0.1875
Outputs:
- moe_out: bfloat16 [8192, 3584], P(('node', 'local'))
Inputs may be any that keep to these rules, and one draw needn't show every extreme that they name: `expert_ids`: expert e belongs to node group e // 4. A token never names two experts of one node group. The 4 ids of each block of 8 rows (the rows of one device) name every node group exactly 1 times. Over all rows r with one value of (r // 8) % 32, no expert is named more than 16 times, and in every node group some expert is named exactly that often.
All inputs are finite; a program needn't handle non-finite values.
Results may differ from a plain program's by a relative error of at most 0.011.
Values may be sent and summed in bfloat16 or wider, within the bound.
No kernel may reach another device: no remote copies, remote signals or barrier semaphores. Data moves between devices by JAX's collectives and lax.ppermute only.
A program may use at most 32 MiB of HBM per device.

v0:
```python
import jax
import jax.numpy as jnp
from jax import lax
from jax.sharding import Mesh
from jax.sharding import PartitionSpec as P

TOP = 4
EXP_NODE = 4
NODE = ("node_0", "node_1")
NODE_LOCAL = ("node_0", "node_1", "local")


def in_blocks(value, dim, count):
    before, after = (value.shape[:dim], value.shape[dim + 1 :])
    return jnp.moveaxis(value.reshape(*before, count, -1, *after), dim, 0)


def in_order(tiles, dim):
    tiles = jnp.moveaxis(tiles, 0, dim)
    lengths = tiles.shape
    return tiles.reshape(*lengths[:dim], lengths[dim] * lengths[dim + 1], *lengths[dim + 2 :])


def turned_blocks(tiles, axes, turns):
    lengths = [lax.axis_size(a) for a in axes]
    tiles = tiles.reshape(*lengths, *tiles.shape[1:])
    for k in turns:
        tiles = lax.all_to_all(tiles, axes[k], split_axis=k, concat_axis=k, tiled=True)
    return tiles.reshape(-1, *tiles.shape[len(axes) :])


def exchange_by_chip(value, groups, turns, split_dim, concat_dim):
    count = lax.axis_size(groups[0]) * lax.axis_size(groups[1])
    tiles = in_blocks(value, split_dim, count)
    return in_order(turned_blocks(tiles, groups, turns), concat_dim)


def rank_within(labels, count):
    marks = (labels[:, None] == jnp.arange(count, dtype=jnp.int32)[None, :]).astype(jnp.int32)
    before = jnp.cumsum(marks, axis=0) - marks
    return jnp.sum(before * marks, axis=1)


def onehot_rows(targets, count):
    return targets[None, :] == jnp.arange(count, dtype=jnp.int32)[:, None]


def body(tokens, expert_ids, combine_codes, gate_weight, up_weight, down_weight):
    node_count = lax.axis_size(NODE)
    local_count = lax.axis_size("local")
    experts_here = EXP_NODE
    slices = local_count // experts_here
    token_count, width = tokens.shape
    route_count = token_count * TOP
    per_node = route_count // node_count
    capacity = min(route_count, 2 * route_count // experts_here)
    flat_ids = expert_ids.reshape(route_count)
    target_node = flat_ids // experts_here
    member = flat_ids % experts_here
    slot = target_node * per_node + rank_within(target_node, node_count)
    select = onehot_rows(slot, route_count)
    route_token = jnp.arange(route_count, dtype=jnp.int32) // TOP
    slot_token = jnp.sum(jnp.where(select, route_token[None, :], 0), axis=1)
    slot_member = jnp.sum(jnp.where(select, member[None, :], 0), axis=1)
    pick = (slot_token[:, None] == jnp.arange(token_count, dtype=jnp.int32)[None, :]).astype(
        jnp.bfloat16
    )
    outgoing = jnp.dot(pick, tokens, preferred_element_type=jnp.float32).astype(jnp.bfloat16)
    outgoing = outgoing.reshape(node_count, per_node, width)
    arrived, arrived_member = (
        lax.all_to_all(outgoing, NODE, split_axis=0, concat_axis=0, tiled=True),
        lax.all_to_all(
            slot_member.reshape(node_count, per_node), NODE, split_axis=0, concat_axis=0, tiled=True
        ),
    )
    arrived = arrived.reshape(route_count, width)
    arrived_member = arrived_member.reshape(route_count)
    place_slot = arrived_member * capacity + rank_within(arrived_member, experts_here)
    place = onehot_rows(place_slot, experts_here * capacity).astype(jnp.bfloat16)
    bundle = jnp.dot(place, arrived, preferred_element_type=jnp.float32).astype(jnp.bfloat16)
    bundle = bundle.reshape(experts_here, 1, capacity, width)
    forward_rows = jnp.broadcast_to(bundle, (experts_here, slices, capacity, width)).reshape(
        local_count, capacity, width
    )
    rows = lax.all_to_all(forward_rows, "local", split_axis=0, concat_axis=0, tiled=True)
    row_shape = rows.shape
    flat_rows = rows.reshape(-1, width)
    gate = jnp.dot(flat_rows, gate_weight[0], preferred_element_type=jnp.float32)
    upper = jnp.dot(flat_rows, up_weight[0], preferred_element_type=jnp.float32)
    hidden = (jax.nn.silu(gate) * upper).astype(jnp.bfloat16)
    projected = jnp.dot(hidden, down_weight[0], preferred_element_type=jnp.float32)
    partial_out = projected.astype(jnp.bfloat16).reshape(row_shape)
    returned = lax.all_to_all(partial_out, "local", split_axis=0, concat_axis=0, tiled=True)
    summed = jnp.sum(
        returned.astype(jnp.float32).reshape(experts_here, slices, capacity, width), axis=1
    )
    summed = summed.astype(jnp.bfloat16)
    results = jnp.dot(
        place.T, summed.reshape(experts_here * capacity, width), preferred_element_type=jnp.float32
    )
    results = results.astype(jnp.bfloat16).reshape(node_count, per_node, width)
    home = exchange_by_chip(results, ("node_0", "node_1"), (1, 0), 0, 0).reshape(route_count, width)
    route_out = jnp.dot(select.T.astype(jnp.bfloat16), home, preferred_element_type=jnp.float32)
    codes = combine_codes.astype(jnp.float32)
    weights = codes / jnp.sum(codes, axis=1, keepdims=True)
    mixed = jnp.sum(weights[:, :, None] * route_out.reshape(token_count, TOP, width), axis=1)
    return mixed.astype(jnp.bfloat16)


def solution(mesh):
    split = Mesh(mesh.devices.reshape(16, 2, mesh.shape["local"]), ("node_0", "node_1", "local"))
    in_specs = (
        P(NODE_LOCAL, None),
        P(NODE_LOCAL, None),
        P(NODE_LOCAL, None),
        P(NODE_LOCAL, None, None),
        P(NODE_LOCAL, None, None),
        P(NODE_LOCAL, None, None),
    )
    out_specs = P(NODE_LOCAL, None)
    return jax.shard_map(body, mesh=split, in_specs=in_specs, out_specs=out_specs, check_vma=False)
```

profile of v0, /device:TPU:8, one launch (start us, length us, event | category | flops | bytes accessed | tf_op | source)
XLA Modules:
  0.0 280.8 jit_solution(4756857837059465893)
XLA Ops:
  0.0 0.0 copy-start
  0.0 0.8 copy.29
  0.8 0.1 reshape.161
  0.9 0.1 fusion.19
  1.0 0.1 reduce_window_sum.22
  1.1 0.2 select_reduce_fusion.3
  1.3 0.1 select_reduce_fusion.2
  1.4 0.7 copy.35
  2.1 19.2 %all-to-all-start = ((s32[32,1,1]{2,1,0:T(1,128)}), s32[32,1,1]{2,1,0:T(1,128)S(1)}, u32[]{:S(2)}, u32[]{:S(2)}) async-start(s32[32,1,1]{2,1,0:T(1,128)} %copy.35), calls=%async_computation | async-start | bytes 32768 | tf_op jit(solution)/shard_map/all_to_all | solution.py:72
  21.2 1.1 fusion
  22.3 0.6 broadcast.167
  22.9 0.8 reduce.3
  23.7 0.7 reshape.173
  24.4 9.2 %all-to-all-done = s32[32,1,1]{2,1,0:T(1,128)S(1)} async-done(((s32[32,1,1]{2,1,0:T(1,128)}), s32[32,1,1]{2,1,0:T(1,128)S(1)}, u32[]{:S(2)}, u32[]{:S(2)}) %all-to-all-start) | async-done | bytes 160 | tf_op jit(solution)/shard_map/all_to_all | solution.py:72
  33.7 3.9 %all-to-all-start.1 = ((bf16[32,2,1792]{2,1,0:T(2,128)(2,1)}), bf16[32,2,1792]{2,1,0:T(2,128)(2,1)S(1)}, u32[]{:S(2)}, u32[]{:S(2)}) async-start(bf16[32,2,1792]{2,1,0:T(2,128)(2,1)} %reshape.173), calls=%async_computation.1 | async-start | bytes 458752 | tf_op jit(solution)/shard_map/all_to_all | solution.py:71
  37.5 0.7 reduce.1
  38.2 0.1 fusion.18
  38.3 0.1 reduce_window_sum.23
  38.3 0.2 select_reduce_fusion.1
  38.5 20.4 %all-to-all-done.1 = bf16[32,2,1792]{2,1,0:T(2,128)(2,1)S(1)} async-done(((bf16[32,2,1792]{2,1,0:T(2,128)(2,1)}), bf16[32,2,1792]{2,1,0:T(2,128)(2,1)S(1)}, u32[]{:S(2)}, u32[]{:S(2)}) %all-to-all-start.1) | async-done | bytes 229408 | tf_op jit(solution)/shard_map/all_to_all | solution.py:71
  58.9 0.2 reshape.174
  59.1 0.3 convolution_convert_fusion.1
  59.4 0.4 broadcast_in_dim.23
  59.8 0.0 copy-start.3
  59.8 94.0 %all_to_all.34 = bf16[32,16,3584]{2,1,0:T(8,128)(2,1)S(1)} all-to-all(bf16[32,16,3584]{2,1,0:T(8,128)(2,1)S(1)} %bitcast.36), channel_id=1, replica_groups=mesh['node_0'=16,'node_1'=2,'local'=32] {'local'}, dimensions={0} | all-to-all | bytes 7340032 | tf_op jit(solution)/shard_map/all_to_all | solution.py:85
  153.8 0.0 copy-start.1
  153.8 0.0 copy-start.2
  153.8 1.8 copy-done.1
  155.6 0.0 copy-done.3
  155.6 1.1 fusion.6
  156.7 0.0 copy-done
  156.8 0.0 copy-done.2
  156.8 7.8 %convolution_convert_fusion = bf16[512,3584]{1,0:T(8,128)(2,1)} fusion(bf16[512,3584]{1,0:T(8,128)(2,1)} %bitcast.34, bf16[1,128,3584]{2,1,0:T(8,128)(2,1)S(1)} %copy-done, bf16[1,3584,128]{2,1,0:T(8,128)(2,1)S(1)} %copy-done.2, f32[512,128]{1,0:T(8,128)S(1)} %fusion.6), kind=kOutput, calls=%fused_computation | convolution fusion | flops 941752320 | bytes 9437184 | tf_op jit(solution)/shard_map/dot_general | solution.py:91
  164.6 88.8 %all_to_all.35 = bf16[32,16,3584]{2,1,0:T(8,128)(2,1)S(1)} all-to-all(bf16[32,16,3584]{2,1,0:T(8,128)(2,1)} %bitcast.35), channel_id=1, replica_groups=mesh['node_0'=16,'node_1'=2,'local'=32] {'local'}, dimensions={0} | all-to-all | bytes 7340032 | tf_op jit(solution)/shard_map/all_to_all | solution.py:93
  253.4 0.0 copy-start.4
  253.4 0.5 bitcast_reduce_fusion
  253.9 0.3 convolution_convert_fusion.2
  254.2 0.1 reshape_reshape_reshape.6
  254.3 3.9 %all_to_all.36 = bf16[16,2,1,1,3584]{4,0,3,2,1:T(8,128)(2,1)S(1)} all-to-all(bf16[16,2,1,1,3584]{4,0,3,2,1:T(8,128)(2,1)S(1)} %copy.37), channel_id=1, replica_groups=mesh['node_0'=16,'node_1'=2,'local'=32] {'node_1'}, dimensions={1} | all-to-all | bytes 458752 | tf_op jit(solution)/shard_map/all_to_all | solution.py:28
  258.2 0.9 copy.38
  259.1 3.5 %all-to-all-start.5 = ((bf16[16,2,1,1,3584]{4,1,3,2,0:T(2,128)(2,1)}), bf16[16,2,1,1,3584]{4,1,3,2,0:T(2,128)(2,1)S(1)}, u32[]{:S(2)}, u32[]{:S(2)}) async-start(bf16[16,2,1,1,3584]{4,1,3,2,0:T(2,128)(2,1)} %copy.38), calls=%async_computation.5 | async-start | bytes 458752 | tf_op jit(solution)/shard_map/all_to_all | solution.py:28
  262.7 0.1 reduce_sum.67
  262.7 0.1 copy.34
  262.8 0.0 copy-done.4
  262.9 17.0 %all-to-all-done.5 = bf16[16,2,1,1,3584]{4,1,3,2,0:T(2,128)(2,1)S(1)} async-done(((bf16[16,2,1,1,3584]{4,1,3,2,0:T(2,128)(2,1)}), bf16[16,2,1,1,3584]{4,1,3,2,0:T(2,128)(2,1)S(1)}, u32[]{:S(2)}, u32[]{:S(2)}) %all-to-all-start.5) | async-done | bytes 229408 | tf_op jit(solution)/shard_map/all_to_all | solution.py:28
  279.9 0.1 reshape.170
  280.0 0.9 fusion.1
  (7 shorter events, 0.1 us)
Async XLA Ops:
  0.0 156.7 %copy-start = (bf16[1,128,3584]{2,1,0:T(8,128)(2,1)S(1)}, bf16[1,128,3584]{2,1,0:T(8,128)(2,1)}, u32[]{:S(2)}) copy-start(bf16[1,128,3584]{2,1,0:T(8,128)(2,1)} %param.11) | copy-start | bytes 2752516
  2.1 31.6 %all-to-all-start = ((s32[32,1,1]{2,1,0:T(1,128)}), s32[32,1,1]{2,1,0:T(1,128)S(1)}, u32[]{:S(2)}, u32[]{:S(2)}) async-start(s32[32,1,1]{2,1,0:T(1,128)} %copy.35), calls=%async_computation | async-start | bytes 32768 | tf_op jit(solution)/shard_map/all_to_all | solution.py:72
  33.7 25.3 %all-to-all-start.1 = ((bf16[32,2,1792]{2,1,0:T(2,128)(2,1)}), bf16[32,2,1792]{2,1,0:T(2,128)(2,1)S(1)}, u32[]{:S(2)}, u32[]{:S(2)}) async-start(bf16[32,2,1792]{2,1,0:T(2,128)(2,1)} %reshape.173), calls=%async_computation.1 | async-start | bytes 458752 | tf_op jit(solution)/shard_map/all_to_all | solution.py:71
  59.8 95.8 %copy-start.3 = (bf16[1,3584,128]{2,1,0:T(8,128)(2,1)S(1)}, bf16[1,3584,128]{2,1,0:T(8,128)(2,1)}, u32[]{:S(2)}) copy-start(bf16[1,3584,128]{2,1,0:T(8,128)(2,1)} %param.9) | copy-start | bytes 2752516
  153.8 1.8 copy-start.1
  153.8 2.9 %copy-start.2 = (bf16[1,3584,128]{2,1,0:T(8,128)(2,1)S(1)}, bf16[1,3584,128]{2,1,0:T(8,128)(2,1)}, u32[]{:S(2)}) copy-start(bf16[1,3584,128]{2,1,0:T(8,128)(2,1)} %param.10) | copy-start | bytes 2752516
  253.4 9.4 %copy-start.4 = (s32[8,4]{0,1:T(4,128)S(1)}, s32[8,4]{0,1:T(4,128)}, u32[]{:S(2)}) copy-start(s32[8,4]{0,1:T(4,128)} %param.8) | copy-start | bytes 388
  259.1 20.8 %all-to-all-start.5 = ((bf16[16,2,1,1,3584]{4,1,3,2,0:T(2,128)(2,1)}), bf16[16,2,1,1,3584]{4,1,3,2,0:T(2,128)(2,1)S(1)}, u32[]{:S(2)}, u32[]{:S(2)}) async-start(bf16[16,2,1,1,3584]{4,1,3,2,0:T(2,128)(2,1)} %copy.38), calls=%async_computation.5 | async-start | bytes 458752 | tf_op jit(solution)/shard_map/all_to_all | solution.py:28
where the time goes:
time: 282 us; the launch traced here: 281 us
  blocking collectives  187 us (66%)
  waiting for transfers between devices  46.6 us (17%)
  starting transfers between devices  26.5 us (9%)
  matrix products  11.4 us (4%)
  local copies, waits for them, and re-layouts  6.61 us (2%)
    all_to_all x1, blocking collectives, body(): lax.all_to_all(forward_rows, 'local', split_axis=0, concat_axis=0, tiled=...  94 us
    all_to_all x1, blocking collectives, body(): lax.all_to_all(partial_out, 'local', split_axis=0, concat_axis=0, tiled=T...  88.8 us
    all_to_all x1, waiting for transfers between devices, body(): lax.all_to_all(outgoing, NODE, split_axis=0, concat_axis=0, tiled=True)  20.4 us
    all_to_all x1, starting transfers between devices, body(): lax.all_to_all(slot_member.reshape(node_count, per_node), NODE, split_axi...  19.2 us
    all_to_all x1, waiting for transfers between devices, turned_blocks(): lax.all_to_all(tiles, axes[k], split_axis=k, concat_axis=k, tiled=True)  17 us
    all_to_all x1, waiting for transfers between devices, body(): lax.all_to_all(slot_member.reshape(node_count, per_node), NODE, split_axi...  9.23 us
    dot_general x1, matrix products, body(): jnp.dot(hidden, down_weight[0], preferred_element_type=jnp.float32)  7.81 us
  transfers between devices with their start and end apart: 3, of which 3 were waited for; matrix products, arithmetic and copies ran while one was open for 2% of the time, Pallas kernels for 0%

commit v1 on v0

v1 whole, which is shorter than its diff:
```python
import functools

import jax
import jax.numpy as jnp
from jax import lax
from jax.experimental import pallas as pl
from jax.experimental.pallas import tpu as pltpu
from jax.sharding import Mesh
from jax.sharding import PartitionSpec as P

TOP = 4
MEMBERS = 4
CAP = 16
LANES = 128
NODE = ("z", "core")
LOCAL = ("x", "y")
ALL = ("z", "core", "y", "x")
f32, bf16, i32 = jnp.float32, jnp.bfloat16, jnp.int32
VMEM = pl.BlockSpec(memory_space=pltpu.VMEM)
SMEM = pl.BlockSpec(memory_space=pltpu.SMEM)


def exchange(value, axes):
    return lax.all_to_all(value, axes, split_axis=0, concat_axis=0, tiled=True)


def shift(value, by, count):
    return lax.ppermute(value, "x", [(i, (i + by) % count) for i in range(count)])


def mix_kernel(ids_ref, codes_ref, mix_ref):
    codes = codes_ref[...].astype(f32)
    weights = codes / jnp.sum(codes, axis=0, keepdims=True)
    target = ids_ref[...] // MEMBERS
    node = lax.broadcasted_iota(i32, mix_ref.shape, 0)
    mix = jnp.zeros(mix_ref.shape, f32)
    for k in range(TOP):
        mix = mix + jnp.where(target[k : k + 1, :] == node, weights[k : k + 1, :], 0.0)
    mix_ref[...] = mix


def spread_kernel(slot_ref, spread_ref):
    row = lax.broadcasted_iota(i32, spread_ref.shape, 0)
    pair = spread_ref.shape[0] // (MEMBERS * CAP)
    wanted = row // (pair * CAP) * CAP + row % CAP
    spread_ref[...] = jnp.where(wanted == slot_ref[...], 1.0, 0.0).astype(bf16)


def share_kernel(xs, x_ref, rows_ref, *refs):
    weights, out_ref = refs[:-1], refs[-1]
    x = x_ref[0]
    per = out_ref.shape[0] // xs
    for k in range(xs):
        source = lax.rem(x - k + xs, xs)
        gate_at = pl.multiple_of(source * LANES, LANES)
        up_at = pl.multiple_of((source + xs) * LANES, LANES)
        for q in range(xs):
            part = jnp.dot(
                rows_ref[q * per : (q + 1) * per, :], weights[k][...], preferred_element_type=f32
            ).astype(bf16)
            out_ref[q * per : (q + 1) * per, pl.ds(gate_at, LANES)] = part[:, :LANES]
            out_ref[q * per : (q + 1) * per, pl.ds(up_at, LANES)] = part[:, LANES:]


def down_kernel(xs, x_ref, share_ref, w0_ref, w1_ref, w3_ref, w2a_ref, w2b_ref, out_ref, hid_ref):
    x = x_ref[0]
    both = share_ref[0].astype(f32)
    for q in range(1, xs):
        both = both + share_ref[q].astype(f32)
    units = xs * LANES
    hid_ref[...] = (jax.nn.silu(both[:, :units]) * both[:, units:]).astype(bf16)
    mine = [
        hid_ref[:, pl.ds(pl.multiple_of(lax.rem(x - k + xs, xs) * LANES, LANES), LANES)]
        for k in range(xs)
    ]
    half = LANES // 2
    step = 512
    for n in range(0, out_ref.shape[1], step):
        cols = slice(n, n + step)
        total = jnp.dot(mine[0], w0_ref[:, cols], preferred_element_type=f32)
        total += jnp.dot(mine[1], w1_ref[:, cols], preferred_element_type=f32)
        total += jnp.dot(mine[3], w3_ref[:, cols], preferred_element_type=f32)
        total += jnp.dot(mine[2][:, :half], w2a_ref[:, cols], preferred_element_type=f32)
        total += jnp.dot(mine[2][:, half:], w2b_ref[:, cols], preferred_element_type=f32)
        out_ref[:, cols] = total.astype(bf16)


def body(tokens, expert_ids, combine_codes, gate_weight, up_weight, down_weight):
    nodes = lax.axis_size("z") * lax.axis_size("core")
    ys, xs = lax.axis_size("y"), lax.axis_size("x")
    pair = ys // MEMBERS
    token_count, width = tokens.shape
    chunk = width // xs
    units = gate_weight.shape[2]
    x = lax.axis_index("x")
    x_arg = x.astype(i32)[None]

    target = expert_ids // MEMBERS
    member = expert_ids % MEMBERS
    named = target[None, :, :] == jnp.arange(nodes, dtype=i32)[:, None, None]
    pick = jnp.any(named, axis=2).astype(bf16)
    slot_member = jnp.sum(jnp.where(named, member[None], 0), axis=(1, 2))
    outgoing = jnp.dot(pick, tokens, preferred_element_type=f32).astype(bf16)
    tag = jnp.broadcast_to(slot_member.astype(bf16)[:, None, None], (nodes, 4, LANES))
    outgoing = jnp.concatenate([outgoing.reshape(nodes, width // LANES, LANES), tag], axis=1)
    arrived = exchange(outgoing, NODE)
    arrived_member = arrived[:, -1, 0].astype(i32)
    arrived = arrived[:, : width // LANES].reshape(nodes, width)

    mix = pl.pallas_call(
        mix_kernel,
        out_shape=jax.ShapeDtypeStruct((nodes, token_count), f32),
        in_specs=[VMEM, VMEM],
        out_specs=VMEM,
        compiler_params=pltpu.CompilerParams(vmem_limit_bytes=1 << 20),
    )(expert_ids.T, combine_codes.T)

    joined = jnp.concatenate([gate_weight[0], up_weight[0]], axis=1)
    blocks = []
    for k in range(xs):
        block = lax.dynamic_slice_in_dim(joined, lax.rem(x + k, xs) * chunk, chunk, 0)
        blocks.append(shift(block, k, xs) if k else block)
    down = down_weight[0]
    down_left = shift(down, 1, xs)
    down_right = shift(down, xs - 1, xs)
    half = units // 2
    down_far_a = shift(down_left[:half], 1, xs)
    down_far_b = shift(down_right[half:], xs - 1, xs)

    marks = arrived_member[:, None] == jnp.arange(MEMBERS, dtype=i32)[None, :]
    counts = marks.astype(i32)
    rank = jnp.sum((jnp.cumsum(counts, axis=0) - counts) * counts, axis=1)
    place_slot = arrived_member * CAP + rank
    place = (place_slot[None, :] == jnp.arange(MEMBERS * CAP, dtype=i32)[:, None]).astype(bf16)
    bundle = jnp.dot(place, arrived, preferred_element_type=f32).astype(bf16)
    bundle = bundle.reshape(MEMBERS, 1, CAP, xs, chunk).transpose(3, 0, 1, 2, 4)
    bundle = jnp.broadcast_to(bundle, (xs, MEMBERS, pair, CAP, chunk)).reshape(xs * ys, CAP, chunk)
    spread = pl.pallas_call(
        spread_kernel,
        out_shape=jax.ShapeDtypeStruct((ys * CAP, nodes), bf16),
        in_specs=[VMEM],
        out_specs=VMEM,
        compiler_params=pltpu.CompilerParams(vmem_limit_bytes=1 << 20),
    )(place_slot[None, :])
    rows = exchange(bundle, LOCAL).reshape(xs * ys * CAP, chunk)

    share = pl.pallas_call(
        functools.partial(share_kernel, xs),
        out_shape=jax.ShapeDtypeStruct((xs * ys * CAP, 2 * xs * units), bf16),
        in_specs=[SMEM] + [VMEM] * (1 + xs),
        out_specs=VMEM,
        compiler_params=pltpu.CompilerParams(vmem_limit_bytes=12 << 20),
        cost_estimate=pl.CostEstimate(flops=2 << 30, bytes_accessed=4 << 20, transcendentals=0),
    )(x_arg, rows, *blocks)
    share = exchange(share.reshape(xs, ys * CAP, 2 * xs * units), "x")
    partial_out = pl.pallas_call(
        functools.partial(down_kernel, xs),
        out_shape=jax.ShapeDtypeStruct((ys * CAP, width), bf16),
        in_specs=[SMEM] + [VMEM] * 6,
        out_specs=VMEM,
        scratch_shapes=[pltpu.VMEM((ys * CAP, xs * units), bf16)],
        compiler_params=pltpu.CompilerParams(vmem_limit_bytes=16 << 20),
        cost_estimate=pl.CostEstimate(flops=1 << 30, bytes_accessed=6 << 20, transcendentals=1 << 16),
    )(x_arg, share, down, down_left, down_right, down_far_a, down_far_b)
    returned = exchange(partial_out.reshape(ys, CAP, width), "y").reshape(ys * CAP, width)

    results = jnp.dot(spread.T, returned, preferred_element_type=f32).astype(bf16)
    home = exchange(results.reshape(nodes, width // LANES, LANES), NODE).reshape(nodes, width)

    mixed = lax.dot(mix.T, home.astype(f32), precision=lax.Precision.HIGHEST)
    return mixed.astype(bf16)


def solution(mesh):
    nodes, locals_ = mesh.shape["node"], mesh.shape["local"]
    split = Mesh(mesh.devices.reshape(nodes // 2, 2, locals_ // 4, 4), ALL)
    in_specs = (
        P(ALL, None),
        P(ALL, None),
        P(ALL, None),
        P(ALL, None, None),
        P(ALL, None, None),
        P(ALL, None, None),
    )

    return jax.shard_map(body, mesh=split, in_specs=in_specs, out_specs=P(ALL, None), check_vma=False)
```

time: 282 us -> 200 us (0.71)
  the two profiles are of different devices: /device:TPU:8 before, /device:TPU:2 now
where the time goes in v1:
time: 200 us; the launch traced here: 199 us
  waiting for transfers between devices  89.7 us (45%)
  starting transfers between devices  47.8 us (24%)
  blocking collectives  41.6 us (21%)
  local copies, waits for them, and re-layouts  10.5 us (5%)
  Pallas kernels  4.89 us (2%)
  other arithmetic  2.7 us (1%)
    all_to_all x4, waiting for transfers between devices, exchange(): return lax.all_to_all(value, axes, split_axis=0, concat_axis=0, tiled=True)  48.8 us
    all_to_all x1, blocking collectives, exchange(): return lax.all_to_all(value, axes, split_axis=0, concat_axis=0, tiled=True)  41.6 us
    ppermute x7, waiting for transfers between devices, shift(): lax.ppermute(value, 'x', [(i, (i + by) % count) for i in range(count)])  40.9 us
    all_to_all x4, starting transfers between devices, exchange(): return lax.all_to_all(value, axes, split_axis=0, concat_axis=0, tiled=True)  25.6 us
    ppermute x7, starting transfers between devices, shift(): lax.ppermute(value, 'x', [(i, (i + by) % count) for i in range(count)])  22.2 us
    unnamed x28, local copies, waits for them, and re-layouts  8.22 us
  transfers between devices with their start and end apart: 11, of which 7 were waited for; matrix products, arithmetic and copies ran while one was open for 0% of the time, Pallas kernels for 1%

profile of v1, /device:TPU:2, one launch (start us, length us, event | category | flops | bytes accessed | tf_op | source)
XLA Modules:
  0.0 199.3 jit_solution(1895548216167767785)
XLA Ops:
  0.0 0.7 add_select_fusion.1
  0.7 0.1 fusion.10
  0.8 0.1 select_reduce_fusion.1
  0.9 0.3 convolution_convert_fusion.2
  1.2 0.1 reshape.66
  1.3 0.1 broadcast_in_dim.22
  1.4 0.1 pad_maximum_fusion
  1.5 41.6 %all_to_all.25 = bf16[32,32,128]{2,1,0:T(8,128)(2,1)S(1)} all-to-all(bf16[32,32,128]{2,1,0:T(8,128)(2,1)S(1)} %pad_maximum_fusion), channel_id=1, replica_groups=mesh['z'=16,'core'=2,'y'=8,'x'=4] {'z','core'}, dimensions={0} | all-to-all | bytes 524288 | tf_op jit(solution)/shard_map/all_to_all | solution.py:24
  43.1 1.2 fusion.11
  44.3 0.1 fusion.9
  44.4 0.1 reduce_window_sum.11
  44.5 0.2 select_reduce_fusion
  44.7 0.3 convolution_convert_fusion
  44.9 0.1 reshape.68
  45.1 1.0 broadcast_in_dim.41
  46.1 10.4 %all-to-all-start.1 = ((bf16[32,16,896]{2,1,0:T(8,128)(2,1)}), bf16[32,16,896]{2,1,0:T(8,128)(2,1)S(1)}, u32[]{:S(2)}, u32[]{:S(2)}) async-start(bf16[32,16,896]{2,1,0:T(8,128)(2,1)} %bitcast.6), calls=%async_computation.1 | async-start | bytes 1835008 | tf_op jit(solution)/shard_map/all_to_all | solution.py:24
  56.6 0.2 fusion
  56.8 3.4 %collective-permute-start = (bf16[896,256]{1,0:T(8,128)(2,1)S(1)}, bf16[896,256]{1,0:T(8,128)(2,1)S(1)}, u32[]{:S(2)}, u32[]{:S(2)}) collective-permute-start(bf16[896,256]{1,0:T(8,128)(2,1)S(1)} %get-tuple-element.9), channel_id=1, source_target_pairs={{0,1},{1,2},{2,3},{3,0},{4,5},{5,6},{6,7},{7,4},{8,9},{9,10},{10,1... | collective-permute-start | bytes 1376264 | tf_op jit(solution)/shard_map/ppermute | solution.py:28
  60.2 2.7 %collective-permute-start.1 = (bf16[896,256]{1,0:T(8,128)(2,1)S(1)}, bf16[896,256]{1,0:T(8,128)(2,1)S(1)}, u32[]{:S(2)}, u32[]{:S(2)}) collective-permute-start(bf16[896,256]{1,0:T(8,128)(2,1)S(1)} %get-tuple-element.10), channel_id=1, source_target_pairs={{0,2},{1,3},{2,0},{3,1},{4,6},{5,7},{6,4},{7,5},{8,10},{9,11},{10,... | collective-permute-start | bytes 1376264 | tf_op jit(solution)/shard_map/ppermute | solution.py:28
  62.9 4.3 %collective-permute-start.2 = (bf16[896,256]{1,0:T(8,128)(2,1)S(1)}, bf16[896,256]{1,0:T(8,128)(2,1)S(1)}, u32[]{:S(2)}, u32[]{:S(2)}) collective-permute-start(bf16[896,256]{1,0:T(8,128)(2,1)S(1)} %get-tuple-element.7), channel_id=1, source_target_pairs={{0,3},{1,0},{2,1},{3,2},{4,7},{5,4},{6,5},{7,6},{8,11},{9,8},{10,9... | collective-permute-start | bytes 1376264 | tf_op jit(solution)/shard_map/ppermute | solution.py:28
  67.3 1.9 collective-permute-start.3
  69.2 3.9 %collective-permute-start.4 = (bf16[128,3584]{1,0:T(8,128)(2,1)}, bf16[128,3584]{1,0:T(8,128)(2,1)S(1)}, u32[]{:S(2)}, u32[]{:S(2)}) collective-permute-start(bf16[128,3584]{1,0:T(8,128)(2,1)} %bitcast.11.w0_ref), channel_id=1, source_target_pairs={{0,3},{1,0},{2,1},{3,2},{4,7},{5,4},{6,5},{7,6},{8,11},{9,8},{10,9... | collective-permute-start | bytes 2752520 | tf_op jit(solution)/shard_map/ppermute | solution.py:28
  73.1 14.6 %collective-permute-done.refs_1_ = bf16[896,256]{1,0:T(8,128)(2,1)S(1)} collective-permute-done((bf16[896,256]{1,0:T(8,128)(2,1)S(1)}, bf16[896,256]{1,0:T(8,128)(2,1)S(1)}, u32[]{:S(2)}, u32[]{:S(2)}) %collective-permute-start) | collective-permute-done | bytes 458784 | tf_op jit(solution)/shard_map/ppermute | solution.py:28
  87.8 0.8 copy-done.6
  88.5 0.8 copy-done.8
  89.3 2.5 %collective-permute-done.2.refs_3_ = bf16[896,256]{1,0:T(8,128)(2,1)S(1)} collective-permute-done((bf16[896,256]{1,0:T(8,128)(2,1)S(1)}, bf16[896,256]{1,0:T(8,128)(2,1)S(1)}, u32[]{:S(2)}, u32[]{:S(2)}) %collective-permute-start.2) | collective-permute-done | bytes 458784 | tf_op jit(solution)/shard_map/ppermute | solution.py:28
  91.9 0.8 copy-done.10
  92.7 1.0 copy-done.7
  93.7 1.0 copy-done.9
  94.7 1.0 copy-done.11
  95.7 1.3 shard_map.66
  97.0 1.0 copy-done.1
  98.0 4.8 %all-to-all-start.2 = ((bf16[4,128,1024]{2,1,0:T(8,128)(2,1)}), bf16[4,128,1024]{2,1,0:T(8,128)(2,1)S(1)}, u32[]{:S(2)}, u32[]{:S(2)}) async-start(bf16[4,128,1024]{2,1,0:T(8,128)(2,1)} %bitcast.32), calls=%async_computation.2 | async-start | bytes 2097152 | tf_op jit(solution)/shard_map/all_to_all | solution.py:24
  102.8 6.1 %collective-permute-done.3.w1_ref = bf16[128,3584]{1,0:T(8,128)(2,1)S(1)} collective-permute-done((bf16[128,3584]{1,0:T(8,128)(2,1)}, bf16[128,3584]{1,0:T(8,128)(2,1)S(1)}, u32[]{:S(2)}, u32[]{:S(2)}) %collective-permute-start.3) | collective-permute-done | bytes 917536 | tf_op jit(solution)/shard_map/ppermute | solution.py:28
  109.0 3.4 %collective-permute-start.5 = (bf16[64,3584]{1,0:T(8,128)(2,1)S(1)}, bf16[64,3584]{1,0:T(8,128)(2,1)S(1)}, u32[]{:S(2)}, u32[]{:S(2)}) collective-permute-start(bf16[64,3584]{1,0:T(8,128)(2,1)S(1)} %slice.18), channel_id=1, source_target_pairs={{0,1},{1,2},{2,3},{3,0},{4,5},{5,6},{6,7},{7,4},{8,9},{9,10},{10,1... | collective-permute-start | bytes 1376264 | tf_op jit(solution)/shard_map/ppermute | solution.py:28
  112.4 2.5 %collective-permute-start.6 = (bf16[64,3584]{1,0:T(8,128)(2,1)S(1)}, bf16[64,3584]{1,0:T(8,128)(2,1)S(1)}, u32[]{:S(2)}, u32[]{:S(2)}) collective-permute-start(bf16[64,3584]{1,0:T(8,128)(2,1)S(1)} %slice.19), channel_id=1, source_target_pairs={{0,3},{1,0},{2,1},{3,2},{4,7},{5,4},{6,5},{7,6},{8,11},{9,8},{10,9... | collective-permute-start | bytes 1376264 | tf_op jit(solution)/shard_map/ppermute | solution.py:28
  114.9 13.8 %collective-permute-done.5.w2a_ref = bf16[64,3584]{1,0:T(8,128)(2,1)S(1)} collective-permute-done((bf16[64,3584]{1,0:T(8,128)(2,1)S(1)}, bf16[64,3584]{1,0:T(8,128)(2,1)S(1)}, u32[]{:S(2)}, u32[]{:S(2)}) %collective-permute-start.5) | collective-permute-done | bytes 458784 | tf_op jit(solution)/shard_map/ppermute | solution.py:28
  128.7 3.8 %collective-permute-done.6.w2b_ref = bf16[64,3584]{1,0:T(8,128)(2,1)S(1)} collective-permute-done((bf16[64,3584]{1,0:T(8,128)(2,1)S(1)}, bf16[64,3584]{1,0:T(8,128)(2,1)S(1)}, u32[]{:S(2)}, u32[]{:S(2)}) %collective-permute-start.6) | collective-permute-done | bytes 458784 | tf_op jit(solution)/shard_map/ppermute | solution.py:28
  132.5 0.8 copy-done.2
  133.3 1.0 copy-done.3
  134.3 3.6 %shard_map.67 = bf16[128,3584]{1,0:T(8,128)(2,1)} custom-call(s32[1]{0:T(128)} %bitcast.3.x_ref, bf16[4,128,1024]{2,1,0:T(8,128)(2,1)S(1)} %all-to-all-done.2.share_ref, bf16[128,3584]{1,0:T(8,128)(2,1)} %bitcast.11.w0_ref, bf16[128,3584]{1,0:T(8,128)(2,1)S(1)} %collective-permute-done.3.w1_ref, bf16[128,3584]{1,0:T(8,128)(2,1)S(1)} %collective-permute-done.4.w3_ref, ...), custom_call_target="tpu_custom_call" | custom-call | flops 1073741824 | bytes 6291456 | tf_op jit(solution)/shard_map/pallas_call | solution.py:156
  137.9 6.5 %all-to-all-start.3 = ((bf16[8,16,3584]{2,1,0:T(8,128)(2,1)}), bf16[8,16,3584]{2,1,0:T(8,128)(2,1)S(1)}, u32[]{:S(2)}, u32[]{:S(2)}) async-start(bf16[8,16,3584]{2,1,0:T(8,128)(2,1)} %bitcast.12), calls=%async_computation.3 | async-start | bytes 1835008 | tf_op jit(solution)/shard_map/all_to_all | solution.py:24
  144.5 26.1 %all-to-all-done.3 = bf16[8,16,3584]{2,1,0:T(8,128)(2,1)S(1)} async-done(((bf16[8,16,3584]{2,1,0:T(8,128)(2,1)}), bf16[8,16,3584]{2,1,0:T(8,128)(2,1)S(1)}, u32[]{:S(2)}, u32[]{:S(2)}) %all-to-all-start.3) | async-done | bytes 917536 | tf_op jit(solution)/shard_map/all_to_all | solution.py:24
  170.6 0.3 convolution_convert_fusion.1
  170.8 0.9 reshape.74
  171.7 3.9 %all-to-all-start.4 = ((bf16[32,28,128]{2,1,0:T(8,128)(2,1)}), bf16[32,28,128]{2,1,0:T(8,128)(2,1)S(1)}, u32[]{:S(2)}, u32[]{:S(2)}) async-start(bf16[32,28,128]{2,1,0:T(8,128)(2,1)} %reshape.74), calls=%async_computation.4 | async-start | bytes 524288 | tf_op jit(solution)/shard_map/all_to_all | solution.py:24
  175.6 22.7 %all-to-all-done.4 = bf16[32,28,128]{2,1,0:T(8,128)(2,1)S(1)} async-done(((bf16[32,28,128]{2,1,0:T(8,128)(2,1)}), bf16[32,28,128]{2,1,0:T(8,128)(2,1)S(1)}, u32[]{:S(2)}, u32[]{:S(2)}) %all-to-all-start.4) | async-done | bytes 229408 | tf_op jit(solution)/shard_map/all_to_all | solution.py:24
  198.4 0.9 convolution_convert_fusion.3
  (31 shorter events, 0.2 us)
Async XLA Ops:
  0.0 0.9 copy-start
  46.1 10.4 %copy-start.12 = (bf16[1,3584,128]{2,1,0:T(8,128)(2,1)S(1)}, bf16[1,3584,128]{2,1,0:T(8,128)(2,1)}, u32[]{:S(2)}) copy-start(bf16[1,3584,128]{2,1,0:T(8,128)(2,1)} %param.9) | copy-start | bytes 2752516
  46.1 10.4 %copy-start.13 = (bf16[1,3584,128]{2,1,0:T(8,128)(2,1)S(1)}, bf16[1,3584,128]{2,1,0:T(8,128)(2,1)}, u32[]{:S(2)}) copy-start(bf16[1,3584,128]{2,1,0:T(8,128)(2,1)} %param.10) | copy-start | bytes 2752516
  46.1 46.5 %all-to-all-start.1 = ((bf16[32,16,896]{2,1,0:T(8,128)(2,1)}), bf16[32,16,896]{2,1,0:T(8,128)(2,1)S(1)}, u32[]{:S(2)}, u32[]{:S(2)}) async-start(bf16[32,16,896]{2,1,0:T(8,128)(2,1)} %bitcast.6), calls=%async_computation.1 | async-start | bytes 1835008 | tf_op jit(solution)/shard_map/all_to_all | solution.py:24
  56.8 31.0 %collective-permute-start = (bf16[896,256]{1,0:T(8,128)(2,1)S(1)}, bf16[896,256]{1,0:T(8,128)(2,1)S(1)}, u32[]{:S(2)}, u32[]{:S(2)}) collective-permute-start(bf16[896,256]{1,0:T(8,128)(2,1)S(1)} %get-tuple-element.9), channel_id=1, source_target_pairs={{0,1},{1,2},{2,3},{3,0},{4,5},{5,6},{6,7},{7,4},{8,9},{9,10},{10,1... | collective-permute-start | bytes 1376264 | tf_op jit(solution)/shard_map/ppermute | solution.py:28
  60.2 28.4 %collective-permute-start.1 = (bf16[896,256]{1,0:T(8,128)(2,1)S(1)}, bf16[896,256]{1,0:T(8,128)(2,1)S(1)}, u32[]{:S(2)}, u32[]{:S(2)}) collective-permute-start(bf16[896,256]{1,0:T(8,128)(2,1)S(1)} %get-tuple-element.10), channel_id=1, source_target_pairs={{0,2},{1,3},{2,0},{3,1},{4,6},{5,7},{6,4},{7,5},{8,10},{9,11},{10,... | collective-permute-start | bytes 1376264 | tf_op jit(solution)/shard_map/ppermute | solution.py:28
  62.9 29.0 %collective-permute-start.2 = (bf16[896,256]{1,0:T(8,128)(2,1)S(1)}, bf16[896,256]{1,0:T(8,128)(2,1)S(1)}, u32[]{:S(2)}, u32[]{:S(2)}) collective-permute-start(bf16[896,256]{1,0:T(8,128)(2,1)S(1)} %get-tuple-element.7), channel_id=1, source_target_pairs={{0,3},{1,0},{2,1},{3,2},{4,7},{5,4},{6,5},{7,6},{8,11},{9,8},{10,9... | collective-permute-start | bytes 1376264 | tf_op jit(solution)/shard_map/ppermute | solution.py:28
  67.3 41.7 %collective-permute-start.3 = (bf16[128,3584]{1,0:T(8,128)(2,1)}, bf16[128,3584]{1,0:T(8,128)(2,1)S(1)}, u32[]{:S(2)}, u32[]{:S(2)}) collective-permute-start(bf16[128,3584]{1,0:T(8,128)(2,1)} %bitcast.11.w0_ref), channel_id=1, source_target_pairs={{0,1},{1,2},{2,3},{3,0},{4,5},{5,6},{6,7},{7,4},{8,9},{9,10},{10,1... | collective-permute-start | bytes 2752520 | tf_op jit(solution)/shard_map/ppermute | solution.py:28
  69.2 43.1 %collective-permute-start.4 = (bf16[128,3584]{1,0:T(8,128)(2,1)}, bf16[128,3584]{1,0:T(8,128)(2,1)S(1)}, u32[]{:S(2)}, u32[]{:S(2)}) collective-permute-start(bf16[128,3584]{1,0:T(8,128)(2,1)} %bitcast.11.w0_ref), channel_id=1, source_target_pairs={{0,3},{1,0},{2,1},{3,2},{4,7},{5,4},{6,5},{7,6},{8,11},{9,8},{10,9... | collective-permute-start | bytes 2752520 | tf_op jit(solution)/shard_map/ppermute | solution.py:28
  87.8 0.8 copy-start.6
  88.5 0.8 copy-start.8
  91.9 0.8 copy-start.10
  92.7 1.0 copy-start.7
  93.7 1.0 copy-start.9
  94.7 1.0 copy-start.11
  97.0 1.0 copy-start.1
  98.0 35.3 %all-to-all-start.2 = ((bf16[4,128,1024]{2,1,0:T(8,128)(2,1)}), bf16[4,128,1024]{2,1,0:T(8,128)(2,1)S(1)}, u32[]{:S(2)}, u32[]{:S(2)}) async-start(bf16[4,128,1024]{2,1,0:T(8,128)(2,1)} %bitcast.32), calls=%async_computation.2 | async-start | bytes 2097152 | tf_op jit(solution)/shard_map/all_to_all | solution.py:24
  109.0 19.7 %collective-permute-start.5 = (bf16[64,3584]{1,0:T(8,128)(2,1)S(1)}, bf16[64,3584]{1,0:T(8,128)(2,1)S(1)}, u32[]{:S(2)}, u32[]{:S(2)}) collective-permute-start(bf16[64,3584]{1,0:T(8,128)(2,1)S(1)} %slice.18), channel_id=1, source_target_pairs={{0,1},{1,2},{2,3},{3,0},{4,5},{5,6},{6,7},{7,4},{8,9},{9,10},{10,1... | collective-permute-start | bytes 1376264 | tf_op jit(solution)/shard_map/ppermute | solution.py:28
  112.4 20.1 %collective-permute-start.6 = (bf16[64,3584]{1,0:T(8,128)(2,1)S(1)}, bf16[64,3584]{1,0:T(8,128)(2,1)S(1)}, u32[]{:S(2)}, u32[]{:S(2)}) collective-permute-start(bf16[64,3584]{1,0:T(8,128)(2,1)S(1)} %slice.19), channel_id=1, source_target_pairs={{0,3},{1,0},{2,1},{3,2},{4,7},{5,4},{6,5},{7,6},{8,11},{9,8},{10,9... | collective-permute-start | bytes 1376264 | tf_op jit(solution)/shard_map/ppermute | solution.py:28
  132.5 0.8 copy-start.2
  133.3 1.0 copy-start.3
  137.9 32.6 %all-to-all-start.3 = ((bf16[8,16,3584]{2,1,0:T(8,128)(2,1)}), bf16[8,16,3584]{2,1,0:T(8,128)(2,1)S(1)}, u32[]{:S(2)}, u32[]{:S(2)}) async-start(bf16[8,16,3584]{2,1,0:T(8,128)(2,1)} %bitcast.12), calls=%async_computation.3 | async-start | bytes 1835008 | tf_op jit(solution)/shard_map/all_to_all | solution.py:24
  170.6 5.0 %copy-start.4 = (s32[8,4]{0,1:T(4,128)S(1)}, s32[8,4]{0,1:T(4,128)}, u32[]{:S(2)}) copy-start(s32[8,4]{0,1:T(4,128)} %param.7) | copy-start | bytes 388
  170.6 5.0 %copy-start.5 = (s32[8,4]{0,1:T(4,128)S(1)}, s32[8,4]{0,1:T(4,128)}, u32[]{:S(2)}) copy-start(s32[8,4]{0,1:T(4,128)} %param.8) | copy-start | bytes 388
  171.7 26.7 %all-to-all-start.4 = ((bf16[32,28,128]{2,1,0:T(8,128)(2,1)}), bf16[32,28,128]{2,1,0:T(8,128)(2,1)S(1)}, u32[]{:S(2)}, u32[]{:S(2)}) async-start(bf16[32,28,128]{2,1,0:T(8,128)(2,1)} %reshape.74), calls=%async_computation.4 | async-start | bytes 524288 | tf_op jit(solution)/shard_map/all_to_all | solution.py:24

commit v2 on v1

v2 whole, which is shorter than its diff:
```python
import functools

import jax
import jax.numpy as jnp
from jax import lax
from jax.experimental import pallas as pl
from jax.experimental.pallas import tpu as pltpu
from jax.sharding import Mesh
from jax.sharding import PartitionSpec as P

TOP = 4
MEMBERS = 4
CAP = 16
LANES = 128
NODE = ("z", "core")
LOCAL = ("x", "y")
ALL = ("z", "core", "y", "x")
f32, bf16, i32 = jnp.float32, jnp.bfloat16, jnp.int32
VMEM = pl.BlockSpec(memory_space=pltpu.VMEM)
SMEM = pl.BlockSpec(memory_space=pltpu.SMEM)
HBM = pl.BlockSpec(memory_space=pltpu.HBM)
ANY = pl.BlockSpec(memory_space=pl.ANY)


def exchange(value, axes):
    return lax.all_to_all(value, axes, split_axis=0, concat_axis=0, tiled=True)


def shift(value, by, count):
    return lax.ppermute(value, "x", [(i, (i + by) % count) for i in range(count)])


def weight_kernel(codes_ref, out_ref):
    codes = codes_ref[...].astype(f32)
    out_ref[...] = codes / jnp.sum(codes, axis=0, keepdims=True)


def target_kernel(ids_ref, out_ref):
    out_ref[...] = ids_ref[...] // MEMBERS


def mix_kernel(target_ref, weights_ref, mix_ref):
    node = lax.broadcasted_iota(i32, mix_ref.shape, 0)
    mix = jnp.zeros(mix_ref.shape, f32)
    for k in range(TOP):
        mix = mix + jnp.where(target_ref[k : k + 1, :] == node, weights_ref[k : k + 1, :], 0.0)
    mix_ref[...] = mix


def split_kernel(mix_ref, out_ref):
    high = mix_ref[...].astype(bf16)
    out_ref[:, : mix_ref.shape[1]] = high
    out_ref[:, mix_ref.shape[1] :] = (mix_ref[...] - high.astype(f32)).astype(bf16)


def slot_kernel(tag_ref, place_ref, spread_ref):
    tag = tag_ref[:, tag_ref.shape[1] - 1, :].astype(f32)
    nodes = tag.shape[0]
    row = lax.broadcasted_iota(i32, (nodes, nodes), 0)
    column = lax.broadcasted_iota(i32, (nodes, nodes), 1)
    earlier = jnp.where(column < row, 1.0, 0.0).astype(bf16)
    slot = tag * CAP
    for m in range(MEMBERS):
        mark = jnp.where(tag == m, 1.0, 0.0)
        slot = slot + mark * jnp.dot(earlier, mark.astype(bf16), preferred_element_type=f32)
    lane = lax.broadcasted_iota(i32, spread_ref.shape, 1)
    pair = spread_ref.shape[1] // (MEMBERS * CAP)
    wanted = lane // (pair * CAP) * CAP + lane % CAP
    spread_ref[...] = jnp.where(slot == wanted.astype(f32), 1.0, 0.0).astype(bf16)
    place = jnp.where(slot == lane.astype(f32), 1.0, 0.0).astype(bf16)
    place_ref[...] = place[:, : place_ref.shape[1]]


def share_kernel(xs, x_ref, rows_ref, gate_ref, up_ref, *refs):
    others, (out_ref, rows, weights, out, row_sem, weight_sem, out_sem) = refs[: xs - 1], refs[xs - 1 :]
    x = x_ref[0]
    depth = weights.shape[1]
    mine = pl.ds(pl.multiple_of(x * depth, depth), depth)
    parts = 2
    per = out_ref.shape[0] // parts
    takes = [
        pltpu.make_async_copy(
            rows_ref.at[q * per : (q + 1) * per], rows.at[q * per : (q + 1) * per], row_sem.at[q]
        )
        for q in range(parts)
    ]
    loads = [[pltpu.make_async_copy(ref, weights.at[k + 1], weight_sem.at[k])] for k, ref in enumerate(others)]
    loads.append(
        [
            pltpu.make_async_copy(
                ref.at[0, mine], weights.at[0, :, i * LANES : (i + 1) * LANES], weight_sem.at[xs - 1 + i]
            )
            for i, ref in enumerate((gate_ref, up_ref))
        ]
    )
    takes[0].start()
    for load in loads:
        for copy in load:
            copy.start()
    takes[1].start()
    sends = []
    for q in range(parts):
        at = slice(q * per, (q + 1) * per)
        takes[q].wait()
        for load, k in zip(loads, (*range(1, xs), 0)):
            if q == 0:
                for copy in load:
                    copy.wait()
            source = lax.rem(x - k + xs, xs)
            gate_at = pl.multiple_of(source * LANES, LANES)
            up_at = pl.multiple_of((source + xs) * LANES, LANES)
            part = jnp.dot(rows[at, :], weights[k], preferred_element_type=f32).astype(bf16)
            out[at, pl.ds(gate_at, LANES)] = part[:, :LANES]
            out[at, pl.ds(up_at, LANES)] = part[:, LANES:]
        send = pltpu.make_async_copy(out.at[at], out_ref.at[at], out_sem.at[q])
        send.start()
        sends.append(send)
    for send in sends:
        send.wait()


def down_kernel(xs, step, x_ref, share_ref, w0_ref, w1_ref, w3_ref, w2a_ref, w2b_ref, out_ref, share, hid, weights, out, share_sem, weight_sem, out_sem):
    width = out_ref.shape[1]
    half = LANES // 2
    parts = 2
    take = pltpu.make_async_copy(share_ref, share, share_sem)
    take.start()
    loads = []
    for c in range(parts):
        cols = slice(c * (width // parts), (c + 1) * (width // parts))
        pieces = (
            (w0_ref, weights.at[0]),
            (w1_ref, weights.at[1]),
            (w3_ref, weights.at[3]),
            (w2a_ref, weights.at[2, :half]),
            (w2b_ref, weights.at[2, half:]),
        )
        load = [
            pltpu.make_async_copy(a.at[:, cols], b.at[:, cols], weight_sem.at[c * len(pieces) + i])
            for i, (a, b) in enumerate(pieces)
        ]
        for copy in load:
            copy.start()
        loads.append(load)
    x = x_ref[0]
    take.wait()
    both = share[0].astype(f32)
    for q in range(1, xs):
        both = both + share[q].astype(f32)
    units = xs * LANES
    hid[...] = (jax.nn.silu(both[:, :units]) * both[:, units:]).astype(bf16)
    mine = [
        hid[:, pl.ds(pl.multiple_of(lax.rem(x - k + xs, xs) * LANES, LANES), LANES)]
        for k in range(xs)
    ]
    sends = []
    for i, n in enumerate(range(0, width, step)):
        if n % (width // parts) == 0:
            for copy in loads[n // (width // parts)]:
                copy.wait()
        cols = slice(n, n + step)
        total = jnp.dot(mine[0], weights[0, :, cols], preferred_element_type=f32)
        for k in range(1, xs):
            total += jnp.dot(mine[k], weights[k, :, cols], preferred_element_type=f32)
        out[:, cols] = total.astype(bf16)
        send = pltpu.make_async_copy(out.at[:, cols], out_ref.at[:, cols], out_sem.at[i])
        send.start()
        sends.append(send)
    for send in sends:
        send.wait()


def held(arrays):
    return [pltpu.with_memory_space_constraint(a, pltpu.HBM) for a in arrays]


def small(kernel, shapes, *args, in_specs=None):
    many = isinstance(shapes, (tuple, list))
    return pl.pallas_call(
        kernel,
        out_shape=shapes,
        in_specs=in_specs or [VMEM] * len(args),
        out_specs=[VMEM] * len(shapes) if many else VMEM,
        compiler_params=pltpu.CompilerParams(vmem_limit_bytes=1 << 20),
    )(*args)


def body(tokens, expert_ids, combine_codes, gate_weight, up_weight, down_weight):
    nodes = lax.axis_size("z") * lax.axis_size("core")
    ys, xs = lax.axis_size("y"), lax.axis_size("x")
    pair = ys // MEMBERS
    token_count, width = tokens.shape
    chunk = width // xs
    units = gate_weight.shape[2]
    x = lax.axis_index("x")
    x_arg = x.astype(i32)[None]

    target = expert_ids // MEMBERS
    member = expert_ids % MEMBERS
    named = target[None, :, :] == jnp.arange(nodes, dtype=i32)[:, None, None]
    pick = jnp.any(named, axis=2).astype(bf16)
    slot_member = jnp.sum(jnp.where(named, member[None], 0), axis=(1, 2))
    outgoing = jnp.dot(pick, tokens, preferred_element_type=f32).astype(bf16)
    tag = jnp.broadcast_to(slot_member.astype(bf16)[:, None, None], (nodes, 4, LANES))
    outgoing = jnp.concatenate([outgoing.reshape(nodes, width // LANES, LANES), tag], axis=1)
    arrived = exchange(outgoing, NODE)
    weights = small(weight_kernel, jax.ShapeDtypeStruct((TOP, token_count), f32), combine_codes.T)

    joined = jnp.concatenate([gate_weight[0], up_weight[0]], axis=1)
    blocks = []
    for k in range(1, xs):
        block = lax.dynamic_slice_in_dim(joined, lax.rem(x + k, xs) * chunk, chunk, 0)
        blocks.append(shift(block, k, xs))
    down = down_weight[0]
    down_left = shift(down, 1, xs)
    down_right = shift(down, xs - 1, xs)
    half = units // 2
    down_far_a = shift(down_left[:half], 1, xs)
    down_far_b = shift(down_right[half:], xs - 1, xs)

    place, spread = pl.pallas_call(
        slot_kernel,
        grid=(1,),
        out_shape=(
            jax.ShapeDtypeStruct((nodes, MEMBERS * CAP), bf16),
            jax.ShapeDtypeStruct((nodes, ys * CAP), bf16),
        ),
        in_specs=[pl.BlockSpec((nodes, 8, LANES), lambda i: (0, arrived.shape[1] // 8 - 1, 0))],
        out_specs=(
            pl.BlockSpec((nodes, MEMBERS * CAP), lambda i: (0, 0)),
            pl.BlockSpec((nodes, ys * CAP), lambda i: (0, 0)),
        ),
        compiler_params=pltpu.CompilerParams(vmem_limit_bytes=1 << 20),
    )(arrived)
    arrived = arrived[:, : width // LANES].reshape(nodes, width)
    bundle = jnp.dot(place.T, arrived, preferred_element_type=f32).astype(bf16)
    bundle = bundle.reshape(MEMBERS, 1, CAP, xs, chunk).transpose(3, 0, 1, 2, 4)
    bundle = jnp.broadcast_to(bundle, (xs, MEMBERS, pair, CAP, chunk)).reshape(xs * ys, CAP, chunk)
    target = small(target_kernel, jax.ShapeDtypeStruct((TOP, token_count), i32), expert_ids.T)
    rows = exchange(bundle, LOCAL).reshape(xs * ys * CAP, chunk)

    share_shape = (xs * ys * CAP, 2 * xs * units)
    share = pl.pallas_call(
        functools.partial(share_kernel, xs),
        out_shape=pltpu.HBM(share_shape, bf16),
        in_specs=[SMEM, ANY] + [HBM] * (1 + xs),
        out_specs=HBM,
        scratch_shapes=[
            pltpu.VMEM((xs * ys * CAP, chunk), bf16),
            pltpu.VMEM((xs, chunk, 2 * units), bf16),
            pltpu.VMEM(share_shape, bf16),
            pltpu.SemaphoreType.DMA((2,)),
            pltpu.SemaphoreType.DMA((xs + 1,)),
            pltpu.SemaphoreType.DMA((2,)),
        ],
        compiler_params=pltpu.CompilerParams(vmem_limit_bytes=20 << 20),
        cost_estimate=pl.CostEstimate(flops=2 << 30, bytes_accessed=4 << 20, transcendentals=0),
    )(x_arg, rows, *held((gate_weight, up_weight, *blocks)))
    share = exchange(share.reshape(xs, ys * CAP, 2 * xs * units), "x")
    step = 256
    out_shape = (ys * CAP, width)
    partial_out = pl.pallas_call(
        functools.partial(down_kernel, xs, step),
        out_shape=pltpu.HBM(out_shape, bf16),
        in_specs=[SMEM, ANY] + [HBM] * 5,
        out_specs=HBM,
        scratch_shapes=[
            pltpu.VMEM((xs, ys * CAP, 2 * xs * units), bf16),
            pltpu.VMEM((ys * CAP, xs * units), bf16),
            pltpu.VMEM((xs, units, width), bf16),
            pltpu.VMEM(out_shape, bf16),
            pltpu.SemaphoreType.DMA(()),
            pltpu.SemaphoreType.DMA((10,)),
            pltpu.SemaphoreType.DMA((width // step,)),
        ],
        compiler_params=pltpu.CompilerParams(vmem_limit_bytes=20 << 20),
        cost_estimate=pl.CostEstimate(flops=1 << 30, bytes_accessed=6 << 20, transcendentals=1 << 16),
    )(x_arg, share, *held((down, down_left, down_right, down_far_a, down_far_b)))
    mix = small(
        mix_kernel, jax.ShapeDtypeStruct((nodes, token_count), f32), target, weights
    )
    returned = exchange(partial_out.reshape(ys, CAP, width), "y").reshape(ys * CAP, width)

    results = jnp.dot(spread, returned, preferred_element_type=f32).astype(bf16)
    terms = small(split_kernel, jax.ShapeDtypeStruct((nodes, 2 * token_count), bf16), mix)
    home = exchange(results.reshape(nodes, width // LANES, LANES), NODE).reshape(nodes, width)
    mixed = jnp.dot(terms.T, home, preferred_element_type=f32)
    return (mixed[:token_count] + mixed[token_count:]).astype(bf16)


def solution(mesh):
    nodes, locals_ = mesh.shape["node"], mesh.shape["local"]
    split = Mesh(mesh.devices.reshape(nodes // 2, 2, locals_ // 4, 4), ALL)
    in_specs = (
        P(ALL, None),
        P(ALL, None),
        P(ALL, None),
        P(ALL, None, None),
        P(ALL, None, None),
        P(ALL, None, None),
    )

    return jax.shard_map(body, mesh=split, in_specs=in_specs, out_specs=P(ALL, None), check_vma=False)
```

time: 200 us -> 197 us (0.985)
  blocking collectives: 41.6 us -> 74.3 us
  waiting for transfers between devices: 89.7 us -> 66 us
  local copies, waits for them, and re-layouts: 10.5 us -> 3.16 us
  starting transfers between devices: 47.8 us -> 41.3 us
  Pallas kernels: 4.89 us -> 8.66 us
    all_to_all x1 -> x2, blocking collectives: 41.6 us -> 74.3 us  [exchange(): return lax.all_to_all(value, axes, split_axis=0, concat_axis=0, tiled=True)]
    all_to_all x4 -> x3, waiting for transfers between devices: 48.8 us -> 22.6 us  [exchange(): return lax.all_to_all(value, axes, split_axis=0, concat_axis=0, tiled=True)]
    unnamed x28 -> x20, local copies, waits for them, and re-layouts: 8.22 us -> 0.85 us
    all_to_all x4 -> x3, starting transfers between devices: 25.6 us -> 19.1 us  [exchange(): return lax.all_to_all(value, axes, split_axis=0, concat_axis=0, tiled=True)]
    pallas_call x4 -> x7, Pallas kernels: 4.89 us -> 8.66 us  [the longest x1 4.55 us: body(): pl.pallas_call(functools.partial(share_kernel, xs), out_shape=pltpu.HBM(s...]
    ppermute x7, waiting for transfers between devices: 40.9 us -> 43.3 us  [shift(): lax.ppermute(value, 'x', [(i, (i + by) % count) for i in range(count)])]
  transfers between devices with their start and end apart: 11 -> 10, of which waited for: 7 -> 6; matrix products, arithmetic and copies ran while one was open for 0% -> 0% of each run, Pallas kernels for 1% -> 2%
where the time goes in v2:
time: 197 us; the launch traced here: 196 us
  blocking collectives  74.3 us (38%)
  waiting for transfers between devices  66 us (34%)
  starting transfers between devices  41.3 us (21%)
  Pallas kernels  8.66 us (4%)
  local copies, waits for them, and re-layouts  3.16 us (2%)
    all_to_all x2, blocking collectives, exchange(): return lax.all_to_all(value, axes, split_axis=0, concat_axis=0, tiled=True)  74.3 us
    ppermute x7, waiting for transfers between devices, shift(): lax.ppermute(value, 'x', [(i, (i + by) % count) for i in range(count)])  43.3 us
    all_to_all x3, waiting for transfers between devices, exchange(): return lax.all_to_all(value, axes, split_axis=0, concat_axis=0, tiled=True)  22.6 us
    ppermute x7, starting transfers between devices, shift(): lax.ppermute(value, 'x', [(i, (i + by) % count) for i in range(count)])  22.2 us
    all_to_all x3, starting transfers between devices, exchange(): return lax.all_to_all(value, axes, split_axis=0, concat_axis=0, tiled=True)  19.1 us
    pallas_call x1, Pallas kernels, body(): pl.pallas_call(functools.partial(share_kernel, xs), out_shape=pltpu.HBM(s...  4.55 us
  transfers between devices with their start and end apart: 10, of which 6 were waited for; matrix products, arithmetic and copies ran while one was open for 0% of the time, Pallas kernels for 2%

profile of v2, /device:TPU:2, one launch (start us, length us, event | category | flops | bytes accessed | tf_op | source)
XLA Modules:
  0.0 196.3 jit_solution(15376620869332436865)
XLA Ops:
  0.0 0.0 copy-start
  0.0 0.7 add_select_fusion.1
  0.7 0.1 fusion.9
  0.8 0.1 select_reduce_fusion
  0.9 0.0 copy-done
  0.9 0.3 convolution_convert_fusion.2
  1.2 0.1 reshape.35
  1.3 0.1 broadcast_in_dim.33
  1.4 0.1 pad_maximum_fusion
  1.5 41.6 %all_to_all.25.tag_ref = bf16[32,32,128]{2,1,0:T(8,128)(2,1)S(1)} all-to-all(bf16[32,32,128]{2,1,0:T(8,128)(2,1)S(1)} %pad_maximum_fusion), channel_id=1, replica_groups=mesh['z'=16,'core'=2,'y'=8,'x'=4] {'z','core'}, dimensions={0} | all-to-all | bytes 524288 | tf_op jit(solution)/shard_map/all_to_all | solution.py:26
  43.1 0.2 shard_map.68
  43.4 0.3 convolution_convert_fusion
  43.7 0.1 reshape.37
  43.8 0.1 copy.13
  43.8 1.0 broadcast_in_dim.36
  44.8 10.4 %all-to-all-start.1 = ((bf16[32,16,896]{2,1,0:T(8,128)(2,1)}), bf16[32,16,896]{2,1,0:T(8,128)(2,1)S(1)}, u32[]{:S(2)}, u32[]{:S(2)}) async-start(bf16[32,16,896]{2,1,0:T(8,128)(2,1)} %bitcast.5), calls=%async_computation.1 | async-start | bytes 1835008 | tf_op jit(solution)/shard_map/all_to_all | solution.py:26
  55.3 0.0 copy-done.5
  55.3 0.0 copy-done.6
  55.3 0.2 fusion
  55.5 3.4 %collective-permute-start = (bf16[896,256]{1,0:T(8,128)(2,1)S(1)}, bf16[896,256]{1,0:T(8,128)(2,1)S(1)}, u32[]{:S(2)}, u32[]{:S(2)}) collective-permute-start(bf16[896,256]{1,0:T(8,128)(2,1)S(1)} %get-tuple-element.10), channel_id=1, source_target_pairs={{0,1},{1,2},{2,3},{3,0},{4,5},{5,6},{6,7},{7,4},{8,9},{9,10},{10,1... | collective-permute-start | bytes 1376264 | tf_op jit(solution)/shard_map/ppermute | solution.py:30
  58.8 2.7 %collective-permute-start.1 = (bf16[896,256]{1,0:T(8,128)(2,1)S(1)}, bf16[896,256]{1,0:T(8,128)(2,1)S(1)}, u32[]{:S(2)}, u32[]{:S(2)}) collective-permute-start(bf16[896,256]{1,0:T(8,128)(2,1)S(1)} %get-tuple-element.11), channel_id=1, source_target_pairs={{0,2},{1,3},{2,0},{3,1},{4,6},{5,7},{6,4},{7,5},{8,10},{9,11},{10,... | collective-permute-start | bytes 1376264 | tf_op jit(solution)/shard_map/ppermute | solution.py:30
  61.6 4.3 %collective-permute-start.2 = (bf16[896,256]{1,0:T(8,128)(2,1)S(1)}, bf16[896,256]{1,0:T(8,128)(2,1)}, u32[]{:S(2)}, u32[]{:S(2)}) collective-permute-start(bf16[896,256]{1,0:T(8,128)(2,1)S(1)} %get-tuple-element.9), channel_id=1, source_target_pairs={{0,3},{1,0},{2,1},{3,2},{4,7},{5,4},{6,5},{7,6},{8,11},{9,8},{10,9... | collective-permute-start | bytes 1376264 | tf_op jit(solution)/shard_map/ppermute | solution.py:30
  65.9 1.9 collective-permute-start.3
  67.9 3.9 %collective-permute-start.4 = (bf16[128,3584]{1,0:T(8,128)(2,1)}, bf16[128,3584]{1,0:T(8,128)(2,1)S(1)}, u32[]{:S(2)}, u32[]{:S(2)}) collective-permute-start(bf16[128,3584]{1,0:T(8,128)(2,1)} %bitcast.10.w0_ref), channel_id=1, source_target_pairs={{0,3},{1,0},{2,1},{3,2},{4,7},{5,4},{6,5},{7,6},{8,11},{9,8},{10,9... | collective-permute-start | bytes 2752520 | tf_op jit(solution)/shard_map/ppermute | solution.py:30
  71.8 14.6 %collective-permute-done.refs_0_ = bf16[896,256]{1,0:T(8,128)(2,1)S(1)} collective-permute-done((bf16[896,256]{1,0:T(8,128)(2,1)S(1)}, bf16[896,256]{1,0:T(8,128)(2,1)S(1)}, u32[]{:S(2)}, u32[]{:S(2)}) %collective-permute-start) | collective-permute-done | bytes 458784 | tf_op jit(solution)/shard_map/ppermute | solution.py:30
  86.4 0.0 collective-permute-done.1.refs_1_
  86.4 0.8 copy-done.9
  87.3 3.4 %collective-permute-done.2.refs_2_ = bf16[896,256]{1,0:T(8,128)(2,1)} collective-permute-done((bf16[896,256]{1,0:T(8,128)(2,1)S(1)}, bf16[896,256]{1,0:T(8,128)(2,1)}, u32[]{:S(2)}, u32[]{:S(2)}) %collective-permute-start.2) | collective-permute-done | bytes 458784 | tf_op jit(solution)/shard_map/ppermute | solution.py:30
  90.7 0.0 all-to-all-done.1
  90.7 4.6 %shard_map.69 = bf16[512,1024]{1,0:T(8,128)(2,1)} custom-call(s32[1]{0:T(128)} %bitcast.2.x_ref, bf16[512,896]{1,0:T(8,128)(2,1)S(1)} %bitcast.30, bf16[1,3584,128]{2,1,0:T(8,128)(2,1)} %gate_ref.1, bf16[1,3584,128]{2,1,0:T(8,128)(2,1)} %up_ref.1, bf16[896,256]{1,0:T(8,128)(2,1)} %copy-done.8, bf16[896,256]{1,0:T(8,128)(2,1)} %copy-done.9, ...), custom_call_target="tpu_custom_call" | custom-call | flops 2147483648 | bytes 4194304 | tf_op jit(solution)/shard_map/pallas_call | solution.py:243
  95.2 4.8 %all-to-all-start.2 = ((bf16[4,128,1024]{2,1,0:T(8,128)(2,1)}), bf16[4,128,1024]{2,1,0:T(8,128)(2,1)S(1)}, u32[]{:S(2)}, u32[]{:S(2)}) async-start(bf16[4,128,1024]{2,1,0:T(8,128)(2,1)} %bitcast.36), calls=%async_computation.2 | async-start | bytes 2097152 | tf_op jit(solution)/shard_map/all_to_all | solution.py:26
  100.1 7.5 %collective-permute-done.3.w1_ref = bf16[128,3584]{1,0:T(8,128)(2,1)S(1)} collective-permute-done((bf16[128,3584]{1,0:T(8,128)(2,1)}, bf16[128,3584]{1,0:T(8,128)(2,1)S(1)}, u32[]{:S(2)}, u32[]{:S(2)}) %collective-permute-start.3) | collective-permute-done | bytes 917536 | tf_op jit(solution)/shard_map/ppermute | solution.py:30
  107.6 3.4 %collective-permute-start.5 = (bf16[64,3584]{1,0:T(8,128)(2,1)S(1)}, bf16[64,3584]{1,0:T(8,128)(2,1)S(1)}, u32[]{:S(2)}, u32[]{:S(2)}) collective-permute-start(bf16[64,3584]{1,0:T(8,128)(2,1)S(1)} %slice.21), channel_id=1, source_target_pairs={{0,1},{1,2},{2,3},{3,0},{4,5},{5,6},{6,7},{7,4},{8,9},{9,10},{10,1... | collective-permute-start | bytes 1376264 | tf_op jit(solution)/shard_map/ppermute | solution.py:30
  111.0 0.0 collective-permute-done.4.w3_ref
  111.1 2.5 %collective-permute-start.6 = (bf16[64,3584]{1,0:T(8,128)(2,1)S(1)}, bf16[64,3584]{1,0:T(8,128)(2,1)}, u32[]{:S(2)}, u32[]{:S(2)}) collective-permute-start(bf16[64,3584]{1,0:T(8,128)(2,1)S(1)} %slice.22), channel_id=1, source_target_pairs={{0,3},{1,0},{2,1},{3,2},{4,7},{5,4},{6,5},{7,6},{8,11},{9,8},{10,9... | collective-permute-start | bytes 1376264 | tf_op jit(solution)/shard_map/ppermute | solution.py:30
  113.6 13.8 %collective-permute-done.5.w2a_ref = bf16[64,3584]{1,0:T(8,128)(2,1)S(1)} collective-permute-done((bf16[64,3584]{1,0:T(8,128)(2,1)S(1)}, bf16[64,3584]{1,0:T(8,128)(2,1)S(1)}, u32[]{:S(2)}, u32[]{:S(2)}) %collective-permute-start.5) | collective-permute-done | bytes 458784 | tf_op jit(solution)/shard_map/ppermute | solution.py:30
  127.3 4.0 %collective-permute-done.6.w2b_ref = bf16[64,3584]{1,0:T(8,128)(2,1)} collective-permute-done((bf16[64,3584]{1,0:T(8,128)(2,1)S(1)}, bf16[64,3584]{1,0:T(8,128)(2,1)}, u32[]{:S(2)}, u32[]{:S(2)}) %collective-permute-start.6) | collective-permute-done | bytes 458784 | tf_op jit(solution)/shard_map/ppermute | solution.py:30
  131.3 0.0 all-to-all-done.2.share_ref
  131.3 0.0 copy-done.7
  131.3 3.7 %shard_map.70 = bf16[128,3584]{1,0:T(8,128)(2,1)} custom-call(s32[1]{0:T(128)} %bitcast.2.x_ref, bf16[4,128,1024]{2,1,0:T(8,128)(2,1)S(1)} %all-to-all-done.2.share_ref, bf16[128,3584]{1,0:T(8,128)(2,1)} %bitcast.10.w0_ref, bf16[128,3584]{1,0:T(8,128)(2,1)} %copy-done.3, bf16[128,3584]{1,0:T(8,128)(2,1)} %copy-done.4, bf16[64,3584]{1,0:T(8,128)(2,1)} %copy-done.7, ...), custom_call_target="tpu_custom_call" | custom-call | flops 1073741824 | bytes 6291456 | tf_op jit(solution)/shard_map/pallas_call | solution.py:262
  135.1 32.6 %all_to_all.26 = bf16[8,16,3584]{2,1,0:T(8,128)(2,1)S(1)} all-to-all(bf16[8,16,3584]{2,1,0:T(8,128)(2,1)} %bitcast.34), channel_id=1, replica_groups=mesh['z'=16,'core'=2,'y'=8,'x'=4] {'y'}, dimensions={0} | all-to-all | bytes 1835008 | tf_op jit(solution)/shard_map/all_to_all | solution.py:26
  167.7 0.2 convolution_convert_fusion.1
  168.0 0.8 reshape.43
  168.8 3.9 %all-to-all-start.4 = ((bf16[32,28,128]{2,1,0:T(8,128)(2,1)}), bf16[32,28,128]{2,1,0:T(8,128)(2,1)S(1)}, u32[]{:S(2)}, u32[]{:S(2)}) async-start(bf16[32,28,128]{2,1,0:T(8,128)(2,1)} %reshape.43), calls=%async_computation.4 | async-start | bytes 524288 | tf_op jit(solution)/shard_map/all_to_all | solution.py:26
  172.8 0.1 shard_map.67
  172.9 22.6 %all-to-all-done.4 = bf16[32,28,128]{2,1,0:T(8,128)(2,1)S(1)} async-done(((bf16[32,28,128]{2,1,0:T(8,128)(2,1)}), bf16[32,28,128]{2,1,0:T(8,128)(2,1)S(1)}, u32[]{:S(2)}, u32[]{:S(2)}) %all-to-all-start.4) | async-done | bytes 229408 | tf_op jit(solution)/shard_map/all_to_all | solution.py:26
  195.5 0.2 fusion.3
  195.7 0.6 fusion.8
  (20 shorter events, 0.1 us)
Async XLA Ops:
  0.0 0.9 copy-start
  44.8 10.4 %copy-start.5 = (bf16[1,3584,128]{2,1,0:T(8,128)(2,1)S(1)}, bf16[1,3584,128]{2,1,0:T(8,128)(2,1)}, u32[]{:S(2)}) copy-start(bf16[1,3584,128]{2,1,0:T(8,128)(2,1)} %gate_ref.1) | copy-start | bytes 2752516
  44.8 10.4 %copy-start.6 = (bf16[1,3584,128]{2,1,0:T(8,128)(2,1)S(1)}, bf16[1,3584,128]{2,1,0:T(8,128)(2,1)}, u32[]{:S(2)}) copy-start(bf16[1,3584,128]{2,1,0:T(8,128)(2,1)} %up_ref.1) | copy-start | bytes 2752516
  44.8 45.8 %all-to-all-start.1 = ((bf16[32,16,896]{2,1,0:T(8,128)(2,1)}), bf16[32,16,896]{2,1,0:T(8,128)(2,1)S(1)}, u32[]{:S(2)}, u32[]{:S(2)}) async-start(bf16[32,16,896]{2,1,0:T(8,128)(2,1)} %bitcast.5), calls=%async_computation.1 | async-start | bytes 1835008 | tf_op jit(solution)/shard_map/all_to_all | solution.py:26
  55.5 31.0 %collective-permute-start = (bf16[896,256]{1,0:T(8,128)(2,1)S(1)}, bf16[896,256]{1,0:T(8,128)(2,1)S(1)}, u32[]{:S(2)}, u32[]{:S(2)}) collective-permute-start(bf16[896,256]{1,0:T(8,128)(2,1)S(1)} %get-tuple-element.10), channel_id=1, source_target_pairs={{0,1},{1,2},{2,3},{3,0},{4,5},{5,6},{6,7},{7,4},{8,9},{9,10},{10,1... | collective-permute-start | bytes 1376264 | tf_op jit(solution)/shard_map/ppermute | solution.py:30
  58.8 27.6 %collective-permute-start.1 = (bf16[896,256]{1,0:T(8,128)(2,1)S(1)}, bf16[896,256]{1,0:T(8,128)(2,1)S(1)}, u32[]{:S(2)}, u32[]{:S(2)}) collective-permute-start(bf16[896,256]{1,0:T(8,128)(2,1)S(1)} %get-tuple-element.11), channel_id=1, source_target_pairs={{0,2},{1,3},{2,0},{3,1},{4,6},{5,7},{6,4},{7,5},{8,10},{9,11},{10,... | collective-permute-start | bytes 1376264 | tf_op jit(solution)/shard_map/ppermute | solution.py:30
  61.6 29.1 %collective-permute-start.2 = (bf16[896,256]{1,0:T(8,128)(2,1)S(1)}, bf16[896,256]{1,0:T(8,128)(2,1)}, u32[]{:S(2)}, u32[]{:S(2)}) collective-permute-start(bf16[896,256]{1,0:T(8,128)(2,1)S(1)} %get-tuple-element.9), channel_id=1, source_target_pairs={{0,3},{1,0},{2,1},{3,2},{4,7},{5,4},{6,5},{7,6},{8,11},{9,8},{10,9... | collective-permute-start | bytes 1376264 | tf_op jit(solution)/shard_map/ppermute | solution.py:30
  65.9 41.7 %collective-permute-start.3 = (bf16[128,3584]{1,0:T(8,128)(2,1)}, bf16[128,3584]{1,0:T(8,128)(2,1)S(1)}, u32[]{:S(2)}, u32[]{:S(2)}) collective-permute-start(bf16[128,3584]{1,0:T(8,128)(2,1)} %bitcast.10.w0_ref), channel_id=1, source_target_pairs={{0,1},{1,2},{2,3},{3,0},{4,5},{5,6},{6,7},{7,4},{8,9},{9,10},{10,1... | collective-permute-start | bytes 2752520 | tf_op jit(solution)/shard_map/ppermute | solution.py:30
  67.9 43.2 %collective-permute-start.4 = (bf16[128,3584]{1,0:T(8,128)(2,1)}, bf16[128,3584]{1,0:T(8,128)(2,1)S(1)}, u32[]{:S(2)}, u32[]{:S(2)}) collective-permute-start(bf16[128,3584]{1,0:T(8,128)(2,1)} %bitcast.10.w0_ref), channel_id=1, source_target_pairs={{0,3},{1,0},{2,1},{3,2},{4,7},{5,4},{6,5},{7,6},{8,11},{9,8},{10,9... | collective-permute-start | bytes 2752520 | tf_op jit(solution)/shard_map/ppermute | solution.py:30
  86.4 4.2 %copy-start.8 = (bf16[896,256]{1,0:T(8,128)(2,1)}, bf16[896,256]{1,0:T(8,128)(2,1)S(1)}, u32[]{:S(2)}) copy-start(bf16[896,256]{1,0:T(8,128)(2,1)S(1)} %collective-permute-done.refs_0_) | copy-start | bytes 1376260
  86.4 0.8 copy-start.9
  95.2 36.1 %all-to-all-start.2 = ((bf16[4,128,1024]{2,1,0:T(8,128)(2,1)}), bf16[4,128,1024]{2,1,0:T(8,128)(2,1)S(1)}, u32[]{:S(2)}, u32[]{:S(2)}) async-start(bf16[4,128,1024]{2,1,0:T(8,128)(2,1)} %bitcast.36), calls=%async_computation.2 | async-start | bytes 2097152 | tf_op jit(solution)/shard_map/all_to_all | solution.py:26
  107.6 23.7 %copy-start.3 = (bf16[128,3584]{1,0:T(8,128)(2,1)}, bf16[128,3584]{1,0:T(8,128)(2,1)S(1)}, u32[]{:S(2)}) copy-start(bf16[128,3584]{1,0:T(8,128)(2,1)S(1)} %collective-permute-done.3.w1_ref) | copy-start | bytes 2752516
  107.6 19.7 %collective-permute-start.5 = (bf16[64,3584]{1,0:T(8,128)(2,1)S(1)}, bf16[64,3584]{1,0:T(8,128)(2,1)S(1)}, u32[]{:S(2)}, u32[]{:S(2)}) collective-permute-start(bf16[64,3584]{1,0:T(8,128)(2,1)S(1)} %slice.21), channel_id=1, source_target_pairs={{0,1},{1,2},{2,3},{3,0},{4,5},{5,6},{6,7},{7,4},{8,9},{9,10},{10,1... | collective-permute-start | bytes 1376264 | tf_op jit(solution)/shard_map/ppermute | solution.py:30
  111.0 20.3 %copy-start.4 = (bf16[128,3584]{1,0:T(8,128)(2,1)}, bf16[128,3584]{1,0:T(8,128)(2,1)S(1)}, u32[]{:S(2)}) copy-start(bf16[128,3584]{1,0:T(8,128)(2,1)S(1)} %collective-permute-done.4.w3_ref) | copy-start | bytes 2752516
  111.1 20.2 %collective-permute-start.6 = (bf16[64,3584]{1,0:T(8,128)(2,1)S(1)}, bf16[64,3584]{1,0:T(8,128)(2,1)}, u32[]{:S(2)}, u32[]{:S(2)}) collective-permute-start(bf16[64,3584]{1,0:T(8,128)(2,1)S(1)} %slice.22), channel_id=1, source_target_pairs={{0,3},{1,0},{2,1},{3,2},{4,7},{5,4},{6,5},{7,6},{8,11},{9,8},{10,9... | collective-permute-start | bytes 1376264 | tf_op jit(solution)/shard_map/ppermute | solution.py:30
  127.3 4.0 %copy-start.7 = (bf16[64,3584]{1,0:T(8,128)(2,1)}, bf16[64,3584]{1,0:T(8,128)(2,1)S(1)}, u32[]{:S(2)}) copy-start(bf16[64,3584]{1,0:T(8,128)(2,1)S(1)} %collective-permute-done.5.w2a_ref) | copy-start | bytes 1376260
  167.7 5.0 %copy-start.1 = (s32[8,4]{0,1:T(4,128)S(1)}, s32[8,4]{0,1:T(4,128)}, u32[]{:S(2)}) copy-start(s32[8,4]{0,1:T(4,128)} %param.7) | copy-start | bytes 388
  167.7 5.0 %copy-start.2 = (s32[8,4]{0,1:T(4,128)S(1)}, s32[8,4]{0,1:T(4,128)}, u32[]{:S(2)}) copy-start(s32[8,4]{0,1:T(4,128)} %param.8) | copy-start | bytes 388
  168.8 26.7 %all-to-all-start.4 = ((bf16[32,28,128]{2,1,0:T(8,128)(2,1)}), bf16[32,28,128]{2,1,0:T(8,128)(2,1)S(1)}, u32[]{:S(2)}, u32[]{:S(2)}) async-start(bf16[32,28,128]{2,1,0:T(8,128)(2,1)} %reshape.43), calls=%async_computation.4 | async-start | bytes 524288 | tf_op jit(solution)/shard_map/all_to_all | solution.py:26

commit v3 on v2

--- a/solution.py
+++ b/solution.py
@@ -39,18 +39,15 @@
     out_ref[...] = ids_ref[...] // MEMBERS
 
 
-def mix_kernel(target_ref, weights_ref, mix_ref):
-    node = lax.broadcasted_iota(i32, mix_ref.shape, 0)
-    mix = jnp.zeros(mix_ref.shape, f32)
+def mix_kernel(target_ref, weights_ref, out_ref):
+    tokens = target_ref.shape[1]
+    node = lax.broadcasted_iota(i32, (out_ref.shape[0], tokens), 0)
+    mix = jnp.zeros(node.shape, f32)
     for k in range(TOP):
         mix = mix + jnp.where(target_ref[k : k + 1, :] == node, weights_ref[k : k + 1, :], 0.0)
-    mix_ref[...] = mix
-
-
-def split_kernel(mix_ref, out_ref):
-    high = mix_ref[...].astype(bf16)
-    out_ref[:, : mix_ref.shape[1]] = high
-    out_ref[:, mix_ref.shape[1] :] = (mix_ref[...] - high.astype(f32)).astype(bf16)
+    high = mix.astype(bf16)
+    out_ref[:, :tokens] = high
+    out_ref[:, tokens:] = (mix - high.astype(f32)).astype(bf16)
 
 
 def slot_kernel(tag_ref, place_ref, spread_ref):
@@ -119,55 +116,27 @@
         send.wait()
 
 
-def down_kernel(xs, step, x_ref, share_ref, w0_ref, w1_ref, w3_ref, w2a_ref, w2b_ref, out_ref, share, hid, weights, out, share_sem, weight_sem, out_sem):
-    width = out_ref.shape[1]
-    half = LANES // 2
-    parts = 2
-    take = pltpu.make_async_copy(share_ref, share, share_sem)
-    take.start()
-    loads = []
-    for c in range(parts):
-        cols = slice(c * (width // parts), (c + 1) * (width // parts))
-        pieces = (
-            (w0_ref, weights.at[0]),
-            (w1_ref, weights.at[1]),
-            (w3_ref, weights.at[3]),
-            (w2a_ref, weights.at[2, :half]),
-            (w2b_ref, weights.at[2, half:]),
-        )
-        load = [
-            pltpu.make_async_copy(a.at[:, cols], b.at[:, cols], weight_sem.at[c * len(pieces) + i])
-            for i, (a, b) in enumerate(pieces)
-        ]
-        for copy in load:
-            copy.start()
-        loads.append(load)
+def down_kernel(xs, x_ref, share_ref, w0_ref, w1_ref, w3_ref, w2a_ref, w2b_ref, out_ref, hid_ref):
     x = x_ref[0]
-    take.wait()
-    both = share[0].astype(f32)
+    both = share_ref[0].astype(f32)
     for q in range(1, xs):
-        both = both + share[q].astype(f32)
+        both = both + share_ref[q].astype(f32)
     units = xs * LANES
-    hid[...] = (jax.nn.silu(both[:, :units]) * both[:, units:]).astype(bf16)
+    hid_ref[...] = (jax.nn.silu(both[:, :units]) * both[:, units:]).astype(bf16)
     mine = [
-        hid[:, pl.ds(pl.multiple_of(lax.rem(x - k + xs, xs) * LANES, LANES), LANES)]
+        hid_ref[:, pl.ds(pl.multiple_of(lax.rem(x - k + xs, xs) * LANES, LANES), LANES)]
         for k in range(xs)
     ]
-    sends = []
-    for i, n in enumerate(range(0, width, step)):
-        if n % (width // parts) == 0:
-            for copy in loads[n // (width // parts)]:
-                copy.wait()
+    half = LANES // 2
+    step = 512
+    for n in range(0, out_ref.shape[1], step):
         cols = slice(n, n + step)
-        total = jnp.dot(mine[0], weights[0, :, cols], preferred_element_type=f32)
-        for k in range(1, xs):
-            total += jnp.dot(mine[k], weights[k, :, cols], preferred_element_type=f32)
-        out[:, cols] = total.astype(bf16)
-        send = pltpu.make_async_copy(out.at[:, cols], out_ref.at[:, cols], out_sem.at[i])
-        send.start()
-        sends.append(send)
-    for send in sends:
-        send.wait()
+        total = jnp.dot(mine[0], w0_ref[:, cols], preferred_element_type=f32)
+        total += jnp.dot(mine[1], w1_ref[:, cols], preferred_element_type=f32)
+        total += jnp.dot(mine[3], w3_ref[:, cols], preferred_element_type=f32)
+        total += jnp.dot(mine[2][:, :half], w2a_ref[:, cols], preferred_element_type=f32)
+        total += jnp.dot(mine[2][:, half:], w2b_ref[:, cols], preferred_element_type=f32)
+        out_ref[:, cols] = total.astype(bf16)
 
 
 def held(arrays):
@@ -201,10 +170,12 @@
     pick = jnp.any(named, axis=2).astype(bf16)
     slot_member = jnp.sum(jnp.where(named, member[None], 0), axis=(1, 2))
     outgoing = jnp.dot(pick, tokens, preferred_element_type=f32).astype(bf16)
-    tag = jnp.broadcast_to(slot_member.astype(bf16)[:, None, None], (nodes, 4, LANES))
-    outgoing = jnp.concatenate([outgoing.reshape(nodes, width // LANES, LANES), tag], axis=1)
+    tag = jnp.broadcast_to(slot_member.astype(bf16)[:, None, None], (nodes, xs, LANES))
+    outgoing = jnp.concatenate([outgoing.reshape(nodes, xs, chunk), tag], axis=2)
     arrived = exchange(outgoing, NODE)
-    weights = small(weight_kernel, jax.ShapeDtypeStruct((TOP, token_count), f32), combine_codes.T)
+    weights = small(
+        weight_kernel, jax.ShapeDtypeStruct((TOP, token_count), f32), combine_codes.T
+    )
 
     joined = jnp.concatenate([gate_weight[0], up_weight[0]], axis=1)
     blocks = []
@@ -225,16 +196,15 @@
             jax.ShapeDtypeStruct((nodes, MEMBERS * CAP), bf16),
             jax.ShapeDtypeStruct((nodes, ys * CAP), bf16),
         ),
-        in_specs=[pl.BlockSpec((nodes, 8, LANES), lambda i: (0, arrived.shape[1] // 8 - 1, 0))],
+        in_specs=[pl.BlockSpec((nodes, xs, LANES), lambda i: (0, 0, chunk // LANES))],
         out_specs=(
             pl.BlockSpec((nodes, MEMBERS * CAP), lambda i: (0, 0)),
             pl.BlockSpec((nodes, ys * CAP), lambda i: (0, 0)),
         ),
         compiler_params=pltpu.CompilerParams(vmem_limit_bytes=1 << 20),
     )(arrived)
-    arrived = arrived[:, : width // LANES].reshape(nodes, width)
-    bundle = jnp.dot(place.T, arrived, preferred_element_type=f32).astype(bf16)
-    bundle = bundle.reshape(MEMBERS, 1, CAP, xs, chunk).transpose(3, 0, 1, 2, 4)
+    bundle = jnp.dot(place.T, arrived.reshape(nodes, -1), preferred_element_type=f32).astype(bf16)
+    bundle = bundle.reshape(MEMBERS, 1, CAP, xs, chunk + LANES)[..., :chunk].transpose(3, 0, 1, 2, 4)
     bundle = jnp.broadcast_to(bundle, (xs, MEMBERS, pair, CAP, chunk)).reshape(xs * ys, CAP, chunk)
     target = small(target_kernel, jax.ShapeDtypeStruct((TOP, token_count), i32), expert_ids.T)
     rows = exchange(bundle, LOCAL).reshape(xs * ys * CAP, chunk)
@@ -257,33 +227,22 @@
         cost_estimate=pl.CostEstimate(flops=2 << 30, bytes_accessed=4 << 20, transcendentals=0),
     )(x_arg, rows, *held((gate_weight, up_weight, *blocks)))
     share = exchange(share.reshape(xs, ys * CAP, 2 * xs * units), "x")
-    step = 256
-    out_shape = (ys * CAP, width)
     partial_out = pl.pallas_call(
-        functools.partial(down_kernel, xs, step),
-        out_shape=pltpu.HBM(out_shape, bf16),
-        in_specs=[SMEM, ANY] + [HBM] * 5,
-        out_specs=HBM,
-        scratch_shapes=[
-            pltpu.VMEM((xs, ys * CAP, 2 * xs * units), bf16),
-            pltpu.VMEM((ys * CAP, xs * units), bf16),
-            pltpu.VMEM((xs, units, width), bf16),
-            pltpu.VMEM(out_shape, bf16),
-            pltpu.SemaphoreType.DMA(()),
-            pltpu.SemaphoreType.DMA((10,)),
-            pltpu.SemaphoreType.DMA((width // step,)),
-        ],
-        compiler_params=pltpu.CompilerParams(vmem_limit_bytes=20 << 20),
+        functools.partial(down_kernel, xs),
+        out_shape=jax.ShapeDtypeStruct((ys * CAP, width), bf16),
+        in_specs=[SMEM] + [VMEM] * 6,
+        out_specs=VMEM,
+        scratch_shapes=[pltpu.VMEM((ys * CAP, xs * units), bf16)],
+        compiler_params=pltpu.CompilerParams(vmem_limit_bytes=16 << 20),
         cost_estimate=pl.CostEstimate(flops=1 << 30, bytes_accessed=6 << 20, transcendentals=1 << 16),
-    )(x_arg, share, *held((down, down_left, down_right, down_far_a, down_far_b)))
-    mix = small(
-        mix_kernel, jax.ShapeDtypeStruct((nodes, token_count), f32), target, weights
-    )
+    )(x_arg, share, down, down_left, down_right, down_far_a, down_far_b)
     returned = exchange(partial_out.reshape(ys, CAP, width), "y").reshape(ys * CAP, width)
 
     results = jnp.dot(spread, returned, preferred_element_type=f32).astype(bf16)
-    terms = small(split_kernel, jax.ShapeDtypeStruct((nodes, 2 * token_count), bf16), mix)
-    home = exchange(results.reshape(nodes, width // LANES, LANES), NODE).reshape(nodes, width)
+    terms = small(
+        mix_kernel, jax.ShapeDtypeStruct((nodes, 2 * token_count), bf16), target, weights
+    )
+    home = exchange(results.reshape(nodes, xs, chunk), NODE).reshape(nodes, width)
     mixed = jnp.dot(terms.T, home, preferred_element_type=f32)
     return (mixed[:token_count] + mixed[token_count:]).astype(bf16)
 

time: 197 us -> 197 us (level)
  local copies, waits for them, and re-layouts: 3.16 us -> 6.07 us
  waiting for transfers between devices: 66 us -> 63.7 us
    unnamed x20, local copies, waits for them, and re-layouts: 0.85 us -> 3.52 us
where the time goes in v3:
time: 197 us; the launch traced here: 196 us
  blocking collectives  74.1 us (38%)
  waiting for transfers between devices  63.7 us (32%)
  starting transfers between devices  41.3 us (21%)
  Pallas kernels  7.57 us (4%)
  local copies, waits for them, and re-layouts  6.07 us (3%)
    all_to_all x2, blocking collectives, exchange(): return lax.all_to_all(value, axes, split_axis=0, concat_axis=0, tiled=True)  74.1 us
    ppermute x7, waiting for transfers between devices, shift(): lax.ppermute(value, 'x', [(i, (i + by) % count) for i in range(count)])  42.5 us
    ppermute x7, starting transfers between devices, shift(): lax.ppermute(value, 'x', [(i, (i + by) % count) for i in range(count)])  22.2 us
    all_to_all x3, waiting for transfers between devices, exchange(): return lax.all_to_all(value, axes, split_axis=0, concat_axis=0, tiled=True)  21.2 us
    all_to_all x3, starting transfers between devices, exchange(): return lax.all_to_all(value, axes, split_axis=0, concat_axis=0, tiled=True)  19.1 us
    pallas_call x1, Pallas kernels, body(): pl.pallas_call(functools.partial(share_kernel, xs), out_shape=pltpu.HBM(s...  4.55 us
  transfers between devices with their start and end apart: 10, of which 6 were waited for; matrix products, arithmetic and copies ran while one was open for 0% of the time, Pallas kernels for 2%

profile of v3, /device:TPU:2, one launch (start us, length us, event | category | flops | bytes accessed | tf_op | source)
XLA Modules:
  0.0 195.8 jit_solution(16346744373748917510)
XLA Ops:
  0.0 0.7 add_select_fusion.1
  0.7 0.1 fusion.4
  0.8 0.1 select_reduce_fusion
  0.9 0.3 convolution_convert_fusion.2
  1.2 0.1 reshape.35
  1.2 0.1 broadcast_in_dim.33
  1.3 0.1 pad_maximum_fusion
  1.5 41.6 %all_to_all.25.tag_ref = bf16[32,4,1024]{2,1,0:T(4,128)(2,1)S(1)} all-to-all(bf16[32,4,1024]{2,1,0:T(4,128)(2,1)S(1)} %pad_maximum_fusion), channel_id=1, replica_groups=mesh['z'=16,'core'=2,'y'=8,'x'=4] {'z','core'}, dimensions={0} | all-to-all | bytes 524288 | tf_op jit(solution)/shard_map/all_to_all | solution.py:26
  43.1 0.1 copy.11
  43.2 0.3 shard_map.67
  43.4 0.3 convolution_convert_fusion
  43.7 0.4 reshape.37
  44.1 0.2 slice_bitcast_fusion
  44.3 0.1 copy.10
  44.4 1.0 broadcast_in_dim.36
  45.4 10.4 %all-to-all-start.1 = ((bf16[32,16,896]{2,1,0:T(8,128)(2,1)}), bf16[32,16,896]{2,1,0:T(8,128)(2,1)S(1)}, u32[]{:S(2)}, u32[]{:S(2)}) async-start(bf16[32,16,896]{2,1,0:T(8,128)(2,1)} %bitcast.5), calls=%async_computation.1 | async-start | bytes 1835008 | tf_op jit(solution)/shard_map/all_to_all | solution.py:26
  55.8 0.2 fusion
  56.0 3.4 %collective-permute-start = (bf16[896,256]{1,0:T(8,128)(2,1)S(1)}, bf16[896,256]{1,0:T(8,128)(2,1)S(1)}, u32[]{:S(2)}, u32[]{:S(2)}) collective-permute-start(bf16[896,256]{1,0:T(8,128)(2,1)S(1)} %get-tuple-element.10), channel_id=1, source_target_pairs={{0,1},{1,2},{2,3},{3,0},{4,5},{5,6},{6,7},{7,4},{8,9},{9,10},{10,1... | collective-permute-start | bytes 1376264 | tf_op jit(solution)/shard_map/ppermute | solution.py:30
  59.4 2.7 %collective-permute-start.1 = (bf16[896,256]{1,0:T(8,128)(2,1)S(1)}, bf16[896,256]{1,0:T(8,128)(2,1)S(1)}, u32[]{:S(2)}, u32[]{:S(2)}) collective-permute-start(bf16[896,256]{1,0:T(8,128)(2,1)S(1)} %get-tuple-element.11), channel_id=1, source_target_pairs={{0,2},{1,3},{2,0},{3,1},{4,6},{5,7},{6,4},{7,5},{8,10},{9,11},{10,... | collective-permute-start | bytes 1376264 | tf_op jit(solution)/shard_map/ppermute | solution.py:30
  62.1 4.3 %collective-permute-start.2 = (bf16[896,256]{1,0:T(8,128)(2,1)S(1)}, bf16[896,256]{1,0:T(8,128)(2,1)}, u32[]{:S(2)}, u32[]{:S(2)}) collective-permute-start(bf16[896,256]{1,0:T(8,128)(2,1)S(1)} %get-tuple-element.9), channel_id=1, source_target_pairs={{0,3},{1,0},{2,1},{3,2},{4,7},{5,4},{6,5},{7,6},{8,11},{9,8},{10,9... | collective-permute-start | bytes 1376264 | tf_op jit(solution)/shard_map/ppermute | solution.py:30
  66.5 1.9 collective-permute-start.3
  68.4 3.9 %collective-permute-start.4 = (bf16[128,3584]{1,0:T(8,128)(2,1)}, bf16[128,3584]{1,0:T(8,128)(2,1)S(1)}, u32[]{:S(2)}, u32[]{:S(2)}) collective-permute-start(bf16[128,3584]{1,0:T(8,128)(2,1)} %bitcast.10.w0_ref), channel_id=1, source_target_pairs={{0,3},{1,0},{2,1},{3,2},{4,7},{5,4},{6,5},{7,6},{8,11},{9,8},{10,9... | collective-permute-start | bytes 2752520 | tf_op jit(solution)/shard_map/ppermute | solution.py:30
  72.3 14.6 %collective-permute-done.refs_0_ = bf16[896,256]{1,0:T(8,128)(2,1)S(1)} collective-permute-done((bf16[896,256]{1,0:T(8,128)(2,1)S(1)}, bf16[896,256]{1,0:T(8,128)(2,1)S(1)}, u32[]{:S(2)}, u32[]{:S(2)}) %collective-permute-start) | collective-permute-done | bytes 458784 | tf_op jit(solution)/shard_map/ppermute | solution.py:30
  87.0 0.0 collective-permute-done.1.refs_1_
  87.0 0.8 copy-done.7
  87.8 0.8 copy-done.8
  88.5 2.7 %collective-permute-done.2.refs_2_ = bf16[896,256]{1,0:T(8,128)(2,1)} collective-permute-done((bf16[896,256]{1,0:T(8,128)(2,1)S(1)}, bf16[896,256]{1,0:T(8,128)(2,1)}, u32[]{:S(2)}, u32[]{:S(2)}) %collective-permute-start.2) | collective-permute-done | bytes 458784 | tf_op jit(solution)/shard_map/ppermute | solution.py:30
  91.2 0.0 all-to-all-done.1
  91.2 4.6 %shard_map.68 = bf16[512,1024]{1,0:T(8,128)(2,1)} custom-call(s32[1]{0:T(128)} %bitcast.2.x_ref, bf16[512,896]{1,0:T(8,128)(2,1)S(1)} %bitcast.29, bf16[1,3584,128]{2,1,0:T(8,128)(2,1)} %gate_ref.1, bf16[1,3584,128]{2,1,0:T(8,128)(2,1)} %up_ref.1, bf16[896,256]{1,0:T(8,128)(2,1)} %copy-done.7, bf16[896,256]{1,0:T(8,128)(2,1)} %copy-done.8, ...), custom_call_target="tpu_custom_call" | custom-call | flops 2147483648 | bytes 4194304 | tf_op jit(solution)/shard_map/pallas_call | solution.py:213
  95.8 4.8 %all-to-all-start.2 = ((bf16[4,128,1024]{2,1,0:T(8,128)(2,1)}), bf16[4,128,1024]{2,1,0:T(8,128)(2,1)S(1)}, u32[]{:S(2)}, u32[]{:S(2)}) async-start(bf16[4,128,1024]{2,1,0:T(8,128)(2,1)} %bitcast.34), calls=%async_computation.2 | async-start | bytes 2097152 | tf_op jit(solution)/shard_map/all_to_all | solution.py:26
  100.6 7.5 %collective-permute-done.3.w1_ref = bf16[128,3584]{1,0:T(8,128)(2,1)S(1)} collective-permute-done((bf16[128,3584]{1,0:T(8,128)(2,1)}, bf16[128,3584]{1,0:T(8,128)(2,1)S(1)}, u32[]{:S(2)}, u32[]{:S(2)}) %collective-permute-start.3) | collective-permute-done | bytes 917536 | tf_op jit(solution)/shard_map/ppermute | solution.py:30
  108.2 3.4 %collective-permute-start.5 = (bf16[64,3584]{1,0:T(8,128)(2,1)S(1)}, bf16[64,3584]{1,0:T(8,128)(2,1)S(1)}, u32[]{:S(2)}, u32[]{:S(2)}) collective-permute-start(bf16[64,3584]{1,0:T(8,128)(2,1)S(1)} %slice.21), channel_id=1, source_target_pairs={{0,1},{1,2},{2,3},{3,0},{4,5},{5,6},{6,7},{7,4},{8,9},{9,10},{10,1... | collective-permute-start | bytes 1376264 | tf_op jit(solution)/shard_map/ppermute | solution.py:30
  111.5 0.0 collective-permute-done.4.w3_ref
  111.6 2.5 %collective-permute-start.6 = (bf16[64,3584]{1,0:T(8,128)(2,1)S(1)}, bf16[64,3584]{1,0:T(8,128)(2,1)S(1)}, u32[]{:S(2)}, u32[]{:S(2)}) collective-permute-start(bf16[64,3584]{1,0:T(8,128)(2,1)S(1)} %slice.22), channel_id=1, source_target_pairs={{0,3},{1,0},{2,1},{3,2},{4,7},{5,4},{6,5},{7,6},{8,11},{9,8},{10,9... | collective-permute-start | bytes 1376264 | tf_op jit(solution)/shard_map/ppermute | solution.py:30
  114.1 13.8 %collective-permute-done.5.w2a_ref = bf16[64,3584]{1,0:T(8,128)(2,1)S(1)} collective-permute-done((bf16[64,3584]{1,0:T(8,128)(2,1)S(1)}, bf16[64,3584]{1,0:T(8,128)(2,1)S(1)}, u32[]{:S(2)}, u32[]{:S(2)}) %collective-permute-start.5) | collective-permute-done | bytes 458784 | tf_op jit(solution)/shard_map/ppermute | solution.py:30
  127.9 3.9 %collective-permute-done.6.w2b_ref = bf16[64,3584]{1,0:T(8,128)(2,1)S(1)} collective-permute-done((bf16[64,3584]{1,0:T(8,128)(2,1)S(1)}, bf16[64,3584]{1,0:T(8,128)(2,1)S(1)}, u32[]{:S(2)}, u32[]{:S(2)}) %collective-permute-start.6) | collective-permute-done | bytes 458784 | tf_op jit(solution)/shard_map/ppermute | solution.py:30
  131.7 0.8 copy-done.1
  132.5 0.0 all-to-all-done.2.share_ref
  132.5 1.0 copy-done.2
  133.6 2.7 %shard_map.69 = bf16[128,3584]{1,0:T(8,128)(2,1)S(1)} custom-call(s32[1]{0:T(128)} %bitcast.2.x_ref, bf16[4,128,1024]{2,1,0:T(8,128)(2,1)S(1)} %all-to-all-done.2.share_ref, bf16[128,3584]{1,0:T(8,128)(2,1)} %bitcast.10.w0_ref, bf16[128,3584]{1,0:T(8,128)(2,1)S(1)} %collective-permute-done.3.w1_ref, bf16[128,3584]{1,0:T(8,128)(2,1)S(1)} %collective-permute-done.4.w3_ref, ...), custom_call_target="tpu_custom_call" | custom-call | flops 1073741824 | bytes 6291456 | tf_op jit(solution)/shard_map/pallas_call | solution.py:230
  136.2 32.4 %all_to_all.26 = bf16[8,16,3584]{2,1,0:T(8,128)(2,1)S(1)} all-to-all(bf16[8,16,3584]{2,1,0:T(8,128)(2,1)S(1)} %bitcast.27), channel_id=1, replica_groups=mesh['z'=16,'core'=2,'y'=8,'x'=4] {'y'}, dimensions={0} | all-to-all | bytes 1835008 | tf_op jit(solution)/shard_map/all_to_all | solution.py:26
  168.6 0.2 convolution_convert_fusion.1
  168.9 0.7 reshape.43
  169.6 3.9 %all-to-all-start.4 = ((bf16[32,4,896]{2,1,0:T(4,128)(2,1)}), bf16[32,4,896]{2,1,0:T(4,128)(2,1)S(1)}, u32[]{:S(2)}, u32[]{:S(2)}) async-start(bf16[32,4,896]{2,1,0:T(4,128)(2,1)} %reshape.43), calls=%async_computation.4 | async-start | bytes 458752 | tf_op jit(solution)/shard_map/all_to_all | solution.py:26
  173.6 0.1 shard_map.66
  173.7 21.2 %all-to-all-done.4 = bf16[32,4,896]{2,1,0:T(4,128)(2,1)S(1)} async-done(((bf16[32,4,896]{2,1,0:T(4,128)(2,1)}), bf16[32,4,896]{2,1,0:T(4,128)(2,1)S(1)}, u32[]{:S(2)}, u32[]{:S(2)}) %all-to-all-start.4) | async-done | bytes 229408 | tf_op jit(solution)/shard_map/all_to_all | solution.py:26
  194.9 0.2 fusion.6
  195.1 0.6 fusion.3
  (20 shorter events, 0.1 us)
Async XLA Ops:
  0.0 0.9 copy-start
  45.4 10.4 %copy-start.5 = (bf16[1,3584,128]{2,1,0:T(8,128)(2,1)S(1)}, bf16[1,3584,128]{2,1,0:T(8,128)(2,1)}, u32[]{:S(2)}) copy-start(bf16[1,3584,128]{2,1,0:T(8,128)(2,1)} %gate_ref.1) | copy-start | bytes 2752516
  45.4 10.4 %copy-start.6 = (bf16[1,3584,128]{2,1,0:T(8,128)(2,1)S(1)}, bf16[1,3584,128]{2,1,0:T(8,128)(2,1)}, u32[]{:S(2)}) copy-start(bf16[1,3584,128]{2,1,0:T(8,128)(2,1)} %up_ref.1) | copy-start | bytes 2752516
  45.4 45.8 %all-to-all-start.1 = ((bf16[32,16,896]{2,1,0:T(8,128)(2,1)}), bf16[32,16,896]{2,1,0:T(8,128)(2,1)S(1)}, u32[]{:S(2)}, u32[]{:S(2)}) async-start(bf16[32,16,896]{2,1,0:T(8,128)(2,1)} %bitcast.5), calls=%async_computation.1 | async-start | bytes 1835008 | tf_op jit(solution)/shard_map/all_to_all | solution.py:26
  56.0 31.0 %collective-permute-start = (bf16[896,256]{1,0:T(8,128)(2,1)S(1)}, bf16[896,256]{1,0:T(8,128)(2,1)S(1)}, u32[]{:S(2)}, u32[]{:S(2)}) collective-permute-start(bf16[896,256]{1,0:T(8,128)(2,1)S(1)} %get-tuple-element.10), channel_id=1, source_target_pairs={{0,1},{1,2},{2,3},{3,0},{4,5},{5,6},{6,7},{7,4},{8,9},{9,10},{10,1... | collective-permute-start | bytes 1376264 | tf_op jit(solution)/shard_map/ppermute | solution.py:30
  59.4 27.6 %collective-permute-start.1 = (bf16[896,256]{1,0:T(8,128)(2,1)S(1)}, bf16[896,256]{1,0:T(8,128)(2,1)S(1)}, u32[]{:S(2)}, u32[]{:S(2)}) collective-permute-start(bf16[896,256]{1,0:T(8,128)(2,1)S(1)} %get-tuple-element.11), channel_id=1, source_target_pairs={{0,2},{1,3},{2,0},{3,1},{4,6},{5,7},{6,4},{7,5},{8,10},{9,11},{10,... | collective-permute-start | bytes 1376264 | tf_op jit(solution)/shard_map/ppermute | solution.py:30
  62.1 29.1 %collective-permute-start.2 = (bf16[896,256]{1,0:T(8,128)(2,1)S(1)}, bf16[896,256]{1,0:T(8,128)(2,1)}, u32[]{:S(2)}, u32[]{:S(2)}) collective-permute-start(bf16[896,256]{1,0:T(8,128)(2,1)S(1)} %get-tuple-element.9), channel_id=1, source_target_pairs={{0,3},{1,0},{2,1},{3,2},{4,7},{5,4},{6,5},{7,6},{8,11},{9,8},{10,9... | collective-permute-start | bytes 1376264 | tf_op jit(solution)/shard_map/ppermute | solution.py:30
  66.5 41.7 %collective-permute-start.3 = (bf16[128,3584]{1,0:T(8,128)(2,1)}, bf16[128,3584]{1,0:T(8,128)(2,1)S(1)}, u32[]{:S(2)}, u32[]{:S(2)}) collective-permute-start(bf16[128,3584]{1,0:T(8,128)(2,1)} %bitcast.10.w0_ref), channel_id=1, source_target_pairs={{0,1},{1,2},{2,3},{3,0},{4,5},{5,6},{6,7},{7,4},{8,9},{9,10},{10,1... | collective-permute-start | bytes 2752520 | tf_op jit(solution)/shard_map/ppermute | solution.py:30
  68.4 43.1 %collective-permute-start.4 = (bf16[128,3584]{1,0:T(8,128)(2,1)}, bf16[128,3584]{1,0:T(8,128)(2,1)S(1)}, u32[]{:S(2)}, u32[]{:S(2)}) collective-permute-start(bf16[128,3584]{1,0:T(8,128)(2,1)} %bitcast.10.w0_ref), channel_id=1, source_target_pairs={{0,3},{1,0},{2,1},{3,2},{4,7},{5,4},{6,5},{7,6},{8,11},{9,8},{10,9... | collective-permute-start | bytes 2752520 | tf_op jit(solution)/shard_map/ppermute | solution.py:30
  86.9 0.8 copy-start.7
  87.8 0.8 copy-start.8
  95.8 36.8 %all-to-all-start.2 = ((bf16[4,128,1024]{2,1,0:T(8,128)(2,1)}), bf16[4,128,1024]{2,1,0:T(8,128)(2,1)S(1)}, u32[]{:S(2)}, u32[]{:S(2)}) async-start(bf16[4,128,1024]{2,1,0:T(8,128)(2,1)} %bitcast.34), calls=%async_computation.2 | async-start | bytes 2097152 | tf_op jit(solution)/shard_map/all_to_all | solution.py:26
  108.2 19.7 %collective-permute-start.5 = (bf16[64,3584]{1,0:T(8,128)(2,1)S(1)}, bf16[64,3584]{1,0:T(8,128)(2,1)S(1)}, u32[]{:S(2)}, u32[]{:S(2)}) collective-permute-start(bf16[64,3584]{1,0:T(8,128)(2,1)S(1)} %slice.21), channel_id=1, source_target_pairs={{0,1},{1,2},{2,3},{3,0},{4,5},{5,6},{6,7},{7,4},{8,9},{9,10},{10,1... | collective-permute-start | bytes 1376264 | tf_op jit(solution)/shard_map/ppermute | solution.py:30
  111.6 20.1 %collective-permute-start.6 = (bf16[64,3584]{1,0:T(8,128)(2,1)S(1)}, bf16[64,3584]{1,0:T(8,128)(2,1)S(1)}, u32[]{:S(2)}, u32[]{:S(2)}) collective-permute-start(bf16[64,3584]{1,0:T(8,128)(2,1)S(1)} %slice.22), channel_id=1, source_target_pairs={{0,3},{1,0},{2,1},{3,2},{4,7},{5,4},{6,5},{7,6},{8,11},{9,8},{10,9... | collective-permute-start | bytes 1376264 | tf_op jit(solution)/shard_map/ppermute | solution.py:30
  131.7 0.8 copy-start.1
  132.5 1.0 copy-start.2
  168.6 4.9 %copy-start.3 = (s32[8,4]{0,1:T(4,128)S(1)}, s32[8,4]{0,1:T(4,128)}, u32[]{:S(2)}) copy-start(s32[8,4]{0,1:T(4,128)} %param.7) | copy-start | bytes 388
  168.6 4.9 %copy-start.4 = (s32[8,4]{0,1:T(4,128)S(1)}, s32[8,4]{0,1:T(4,128)}, u32[]{:S(2)}) copy-start(s32[8,4]{0,1:T(4,128)} %param.8) | copy-start | bytes 388
  169.6 25.3 %all-to-all-start.4 = ((bf16[32,4,896]{2,1,0:T(4,128)(2,1)}), bf16[32,4,896]{2,1,0:T(4,128)(2,1)S(1)}, u32[]{:S(2)}, u32[]{:S(2)}) async-start(bf16[32,4,896]{2,1,0:T(4,128)(2,1)} %reshape.43), calls=%async_computation.4 | async-start | bytes 458752 | tf_op jit(solution)/shard_map/all_to_all | solution.py:26

commit v4 on v3

--- a/solution.py
+++ b/solution.py
@@ -69,18 +69,12 @@
 
 
 def share_kernel(xs, x_ref, rows_ref, gate_ref, up_ref, *refs):
-    others, (out_ref, rows, weights, out, row_sem, weight_sem, out_sem) = refs[: xs - 1], refs[xs - 1 :]
+    others, (out_ref, weights, out, weight_sem, out_sem) = refs[: xs - 1], refs[xs - 1 :]
     x = x_ref[0]
     depth = weights.shape[1]
     mine = pl.ds(pl.multiple_of(x * depth, depth), depth)
-    parts = 2
+    parts = xs
     per = out_ref.shape[0] // parts
-    takes = [
-        pltpu.make_async_copy(
-            rows_ref.at[q * per : (q + 1) * per], rows.at[q * per : (q + 1) * per], row_sem.at[q]
-        )
-        for q in range(parts)
-    ]
     loads = [[pltpu.make_async_copy(ref, weights.at[k + 1], weight_sem.at[k])] for k, ref in enumerate(others)]
     loads.append(
         [
@@ -90,15 +84,12 @@
             for i, ref in enumerate((gate_ref, up_ref))
         ]
     )
-    takes[0].start()
     for load in loads:
         for copy in load:
             copy.start()
-    takes[1].start()
     sends = []
     for q in range(parts):
         at = slice(q * per, (q + 1) * per)
-        takes[q].wait()
         for load, k in zip(loads, (*range(1, xs), 0)):
             if q == 0:
                 for copy in load:
@@ -106,7 +97,7 @@
             source = lax.rem(x - k + xs, xs)
             gate_at = pl.multiple_of(source * LANES, LANES)
             up_at = pl.multiple_of((source + xs) * LANES, LANES)
-            part = jnp.dot(rows[at, :], weights[k], preferred_element_type=f32).astype(bf16)
+            part = jnp.dot(rows_ref[at, :], weights[k], preferred_element_type=f32).astype(bf16)
             out[at, pl.ds(gate_at, LANES)] = part[:, :LANES]
             out[at, pl.ds(up_at, LANES)] = part[:, LANES:]
         send = pltpu.make_async_copy(out.at[at], out_ref.at[at], out_sem.at[q])
@@ -173,9 +164,7 @@
     tag = jnp.broadcast_to(slot_member.astype(bf16)[:, None, None], (nodes, xs, LANES))
     outgoing = jnp.concatenate([outgoing.reshape(nodes, xs, chunk), tag], axis=2)
     arrived = exchange(outgoing, NODE)
-    weights = small(
-        weight_kernel, jax.ShapeDtypeStruct((TOP, token_count), f32), combine_codes.T
-    )
+    weights = small(weight_kernel, jax.ShapeDtypeStruct((TOP, token_count), f32), combine_codes.T)
 
     joined = jnp.concatenate([gate_weight[0], up_weight[0]], axis=1)
     blocks = []
@@ -206,6 +195,8 @@
     bundle = jnp.dot(place.T, arrived.reshape(nodes, -1), preferred_element_type=f32).astype(bf16)
     bundle = bundle.reshape(MEMBERS, 1, CAP, xs, chunk + LANES)[..., :chunk].transpose(3, 0, 1, 2, 4)
     bundle = jnp.broadcast_to(bundle, (xs, MEMBERS, pair, CAP, chunk)).reshape(xs * ys, CAP, chunk)
+    cores = lax.axis_size("core")
+    by_core = spread.reshape(nodes // cores, cores, -1).transpose(1, 0, 2).reshape(spread.shape)
     target = small(target_kernel, jax.ShapeDtypeStruct((TOP, token_count), i32), expert_ids.T)
     rows = exchange(bundle, LOCAL).reshape(xs * ys * CAP, chunk)
 
@@ -213,15 +204,13 @@
     share = pl.pallas_call(
         functools.partial(share_kernel, xs),
         out_shape=pltpu.HBM(share_shape, bf16),
-        in_specs=[SMEM, ANY] + [HBM] * (1 + xs),
+        in_specs=[SMEM, VMEM] + [HBM] * (1 + xs),
         out_specs=HBM,
         scratch_shapes=[
-            pltpu.VMEM((xs * ys * CAP, chunk), bf16),
             pltpu.VMEM((xs, chunk, 2 * units), bf16),
             pltpu.VMEM(share_shape, bf16),
-            pltpu.SemaphoreType.DMA((2,)),
             pltpu.SemaphoreType.DMA((xs + 1,)),
-            pltpu.SemaphoreType.DMA((2,)),
+            pltpu.SemaphoreType.DMA((xs,)),
         ],
         compiler_params=pltpu.CompilerParams(vmem_limit_bytes=20 << 20),
         cost_estimate=pl.CostEstimate(flops=2 << 30, bytes_accessed=4 << 20, transcendentals=0),
@@ -238,11 +227,11 @@
     )(x_arg, share, down, down_left, down_right, down_far_a, down_far_b)
     returned = exchange(partial_out.reshape(ys, CAP, width), "y").reshape(ys * CAP, width)
 
-    results = jnp.dot(spread, returned, preferred_element_type=f32).astype(bf16)
-    terms = small(
-        mix_kernel, jax.ShapeDtypeStruct((nodes, 2 * token_count), bf16), target, weights
-    )
-    home = exchange(results.reshape(nodes, xs, chunk), NODE).reshape(nodes, width)
+    results = jnp.dot(by_core, returned, preferred_element_type=f32).astype(bf16)
+    results = exchange(results.reshape(cores, nodes // cores, xs, chunk), "core")
+    results = results.transpose(1, 0, 2, 3)
+    terms = small(mix_kernel, jax.ShapeDtypeStruct((nodes, 2 * token_count), bf16), target, weights)
+    home = exchange(results, "z").reshape(nodes, width)
     mixed = jnp.dot(terms.T, home, preferred_element_type=f32)
     return (mixed[:token_count] + mixed[token_count:]).astype(bf16)
 

time: 197 us -> 197 us (level)
  the two profiles are of different devices: /device:TPU:2 before, /device:TPU:66 now
where the time goes in v4:
time: 197 us; the launch traced here: 196 us
  waiting for transfers between devices  85.6 us (43%)
  starting transfers between devices  50.5 us (26%)
  blocking collectives  43.2 us (22%)
  Pallas kernels  7.82 us (4%)
  local copies, waits for them, and re-layouts  6.12 us (3%)
    all_to_all x4, waiting for transfers between devices, exchange(): return lax.all_to_all(value, axes, split_axis=0, concat_axis=0, tiled=True)  43.8 us
    all_to_all x2, blocking collectives, exchange(): return lax.all_to_all(value, axes, split_axis=0, concat_axis=0, tiled=True)  43.2 us
    ppermute x7, waiting for transfers between devices, shift(): lax.ppermute(value, 'x', [(i, (i + by) % count) for i in range(count)])  41.8 us
    all_to_all x4, starting transfers between devices, exchange(): return lax.all_to_all(value, axes, split_axis=0, concat_axis=0, tiled=True)  28.4 us
    ppermute x7, starting transfers between devices, shift(): lax.ppermute(value, 'x', [(i, (i + by) % count) for i in range(count)])  22.2 us
  transfers between devices with their start and end apart: 11, of which 7 were waited for; matrix products, arithmetic and copies ran while one was open for 0% of the time, Pallas kernels for 2%

profile of v4, /device:TPU:66, one launch (start us, length us, event | category | flops | bytes accessed | tf_op | source)
XLA Modules:
  0.0 196.4 jit_solution(17514855389912619985)
XLA Ops:
  0.0 0.7 add_select_fusion.1
  0.7 0.1 fusion.4
  0.8 0.1 select_reduce_fusion
  0.9 0.3 convolution_convert_fusion.2
  1.2 0.1 reshape.41
  1.2 0.1 broadcast_in_dim.33
  1.3 0.1 pad_maximum_fusion
  1.5 39.3 %all_to_all.30.tag_ref = bf16[32,4,1024]{2,1,0:T(4,128)(2,1)S(1)} all-to-all(bf16[32,4,1024]{2,1,0:T(4,128)(2,1)S(1)} %pad_maximum_fusion), channel_id=1, replica_groups=mesh['z'=16,'core'=2,'y'=8,'x'=4] {'z','core'}, dimensions={0} | all-to-all | bytes 524288 | tf_op jit(solution)/shard_map/all_to_all | solution.py:26
  40.8 0.1 copy.28
  40.9 0.3 shard_map.67
  41.1 0.3 convolution_convert_fusion
  41.5 0.4 reshape.45
  41.8 0.2 slice_bitcast_fusion
  42.0 0.1 copy.26
  42.1 1.0 broadcast_in_dim.36
  43.1 10.4 %all-to-all-start.1 = ((bf16[32,16,896]{2,1,0:T(8,128)(2,1)}), bf16[32,16,896]{2,1,0:T(8,128)(2,1)S(1)}, u32[]{:S(2)}, u32[]{:S(2)}) async-start(bf16[32,16,896]{2,1,0:T(8,128)(2,1)} %bitcast.8), calls=%async_computation.1 | async-start | bytes 1835008 | tf_op jit(solution)/shard_map/all_to_all | solution.py:26
  53.5 0.2 fusion
  53.7 3.4 %collective-permute-start = (bf16[896,256]{1,0:T(8,128)(2,1)S(1)}, bf16[896,256]{1,0:T(8,128)(2,1)S(1)}, u32[]{:S(2)}, u32[]{:S(2)}) collective-permute-start(bf16[896,256]{1,0:T(8,128)(2,1)S(1)} %get-tuple-element.10), channel_id=1, source_target_pairs={{0,1},{1,2},{2,3},{3,0},{4,5},{5,6},{6,7},{7,4},{8,9},{9,10},{10,1... | collective-permute-start | bytes 1376264 | tf_op jit(solution)/shard_map/ppermute | solution.py:30
  57.1 2.7 %collective-permute-start.1 = (bf16[896,256]{1,0:T(8,128)(2,1)S(1)}, bf16[896,256]{1,0:T(8,128)(2,1)S(1)}, u32[]{:S(2)}, u32[]{:S(2)}) collective-permute-start(bf16[896,256]{1,0:T(8,128)(2,1)S(1)} %get-tuple-element.11), channel_id=1, source_target_pairs={{0,2},{1,3},{2,0},{3,1},{4,6},{5,7},{6,4},{7,5},{8,10},{9,11},{10,... | collective-permute-start | bytes 1376264 | tf_op jit(solution)/shard_map/ppermute | solution.py:30
  59.8 4.3 %collective-permute-start.2 = (bf16[896,256]{1,0:T(8,128)(2,1)S(1)}, bf16[896,256]{1,0:T(8,128)(2,1)}, u32[]{:S(2)}, u32[]{:S(2)}) collective-permute-start(bf16[896,256]{1,0:T(8,128)(2,1)S(1)} %get-tuple-element.9), channel_id=1, source_target_pairs={{0,3},{1,0},{2,1},{3,2},{4,7},{5,4},{6,5},{7,6},{8,11},{9,8},{10,9... | collective-permute-start | bytes 1376264 | tf_op jit(solution)/shard_map/ppermute | solution.py:30
  64.2 1.9 collective-permute-start.3
  66.1 3.9 %collective-permute-start.4 = (bf16[128,3584]{1,0:T(8,128)(2,1)}, bf16[128,3584]{1,0:T(8,128)(2,1)S(1)}, u32[]{:S(2)}, u32[]{:S(2)}) collective-permute-start(bf16[128,3584]{1,0:T(8,128)(2,1)} %bitcast.13.w0_ref), channel_id=1, source_target_pairs={{0,3},{1,0},{2,1},{3,2},{4,7},{5,4},{6,5},{7,6},{8,11},{9,8},{10,9... | collective-permute-start | bytes 2752520 | tf_op jit(solution)/shard_map/ppermute | solution.py:30
  70.0 14.4 %collective-permute-done.refs_0_ = bf16[896,256]{1,0:T(8,128)(2,1)S(1)} collective-permute-done((bf16[896,256]{1,0:T(8,128)(2,1)S(1)}, bf16[896,256]{1,0:T(8,128)(2,1)S(1)}, u32[]{:S(2)}, u32[]{:S(2)}) %collective-permute-start) | collective-permute-done | bytes 458784 | tf_op jit(solution)/shard_map/ppermute | solution.py:30
  84.4 0.8 copy-done.7
  85.2 0.8 copy-done.8
  86.0 2.0 %collective-permute-done.2.refs_2_ = bf16[896,256]{1,0:T(8,128)(2,1)} collective-permute-done((bf16[896,256]{1,0:T(8,128)(2,1)S(1)}, bf16[896,256]{1,0:T(8,128)(2,1)}, u32[]{:S(2)}, u32[]{:S(2)}) %collective-permute-start.2) | collective-permute-done | bytes 458784 | tf_op jit(solution)/shard_map/ppermute | solution.py:30
  88.0 3.9 %shard_map.68 = bf16[512,1024]{1,0:T(8,128)(2,1)} custom-call(s32[1]{0:T(128)} %bitcast.5.x_ref, bf16[512,896]{1,0:T(8,128)(2,1)S(1)} %bitcast.34, bf16[1,3584,128]{2,1,0:T(8,128)(2,1)} %gate_ref.1, bf16[1,3584,128]{2,1,0:T(8,128)(2,1)} %up_ref.1, bf16[896,256]{1,0:T(8,128)(2,1)} %copy-done.7, bf16[896,256]{1,0:T(8,128)(2,1)} %copy-done.8, ...), custom_call_target="tpu_custom_call" | custom-call | flops 2147483648 | bytes 4194304 | tf_op jit(solution)/shard_map/pallas_call | solution.py:204
  91.9 5.3 %all-to-all-start.2 = ((bf16[4,128,1024]{2,1,0:T(8,128)(2,1)}), bf16[4,128,1024]{2,1,0:T(8,128)(2,1)S(1)}, u32[]{:S(2)}, u32[]{:S(2)}) async-start(bf16[4,128,1024]{2,1,0:T(8,128)(2,1)} %bitcast.40), calls=%async_computation.2 | async-start | bytes 2097152 | tf_op jit(solution)/shard_map/all_to_all | solution.py:26
  97.2 8.4 %collective-permute-done.3.w1_ref = bf16[128,3584]{1,0:T(8,128)(2,1)S(1)} collective-permute-done((bf16[128,3584]{1,0:T(8,128)(2,1)}, bf16[128,3584]{1,0:T(8,128)(2,1)S(1)}, u32[]{:S(2)}, u32[]{:S(2)}) %collective-permute-start.3) | collective-permute-done | bytes 917536 | tf_op jit(solution)/shard_map/ppermute | solution.py:30
  105.6 3.4 %collective-permute-start.5 = (bf16[64,3584]{1,0:T(8,128)(2,1)S(1)}, bf16[64,3584]{1,0:T(8,128)(2,1)S(1)}, u32[]{:S(2)}, u32[]{:S(2)}) collective-permute-start(bf16[64,3584]{1,0:T(8,128)(2,1)S(1)} %slice.21), channel_id=1, source_target_pairs={{0,1},{1,2},{2,3},{3,0},{4,5},{5,6},{6,7},{7,4},{8,9},{9,10},{10,1... | collective-permute-start | bytes 1376264 | tf_op jit(solution)/shard_map/ppermute | solution.py:30
  109.1 2.5 %collective-permute-start.6 = (bf16[64,3584]{1,0:T(8,128)(2,1)S(1)}, bf16[64,3584]{1,0:T(8,128)(2,1)S(1)}, u32[]{:S(2)}, u32[]{:S(2)}) collective-permute-start(bf16[64,3584]{1,0:T(8,128)(2,1)S(1)} %slice.22), channel_id=1, source_target_pairs={{0,3},{1,0},{2,1},{3,2},{4,7},{5,4},{6,5},{7,6},{8,11},{9,8},{10,9... | collective-permute-start | bytes 1376264 | tf_op jit(solution)/shard_map/ppermute | solution.py:30
  111.6 13.5 %collective-permute-done.5.w2a_ref = bf16[64,3584]{1,0:T(8,128)(2,1)S(1)} collective-permute-done((bf16[64,3584]{1,0:T(8,128)(2,1)S(1)}, bf16[64,3584]{1,0:T(8,128)(2,1)S(1)}, u32[]{:S(2)}, u32[]{:S(2)}) %collective-permute-start.5) | collective-permute-done | bytes 458784 | tf_op jit(solution)/shard_map/ppermute | solution.py:30
  125.1 3.5 %collective-permute-done.6.w2b_ref = bf16[64,3584]{1,0:T(8,128)(2,1)S(1)} collective-permute-done((bf16[64,3584]{1,0:T(8,128)(2,1)S(1)}, bf16[64,3584]{1,0:T(8,128)(2,1)S(1)}, u32[]{:S(2)}, u32[]{:S(2)}) %collective-permute-start.6) | collective-permute-done | bytes 458784 | tf_op jit(solution)/shard_map/ppermute | solution.py:30
  128.5 0.8 copy-done.1
  129.3 1.0 copy-done.2
  130.3 3.6 %shard_map.69 = bf16[128,3584]{1,0:T(8,128)(2,1)} custom-call(s32[1]{0:T(128)} %bitcast.5.x_ref, bf16[4,128,1024]{2,1,0:T(8,128)(2,1)S(1)} %all-to-all-done.2.share_ref, bf16[128,3584]{1,0:T(8,128)(2,1)} %bitcast.13.w0_ref, bf16[128,3584]{1,0:T(8,128)(2,1)S(1)} %collective-permute-done.3.w1_ref, bf16[128,3584]{1,0:T(8,128)(2,1)S(1)} %collective-permute-done.4.w3_ref, ...), custom_call_target="tpu_custom_call" | custom-call | flops 1073741824 | bytes 6291456 | tf_op jit(solution)/shard_map/pallas_call | solution.py:219
  133.9 6.8 %all-to-all-start.3 = ((bf16[8,16,3584]{2,1,0:T(8,128)(2,1)}), bf16[8,16,3584]{2,1,0:T(8,128)(2,1)S(1)}, u32[]{:S(2)}, u32[]{:S(2)}) async-start(bf16[8,16,3584]{2,1,0:T(8,128)(2,1)} %bitcast.14), calls=%async_computation.3 | async-start | bytes 1835008 | tf_op jit(solution)/shard_map/all_to_all | solution.py:26
  140.7 26.1 %all-to-all-done.3 = bf16[8,16,3584]{2,1,0:T(8,128)(2,1)S(1)} async-done(((bf16[8,16,3584]{2,1,0:T(8,128)(2,1)}), bf16[8,16,3584]{2,1,0:T(8,128)(2,1)S(1)}, u32[]{:S(2)}, u32[]{:S(2)}) %all-to-all-start.3) | async-done | bytes 917536 | tf_op jit(solution)/shard_map/all_to_all | solution.py:26
  166.8 0.2 convolution_convert_fusion.1
  167.1 0.0 copy-start.3
  167.1 0.1 reshape.51
  167.1 3.9 %all_to_all.31 = bf16[2,16,4,896]{3,2,1,0:T(4,128)(2,1)S(1)} all-to-all(bf16[2,16,4,896]{3,2,1,0:T(4,128)(2,1)S(1)} %reshape.51), channel_id=1, replica_groups=mesh['z'=16,'core'=2,'y'=8,'x'=4] {'core'}, dimensions={0} | all-to-all | bytes 458752 | tf_op jit(solution)/shard_map/all_to_all | solution.py:26
  171.0 0.8 copy.27
  171.8 5.9 %all-to-all-start.5 = ((bf16[16,2,4,896]{3,2,1,0:T(4,128)(2,1)}), bf16[16,2,4,896]{3,2,1,0:T(4,128)(2,1)S(1)}, u32[]{:S(2)}, u32[]{:S(2)}) async-start(bf16[16,2,4,896]{3,2,1,0:T(4,128)(2,1)} %copy.27), calls=%async_computation.5 | async-start | bytes 458752 | tf_op jit(solution)/shard_map/all_to_all | solution.py:26
  177.8 0.1 shard_map.66
  177.9 17.7 %all-to-all-done.5 = bf16[16,2,4,896]{3,2,1,0:T(4,128)(2,1)S(1)} async-done(((bf16[16,2,4,896]{3,2,1,0:T(4,128)(2,1)}), bf16[16,2,4,896]{3,2,1,0:T(4,128)(2,1)S(1)}, u32[]{:S(2)}, u32[]{:S(2)}) %all-to-all-start.5) | async-done | bytes 229408 | tf_op jit(solution)/shard_map/all_to_all | solution.py:26
  195.6 0.2 fusion.6
  195.8 0.6 fusion.3
  (24 shorter events, 0.2 us)
Async XLA Ops:
  0.0 0.9 copy-start
  43.1 10.4 %copy-start.5 = (bf16[1,3584,128]{2,1,0:T(8,128)(2,1)S(1)}, bf16[1,3584,128]{2,1,0:T(8,128)(2,1)}, u32[]{:S(2)}) copy-start(bf16[1,3584,128]{2,1,0:T(8,128)(2,1)} %gate_ref.1) | copy-start | bytes 2752516
  43.1 10.4 %copy-start.6 = (bf16[1,3584,128]{2,1,0:T(8,128)(2,1)S(1)}, bf16[1,3584,128]{2,1,0:T(8,128)(2,1)}, u32[]{:S(2)}) copy-start(bf16[1,3584,128]{2,1,0:T(8,128)(2,1)} %up_ref.1) | copy-start | bytes 2752516
  43.1 45.0 %all-to-all-start.1 = ((bf16[32,16,896]{2,1,0:T(8,128)(2,1)}), bf16[32,16,896]{2,1,0:T(8,128)(2,1)S(1)}, u32[]{:S(2)}, u32[]{:S(2)}) async-start(bf16[32,16,896]{2,1,0:T(8,128)(2,1)} %bitcast.8), calls=%async_computation.1 | async-start | bytes 1835008 | tf_op jit(solution)/shard_map/all_to_all | solution.py:26
  53.7 30.8 %collective-permute-start = (bf16[896,256]{1,0:T(8,128)(2,1)S(1)}, bf16[896,256]{1,0:T(8,128)(2,1)S(1)}, u32[]{:S(2)}, u32[]{:S(2)}) collective-permute-start(bf16[896,256]{1,0:T(8,128)(2,1)S(1)} %get-tuple-element.10), channel_id=1, source_target_pairs={{0,1},{1,2},{2,3},{3,0},{4,5},{5,6},{6,7},{7,4},{8,9},{9,10},{10,1... | collective-permute-start | bytes 1376264 | tf_op jit(solution)/shard_map/ppermute | solution.py:30
  57.1 27.4 %collective-permute-start.1 = (bf16[896,256]{1,0:T(8,128)(2,1)S(1)}, bf16[896,256]{1,0:T(8,128)(2,1)S(1)}, u32[]{:S(2)}, u32[]{:S(2)}) collective-permute-start(bf16[896,256]{1,0:T(8,128)(2,1)S(1)} %get-tuple-element.11), channel_id=1, source_target_pairs={{0,2},{1,3},{2,0},{3,1},{4,6},{5,7},{6,4},{7,5},{8,10},{9,11},{10,... | collective-permute-start | bytes 1376264 | tf_op jit(solution)/shard_map/ppermute | solution.py:30
  59.8 28.2 %collective-permute-start.2 = (bf16[896,256]{1,0:T(8,128)(2,1)S(1)}, bf16[896,256]{1,0:T(8,128)(2,1)}, u32[]{:S(2)}, u32[]{:S(2)}) collective-permute-start(bf16[896,256]{1,0:T(8,128)(2,1)S(1)} %get-tuple-element.9), channel_id=1, source_target_pairs={{0,3},{1,0},{2,1},{3,2},{4,7},{5,4},{6,5},{7,6},{8,11},{9,8},{10,9... | collective-permute-start | bytes 1376264 | tf_op jit(solution)/shard_map/ppermute | solution.py:30
  64.2 41.4 %collective-permute-start.3 = (bf16[128,3584]{1,0:T(8,128)(2,1)}, bf16[128,3584]{1,0:T(8,128)(2,1)S(1)}, u32[]{:S(2)}, u32[]{:S(2)}) collective-permute-start(bf16[128,3584]{1,0:T(8,128)(2,1)} %bitcast.13.w0_ref), channel_id=1, source_target_pairs={{0,1},{1,2},{2,3},{3,0},{4,5},{5,6},{6,7},{7,4},{8,9},{9,10},{10,1... | collective-permute-start | bytes 2752520 | tf_op jit(solution)/shard_map/ppermute | solution.py:30
  66.1 42.9 %collective-permute-start.4 = (bf16[128,3584]{1,0:T(8,128)(2,1)}, bf16[128,3584]{1,0:T(8,128)(2,1)S(1)}, u32[]{:S(2)}, u32[]{:S(2)}) collective-permute-start(bf16[128,3584]{1,0:T(8,128)(2,1)} %bitcast.13.w0_ref), channel_id=1, source_target_pairs={{0,3},{1,0},{2,1},{3,2},{4,7},{5,4},{6,5},{7,6},{8,11},{9,8},{10,9... | collective-permute-start | bytes 2752520 | tf_op jit(solution)/shard_map/ppermute | solution.py:30
  84.4 0.8 copy-start.7
  85.2 0.8 copy-start.8
  91.9 37.4 %all-to-all-start.2 = ((bf16[4,128,1024]{2,1,0:T(8,128)(2,1)}), bf16[4,128,1024]{2,1,0:T(8,128)(2,1)S(1)}, u32[]{:S(2)}, u32[]{:S(2)}) async-start(bf16[4,128,1024]{2,1,0:T(8,128)(2,1)} %bitcast.40), calls=%async_computation.2 | async-start | bytes 2097152 | tf_op jit(solution)/shard_map/all_to_all | solution.py:26
  105.6 19.4 %collective-permute-start.5 = (bf16[64,3584]{1,0:T(8,128)(2,1)S(1)}, bf16[64,3584]{1,0:T(8,128)(2,1)S(1)}, u32[]{:S(2)}, u32[]{:S(2)}) collective-permute-start(bf16[64,3584]{1,0:T(8,128)(2,1)S(1)} %slice.21), channel_id=1, source_target_pairs={{0,1},{1,2},{2,3},{3,0},{4,5},{5,6},{6,7},{7,4},{8,9},{9,10},{10,1... | collective-permute-start | bytes 1376264 | tf_op jit(solution)/shard_map/ppermute | solution.py:30
  109.1 19.5 %collective-permute-start.6 = (bf16[64,3584]{1,0:T(8,128)(2,1)S(1)}, bf16[64,3584]{1,0:T(8,128)(2,1)S(1)}, u32[]{:S(2)}, u32[]{:S(2)}) collective-permute-start(bf16[64,3584]{1,0:T(8,128)(2,1)S(1)} %slice.22), channel_id=1, source_target_pairs={{0,3},{1,0},{2,1},{3,2},{4,7},{5,4},{6,5},{7,6},{8,11},{9,8},{10,9... | collective-permute-start | bytes 1376264 | tf_op jit(solution)/shard_map/ppermute | solution.py:30
  128.5 0.8 copy-start.1
  129.3 1.0 copy-start.2
  133.9 32.9 %all-to-all-start.3 = ((bf16[8,16,3584]{2,1,0:T(8,128)(2,1)}), bf16[8,16,3584]{2,1,0:T(8,128)(2,1)S(1)}, u32[]{:S(2)}, u32[]{:S(2)}) async-start(bf16[8,16,3584]{2,1,0:T(8,128)(2,1)} %bitcast.14), calls=%async_computation.3 | async-start | bytes 1835008 | tf_op jit(solution)/shard_map/all_to_all | solution.py:26
  167.1 10.7 %copy-start.3 = (s32[8,4]{0,1:T(4,128)S(1)}, s32[8,4]{0,1:T(4,128)}, u32[]{:S(2)}) copy-start(s32[8,4]{0,1:T(4,128)} %param.7) | copy-start | bytes 388
  167.1 10.7 %copy-start.4 = (s32[8,4]{0,1:T(4,128)S(1)}, s32[8,4]{0,1:T(4,128)}, u32[]{:S(2)}) copy-start(s32[8,4]{0,1:T(4,128)} %param.8) | copy-start | bytes 388
  171.8 23.8 %all-to-all-start.5 = ((bf16[16,2,4,896]{3,2,1,0:T(4,128)(2,1)}), bf16[16,2,4,896]{3,2,1,0:T(4,128)(2,1)S(1)}, u32[]{:S(2)}, u32[]{:S(2)}) async-start(bf16[16,2,4,896]{3,2,1,0:T(4,128)(2,1)} %copy.27), calls=%async_computation.5 | async-start | bytes 458752 | tf_op jit(solution)/shard_map/all_to_all | solution.py:26

commit v5 on v4

--- a/solution.py
+++ b/solution.py
@@ -19,7 +19,6 @@
 VMEM = pl.BlockSpec(memory_space=pltpu.VMEM)
 SMEM = pl.BlockSpec(memory_space=pltpu.SMEM)
 HBM = pl.BlockSpec(memory_space=pltpu.HBM)
-ANY = pl.BlockSpec(memory_space=pl.ANY)
 
 
 def exchange(value, axes):
@@ -50,9 +49,10 @@
     out_ref[:, tokens:] = (mix - high.astype(f32)).astype(bf16)
 
 
-def slot_kernel(tag_ref, place_ref, spread_ref):
-    tag = tag_ref[:, tag_ref.shape[1] - 1, :].astype(f32)
-    nodes = tag.shape[0]
+def place_kernel(pair, rows_ref, out_ref, spread_ref, bundle, sem):
+    xs, nodes, _ = rows_ref.shape
+    chunk = bundle.shape[-1]
+    tag = rows_ref[0, :, chunk:].astype(f32)
     row = lax.broadcasted_iota(i32, (nodes, nodes), 0)
     column = lax.broadcasted_iota(i32, (nodes, nodes), 1)
     earlier = jnp.where(column < row, 1.0, 0.0).astype(bf16)
@@ -60,12 +60,22 @@
     for m in range(MEMBERS):
         mark = jnp.where(tag == m, 1.0, 0.0)
         slot = slot + mark * jnp.dot(earlier, mark.astype(bf16), preferred_element_type=f32)
-    lane = lax.broadcasted_iota(i32, spread_ref.shape, 1)
-    pair = spread_ref.shape[1] // (MEMBERS * CAP)
+    lane = lax.broadcasted_iota(i32, slot.shape, 1)
+    place = jnp.where(slot == lane.astype(f32), 1.0, 0.0).astype(bf16)[:, : MEMBERS * CAP]
+    sends = []
+    for q in range(xs):
+        held_rows = lax.dot_general(
+            place, rows_ref[q, :, :chunk], (((0,), (0,)), ((), ())), preferred_element_type=f32
+        )
+        bundle[q] = held_rows.astype(bf16).reshape(MEMBERS, CAP, chunk)
+        for p in range(pair):
+            send = pltpu.make_async_copy(bundle.at[q], out_ref.at[q, :, p], sem.at[q * pair + p])
+            send.start()
+            sends.append(send)
     wanted = lane // (pair * CAP) * CAP + lane % CAP
     spread_ref[...] = jnp.where(slot == wanted.astype(f32), 1.0, 0.0).astype(bf16)
-    place = jnp.where(slot == lane.astype(f32), 1.0, 0.0).astype(bf16)
-    place_ref[...] = place[:, : place_ref.shape[1]]
+    for send in sends:
+        send.wait()
 
 
 def share_kernel(xs, x_ref, rows_ref, gate_ref, up_ref, *refs):
@@ -157,6 +167,7 @@
 
     target = expert_ids // MEMBERS
     member = expert_ids % MEMBERS
+    cores = lax.axis_size("core")
     named = target[None, :, :] == jnp.arange(nodes, dtype=i32)[:, None, None]
     pick = jnp.any(named, axis=2).astype(bf16)
     slot_member = jnp.sum(jnp.where(named, member[None], 0), axis=(1, 2))
@@ -178,24 +189,21 @@
     down_far_a = shift(down_left[:half], 1, xs)
     down_far_b = shift(down_right[half:], xs - 1, xs)
 
-    place, spread = pl.pallas_call(
-        slot_kernel,
-        grid=(1,),
+    bundle, spread = pl.pallas_call(
+        functools.partial(place_kernel, pair),
         out_shape=(
-            jax.ShapeDtypeStruct((nodes, MEMBERS * CAP), bf16),
+            pltpu.HBM((xs, MEMBERS, pair, CAP, chunk), bf16),
             jax.ShapeDtypeStruct((nodes, ys * CAP), bf16),
         ),
-        in_specs=[pl.BlockSpec((nodes, xs, LANES), lambda i: (0, 0, chunk // LANES))],
-        out_specs=(
-            pl.BlockSpec((nodes, MEMBERS * CAP), lambda i: (0, 0)),
-            pl.BlockSpec((nodes, ys * CAP), lambda i: (0, 0)),
-        ),
-        compiler_params=pltpu.CompilerParams(vmem_limit_bytes=1 << 20),
-    )(arrived)
-    bundle = jnp.dot(place.T, arrived.reshape(nodes, -1), preferred_element_type=f32).astype(bf16)
-    bundle = bundle.reshape(MEMBERS, 1, CAP, xs, chunk + LANES)[..., :chunk].transpose(3, 0, 1, 2, 4)
-    bundle = jnp.broadcast_to(bundle, (xs, MEMBERS, pair, CAP, chunk)).reshape(xs * ys, CAP, chunk)
-    cores = lax.axis_size("core")
+        in_specs=[VMEM],
+        out_specs=(HBM, VMEM),
+        scratch_shapes=[
+            pltpu.VMEM((xs, MEMBERS, CAP, chunk), bf16),
+            pltpu.SemaphoreType.DMA((xs * pair,)),
+        ],
+        compiler_params=pltpu.CompilerParams(vmem_limit_bytes=8 << 20),
+    )(arrived.transpose(1, 0, 2))
+    bundle = bundle.reshape(xs * ys, CAP, chunk)
     by_core = spread.reshape(nodes // cores, cores, -1).transpose(1, 0, 2).reshape(spread.shape)
     target = small(target_kernel, jax.ShapeDtypeStruct((TOP, token_count), i32), expert_ids.T)
     rows = exchange(bundle, LOCAL).reshape(xs * ys * CAP, chunk)
@@ -224,7 +232,7 @@
         scratch_shapes=[pltpu.VMEM((ys * CAP, xs * units), bf16)],
         compiler_params=pltpu.CompilerParams(vmem_limit_bytes=16 << 20),
         cost_estimate=pl.CostEstimate(flops=1 << 30, bytes_accessed=6 << 20, transcendentals=1 << 16),
-    )(x_arg, share, down, down_left, down_right, down_far_a, down_far_b)
+    )(x_arg, share, *held((down,)), down_left, down_right, down_far_a, down_far_b)
     returned = exchange(partial_out.reshape(ys, CAP, width), "y").reshape(ys * CAP, width)
 
     results = jnp.dot(by_core, returned, preferred_element_type=f32).astype(bf16)

time: 197 us -> 196 us (level)
  no operation moved by 1% of the time
where the time goes in v5:
time: 196 us
  waiting for transfers between devices  85.6 us (44%)
  starting transfers between devices  50.4 us (26%)
  blocking collectives  43.2 us (22%)
  Pallas kernels  8.92 us (5%)
  local copies, waits for them, and re-layouts  4.54 us (2%)
    all_to_all x4, waiting for transfers between devices, exchange(): return lax.all_to_all(value, axes, split_axis=0, concat_axis=0, tiled=True)  43.8 us
    all_to_all x2, blocking collectives, exchange(): return lax.all_to_all(value, axes, split_axis=0, concat_axis=0, tiled=True)  43.2 us
    ppermute x7, waiting for transfers between devices, shift(): lax.ppermute(value, 'x', [(i, (i + by) % count) for i in range(count)])  41.8 us
    all_to_all x4, starting transfers between devices, exchange(): return lax.all_to_all(value, axes, split_axis=0, concat_axis=0, tiled=True)  28.3 us
    ppermute x7, starting transfers between devices, shift(): lax.ppermute(value, 'x', [(i, (i + by) % count) for i in range(count)])  22.2 us
  transfers between devices with their start and end apart: 11, of which 7 were waited for; matrix products, arithmetic and copies ran while one was open for 0% of the time, Pallas kernels for 2%

profile of v5, /device:TPU:66, one launch (start us, length us, event | category | flops | bytes accessed | tf_op | source)
XLA Modules:
  0.0 195.5 jit_solution(10004717180482713849)
XLA Ops:
  0.0 0.7 add_select_fusion.1
  0.7 0.1 fusion.4
  0.8 0.1 select_reduce_fusion
  0.9 0.3 convolution_convert_fusion.1
  1.2 0.1 reshape.35
  1.2 0.1 broadcast_in_dim.26
  1.3 0.1 pad_maximum_fusion
  1.5 39.3 %all_to_all.30 = bf16[32,4,1024]{2,1,0:T(4,128)(2,1)S(1)} all-to-all(bf16[32,4,1024]{2,1,0:T(4,128)(2,1)S(1)} %pad_maximum_fusion), channel_id=1, replica_groups=mesh['z'=16,'core'=2,'y'=8,'x'=4] {'z','core'}, dimensions={0} | all-to-all | bytes 524288 | tf_op jit(solution)/shard_map/all_to_all | solution.py:25
  40.8 0.1 copy.29
  40.9 0.0 copy-start.5
  40.9 0.0 copy-start.6
  40.9 1.4 shard_map.67
  42.3 10.3 %all-to-all-start.1 = ((bf16[32,16,896]{2,1,0:T(8,128)(2,1)}), bf16[32,16,896]{2,1,0:T(8,128)(2,1)S(1)}, u32[]{:S(2)}, u32[]{:S(2)}) async-start(bf16[32,16,896]{2,1,0:T(8,128)(2,1)} %bitcast.36), calls=%async_computation.1 | async-start | bytes 1835008 | tf_op jit(solution)/shard_map/all_to_all | solution.py:25
  52.6 0.2 fusion
  52.7 3.4 %collective-permute-start = (bf16[896,256]{1,0:T(8,128)(2,1)S(1)}, bf16[896,256]{1,0:T(8,128)(2,1)S(1)}, u32[]{:S(2)}, u32[]{:S(2)}) collective-permute-start(bf16[896,256]{1,0:T(8,128)(2,1)S(1)} %get-tuple-element.10), channel_id=1, source_target_pairs={{0,1},{1,2},{2,3},{3,0},{4,5},{5,6},{6,7},{7,4},{8,9},{9,10},{10,1... | collective-permute-start | bytes 1376264 | tf_op jit(solution)/shard_map/ppermute | solution.py:29
  56.1 2.7 %collective-permute-start.1 = (bf16[896,256]{1,0:T(8,128)(2,1)S(1)}, bf16[896,256]{1,0:T(8,128)(2,1)S(1)}, u32[]{:S(2)}, u32[]{:S(2)}) collective-permute-start(bf16[896,256]{1,0:T(8,128)(2,1)S(1)} %get-tuple-element.11), channel_id=1, source_target_pairs={{0,2},{1,3},{2,0},{3,1},{4,6},{5,7},{6,4},{7,5},{8,10},{9,11},{10,... | collective-permute-start | bytes 1376264 | tf_op jit(solution)/shard_map/ppermute | solution.py:29
  58.9 4.3 %collective-permute-start.2 = (bf16[896,256]{1,0:T(8,128)(2,1)S(1)}, bf16[896,256]{1,0:T(8,128)(2,1)}, u32[]{:S(2)}, u32[]{:S(2)}) collective-permute-start(bf16[896,256]{1,0:T(8,128)(2,1)S(1)} %get-tuple-element.9), channel_id=1, source_target_pairs={{0,3},{1,0},{2,1},{3,2},{4,7},{5,4},{6,5},{7,6},{8,11},{9,8},{10,9... | collective-permute-start | bytes 1376264 | tf_op jit(solution)/shard_map/ppermute | solution.py:29
  63.2 1.9 collective-permute-start.3
  65.2 3.9 %collective-permute-start.4 = (bf16[128,3584]{1,0:T(8,128)(2,1)}, bf16[128,3584]{1,0:T(8,128)(2,1)S(1)}, u32[]{:S(2)}, u32[]{:S(2)}) collective-permute-start(bf16[128,3584]{1,0:T(8,128)(2,1)} %bitcast.12.w0_ref), channel_id=1, source_target_pairs={{0,3},{1,0},{2,1},{3,2},{4,7},{5,4},{6,5},{7,6},{8,11},{9,8},{10,9... | collective-permute-start | bytes 2752520 | tf_op jit(solution)/shard_map/ppermute | solution.py:29
  69.1 14.4 %collective-permute-done.refs_0_ = bf16[896,256]{1,0:T(8,128)(2,1)S(1)} collective-permute-done((bf16[896,256]{1,0:T(8,128)(2,1)S(1)}, bf16[896,256]{1,0:T(8,128)(2,1)S(1)}, u32[]{:S(2)}, u32[]{:S(2)}) %collective-permute-start) | collective-permute-done | bytes 458784 | tf_op jit(solution)/shard_map/ppermute | solution.py:29
  83.5 0.0 collective-permute-done.1.refs_1_
  83.5 0.8 copy-done.7
  84.3 0.8 copy-done.8
  85.1 2.0 %collective-permute-done.2.refs_2_ = bf16[896,256]{1,0:T(8,128)(2,1)} collective-permute-done((bf16[896,256]{1,0:T(8,128)(2,1)S(1)}, bf16[896,256]{1,0:T(8,128)(2,1)}, u32[]{:S(2)}, u32[]{:S(2)}) %collective-permute-start.2) | collective-permute-done | bytes 458784 | tf_op jit(solution)/shard_map/ppermute | solution.py:29
  87.1 0.0 all-to-all-done.1
  87.1 3.9 %shard_map.68 = bf16[512,1024]{1,0:T(8,128)(2,1)} custom-call(s32[1]{0:T(128)} %bitcast.6.x_ref, bf16[512,896]{1,0:T(8,128)(2,1)S(1)} %bitcast.29, bf16[1,3584,128]{2,1,0:T(8,128)(2,1)} %gate_ref.1, bf16[1,3584,128]{2,1,0:T(8,128)(2,1)} %up_ref.1, bf16[896,256]{1,0:T(8,128)(2,1)} %copy-done.7, bf16[896,256]{1,0:T(8,128)(2,1)} %copy-done.8, ...), custom_call_target="tpu_custom_call" | custom-call | flops 2147483648 | bytes 4194304 | tf_op jit(solution)/shard_map/pallas_call | solution.py:212
  91.0 5.3 %all-to-all-start.2 = ((bf16[4,128,1024]{2,1,0:T(8,128)(2,1)}), bf16[4,128,1024]{2,1,0:T(8,128)(2,1)S(1)}, u32[]{:S(2)}, u32[]{:S(2)}) async-start(bf16[4,128,1024]{2,1,0:T(8,128)(2,1)} %bitcast.34), calls=%async_computation.2 | async-start | bytes 2097152 | tf_op jit(solution)/shard_map/all_to_all | solution.py:25
  96.3 8.4 %collective-permute-done.3.w1_ref = bf16[128,3584]{1,0:T(8,128)(2,1)S(1)} collective-permute-done((bf16[128,3584]{1,0:T(8,128)(2,1)}, bf16[128,3584]{1,0:T(8,128)(2,1)S(1)}, u32[]{:S(2)}, u32[]{:S(2)}) %collective-permute-start.3) | collective-permute-done | bytes 917536 | tf_op jit(solution)/shard_map/ppermute | solution.py:29
  104.7 3.4 %collective-permute-start.5 = (bf16[64,3584]{1,0:T(8,128)(2,1)S(1)}, bf16[64,3584]{1,0:T(8,128)(2,1)S(1)}, u32[]{:S(2)}, u32[]{:S(2)}) collective-permute-start(bf16[64,3584]{1,0:T(8,128)(2,1)S(1)} %slice.16), channel_id=1, source_target_pairs={{0,1},{1,2},{2,3},{3,0},{4,5},{5,6},{6,7},{7,4},{8,9},{9,10},{10,1... | collective-permute-start | bytes 1376264 | tf_op jit(solution)/shard_map/ppermute | solution.py:29
  108.2 2.5 %collective-permute-start.6 = (bf16[64,3584]{1,0:T(8,128)(2,1)S(1)}, bf16[64,3584]{1,0:T(8,128)(2,1)S(1)}, u32[]{:S(2)}, u32[]{:S(2)}) collective-permute-start(bf16[64,3584]{1,0:T(8,128)(2,1)S(1)} %slice.17), channel_id=1, source_target_pairs={{0,3},{1,0},{2,1},{3,2},{4,7},{5,4},{6,5},{7,6},{8,11},{9,8},{10,9... | collective-permute-start | bytes 1376264 | tf_op jit(solution)/shard_map/ppermute | solution.py:29
  110.6 13.5 %collective-permute-done.5.w2a_ref = bf16[64,3584]{1,0:T(8,128)(2,1)S(1)} collective-permute-done((bf16[64,3584]{1,0:T(8,128)(2,1)S(1)}, bf16[64,3584]{1,0:T(8,128)(2,1)S(1)}, u32[]{:S(2)}, u32[]{:S(2)}) %collective-permute-start.5) | collective-permute-done | bytes 458784 | tf_op jit(solution)/shard_map/ppermute | solution.py:29
  124.1 3.5 %collective-permute-done.6.w2b_ref = bf16[64,3584]{1,0:T(8,128)(2,1)S(1)} collective-permute-done((bf16[64,3584]{1,0:T(8,128)(2,1)S(1)}, bf16[64,3584]{1,0:T(8,128)(2,1)S(1)}, u32[]{:S(2)}, u32[]{:S(2)}) %collective-permute-start.6) | collective-permute-done | bytes 458784 | tf_op jit(solution)/shard_map/ppermute | solution.py:29
  127.6 0.8 copy-done.1
  128.4 1.0 copy-done.2
  129.4 3.6 %shard_map.69 = bf16[128,3584]{1,0:T(8,128)(2,1)} custom-call(s32[1]{0:T(128)} %bitcast.6.x_ref, bf16[4,128,1024]{2,1,0:T(8,128)(2,1)S(1)} %all-to-all-done.2.share_ref, bf16[128,3584]{1,0:T(8,128)(2,1)} %bitcast.12.w0_ref, bf16[128,3584]{1,0:T(8,128)(2,1)S(1)} %collective-permute-done.3.w1_ref, bf16[128,3584]{1,0:T(8,128)(2,1)S(1)} %collective-permute-done.4.w3_ref, ...), custom_call_target="tpu_custom_call" | custom-call | flops 1073741824 | bytes 6291456 | tf_op jit(solution)/shard_map/pallas_call | solution.py:227
  133.0 6.8 %all-to-all-start.3 = ((bf16[8,16,3584]{2,1,0:T(8,128)(2,1)}), bf16[8,16,3584]{2,1,0:T(8,128)(2,1)S(1)}, u32[]{:S(2)}, u32[]{:S(2)}) async-start(bf16[8,16,3584]{2,1,0:T(8,128)(2,1)} %bitcast.13), calls=%async_computation.3 | async-start | bytes 1835008 | tf_op jit(solution)/shard_map/all_to_all | solution.py:25
  139.8 26.1 %all-to-all-done.3 = bf16[8,16,3584]{2,1,0:T(8,128)(2,1)S(1)} async-done(((bf16[8,16,3584]{2,1,0:T(8,128)(2,1)}), bf16[8,16,3584]{2,1,0:T(8,128)(2,1)S(1)}, u32[]{:S(2)}, u32[]{:S(2)}) %all-to-all-start.3) | async-done | bytes 917536 | tf_op jit(solution)/shard_map/all_to_all | solution.py:25
  165.9 0.2 convolution_convert_fusion
  166.1 0.0 copy-start.3
  166.1 0.0 copy-start.4
  166.1 0.1 reshape.43
  166.2 3.9 %all_to_all.31 = bf16[2,16,4,896]{3,2,1,0:T(4,128)(2,1)S(1)} all-to-all(bf16[2,16,4,896]{3,2,1,0:T(4,128)(2,1)S(1)} %reshape.43), channel_id=1, replica_groups=mesh['z'=16,'core'=2,'y'=8,'x'=4] {'core'}, dimensions={0} | all-to-all | bytes 458752 | tf_op jit(solution)/shard_map/all_to_all | solution.py:25
  170.1 0.8 copy.26
  170.9 5.9 %all-to-all-start.5 = ((bf16[16,2,4,896]{3,2,1,0:T(4,128)(2,1)}), bf16[16,2,4,896]{3,2,1,0:T(4,128)(2,1)S(1)}, u32[]{:S(2)}, u32[]{:S(2)}) async-start(bf16[16,2,4,896]{3,2,1,0:T(4,128)(2,1)} %copy.26), calls=%async_computation.5 | async-start | bytes 458752 | tf_op jit(solution)/shard_map/all_to_all | solution.py:25
  176.9 0.1 shard_map.66
  176.9 17.7 %all-to-all-done.5 = bf16[16,2,4,896]{3,2,1,0:T(4,128)(2,1)S(1)} async-done(((bf16[16,2,4,896]{3,2,1,0:T(4,128)(2,1)}), bf16[16,2,4,896]{3,2,1,0:T(4,128)(2,1)S(1)}, u32[]{:S(2)}, u32[]{:S(2)}) %all-to-all-start.5) | async-done | bytes 229408 | tf_op jit(solution)/shard_map/all_to_all | solution.py:25
  194.7 0.2 fusion.6
  194.9 0.6 fusion.3
  (19 shorter events, 0.1 us)
Async XLA Ops:
  0.0 0.9 copy-start
  40.9 11.7 %copy-start.5 = (bf16[1,3584,128]{2,1,0:T(8,128)(2,1)S(1)}, bf16[1,3584,128]{2,1,0:T(8,128)(2,1)}, u32[]{:S(2)}) copy-start(bf16[1,3584,128]{2,1,0:T(8,128)(2,1)} %gate_ref.1) | copy-start | bytes 2752516
  40.9 11.7 %copy-start.6 = (bf16[1,3584,128]{2,1,0:T(8,128)(2,1)S(1)}, bf16[1,3584,128]{2,1,0:T(8,128)(2,1)}, u32[]{:S(2)}) copy-start(bf16[1,3584,128]{2,1,0:T(8,128)(2,1)} %up_ref.1) | copy-start | bytes 2752516
  42.3 44.9 %all-to-all-start.1 = ((bf16[32,16,896]{2,1,0:T(8,128)(2,1)}), bf16[32,16,896]{2,1,0:T(8,128)(2,1)S(1)}, u32[]{:S(2)}, u32[]{:S(2)}) async-start(bf16[32,16,896]{2,1,0:T(8,128)(2,1)} %bitcast.36), calls=%async_computation.1 | async-start | bytes 1835008 | tf_op jit(solution)/shard_map/all_to_all | solution.py:25
  52.7 30.8 %collective-permute-start = (bf16[896,256]{1,0:T(8,128)(2,1)S(1)}, bf16[896,256]{1,0:T(8,128)(2,1)S(1)}, u32[]{:S(2)}, u32[]{:S(2)}) collective-permute-start(bf16[896,256]{1,0:T(8,128)(2,1)S(1)} %get-tuple-element.10), channel_id=1, source_target_pairs={{0,1},{1,2},{2,3},{3,0},{4,5},{5,6},{6,7},{7,4},{8,9},{9,10},{10,1... | collective-permute-start | bytes 1376264 | tf_op jit(solution)/shard_map/ppermute | solution.py:29
  56.1 27.4 %collective-permute-start.1 = (bf16[896,256]{1,0:T(8,128)(2,1)S(1)}, bf16[896,256]{1,0:T(8,128)(2,1)S(1)}, u32[]{:S(2)}, u32[]{:S(2)}) collective-permute-start(bf16[896,256]{1,0:T(8,128)(2,1)S(1)} %get-tuple-element.11), channel_id=1, source_target_pairs={{0,2},{1,3},{2,0},{3,1},{4,6},{5,7},{6,4},{7,5},{8,10},{9,11},{10,... | collective-permute-start | bytes 1376264 | tf_op jit(solution)/shard_map/ppermute | solution.py:29
  58.9 28.2 %collective-permute-start.2 = (bf16[896,256]{1,0:T(8,128)(2,1)S(1)}, bf16[896,256]{1,0:T(8,128)(2,1)}, u32[]{:S(2)}, u32[]{:S(2)}) collective-permute-start(bf16[896,256]{1,0:T(8,128)(2,1)S(1)} %get-tuple-element.9), channel_id=1, source_target_pairs={{0,3},{1,0},{2,1},{3,2},{4,7},{5,4},{6,5},{7,6},{8,11},{9,8},{10,9... | collective-permute-start | bytes 1376264 | tf_op jit(solution)/shard_map/ppermute | solution.py:29
  63.2 41.4 %collective-permute-start.3 = (bf16[128,3584]{1,0:T(8,128)(2,1)}, bf16[128,3584]{1,0:T(8,128)(2,1)S(1)}, u32[]{:S(2)}, u32[]{:S(2)}) collective-permute-start(bf16[128,3584]{1,0:T(8,128)(2,1)} %bitcast.12.w0_ref), channel_id=1, source_target_pairs={{0,1},{1,2},{2,3},{3,0},{4,5},{5,6},{6,7},{7,4},{8,9},{9,10},{10,1... | collective-permute-start | bytes 2752520 | tf_op jit(solution)/shard_map/ppermute | solution.py:29
  65.2 42.9 %collective-permute-start.4 = (bf16[128,3584]{1,0:T(8,128)(2,1)}, bf16[128,3584]{1,0:T(8,128)(2,1)S(1)}, u32[]{:S(2)}, u32[]{:S(2)}) collective-permute-start(bf16[128,3584]{1,0:T(8,128)(2,1)} %bitcast.12.w0_ref), channel_id=1, source_target_pairs={{0,3},{1,0},{2,1},{3,2},{4,7},{5,4},{6,5},{7,6},{8,11},{9,8},{10,9... | collective-permute-start | bytes 2752520 | tf_op jit(solution)/shard_map/ppermute | solution.py:29
  83.5 0.8 copy-start.7
  84.3 0.8 copy-start.8
  91.0 37.4 %all-to-all-start.2 = ((bf16[4,128,1024]{2,1,0:T(8,128)(2,1)}), bf16[4,128,1024]{2,1,0:T(8,128)(2,1)S(1)}, u32[]{:S(2)}, u32[]{:S(2)}) async-start(bf16[4,128,1024]{2,1,0:T(8,128)(2,1)} %bitcast.34), calls=%async_computation.2 | async-start | bytes 2097152 | tf_op jit(solution)/shard_map/all_to_all | solution.py:25
  104.7 19.4 %collective-permute-start.5 = (bf16[64,3584]{1,0:T(8,128)(2,1)S(1)}, bf16[64,3584]{1,0:T(8,128)(2,1)S(1)}, u32[]{:S(2)}, u32[]{:S(2)}) collective-permute-start(bf16[64,3584]{1,0:T(8,128)(2,1)S(1)} %slice.16), channel_id=1, source_target_pairs={{0,1},{1,2},{2,3},{3,0},{4,5},{5,6},{6,7},{7,4},{8,9},{9,10},{10,1... | collective-permute-start | bytes 1376264 | tf_op jit(solution)/shard_map/ppermute | solution.py:29
  108.2 19.5 %collective-permute-start.6 = (bf16[64,3584]{1,0:T(8,128)(2,1)S(1)}, bf16[64,3584]{1,0:T(8,128)(2,1)S(1)}, u32[]{:S(2)}, u32[]{:S(2)}) collective-permute-start(bf16[64,3584]{1,0:T(8,128)(2,1)S(1)} %slice.17), channel_id=1, source_target_pairs={{0,3},{1,0},{2,1},{3,2},{4,7},{5,4},{6,5},{7,6},{8,11},{9,8},{10,9... | collective-permute-start | bytes 1376264 | tf_op jit(solution)/shard_map/ppermute | solution.py:29
  127.6 0.8 copy-start.1
  128.4 1.0 copy-start.2
  133.0 32.9 %all-to-all-start.3 = ((bf16[8,16,3584]{2,1,0:T(8,128)(2,1)}), bf16[8,16,3584]{2,1,0:T(8,128)(2,1)S(1)}, u32[]{:S(2)}, u32[]{:S(2)}) async-start(bf16[8,16,3584]{2,1,0:T(8,128)(2,1)} %bitcast.13), calls=%async_computation.3 | async-start | bytes 1835008 | tf_op jit(solution)/shard_map/all_to_all | solution.py:25
  166.1 10.7 %copy-start.3 = (s32[8,4]{0,1:T(4,128)S(1)}, s32[8,4]{0,1:T(4,128)}, u32[]{:S(2)}) copy-start(s32[8,4]{0,1:T(4,128)} %param.7) | copy-start | bytes 388
  166.1 10.7 %copy-start.4 = (s32[8,4]{0,1:T(4,128)S(1)}, s32[8,4]{0,1:T(4,128)}, u32[]{:S(2)}) copy-start(s32[8,4]{0,1:T(4,128)} %param.8) | copy-start | bytes 388
  170.9 23.8 %all-to-all-start.5 = ((bf16[16,2,4,896]{3,2,1,0:T(4,128)(2,1)}), bf16[16,2,4,896]{3,2,1,0:T(4,128)(2,1)S(1)}, u32[]{:S(2)}, u32[]{:S(2)}) async-start(bf16[16,2,4,896]{3,2,1,0:T(4,128)(2,1)} %copy.26), calls=%async_computation.5 | async-start | bytes 458752 | tf_op jit(solution)/shard_map/all_to_all | solution.py:25

commit v6 on v5

--- a/solution.py
+++ b/solution.py
@@ -49,7 +49,7 @@
     out_ref[:, tokens:] = (mix - high.astype(f32)).astype(bf16)
 
 
-def place_kernel(pair, rows_ref, out_ref, spread_ref, bundle, sem):
+def place_kernel(pair, cores, rows_ref, out_ref, spread_ref, bundle, sem):
     xs, nodes, _ = rows_ref.shape
     chunk = bundle.shape[-1]
     tag = rows_ref[0, :, chunk:].astype(f32)
@@ -73,7 +73,10 @@
             send.start()
             sends.append(send)
     wanted = lane // (pair * CAP) * CAP + lane % CAP
-    spread_ref[...] = jnp.where(slot == wanted.astype(f32), 1.0, 0.0).astype(bf16)
+    spread = jnp.where(slot == wanted.astype(f32), 1.0, 0.0).astype(bf16)
+    by_core = row % (nodes // cores) * cores + row // (nodes // cores)
+    turn = jnp.where(column == by_core, 1.0, 0.0).astype(bf16)
+    spread_ref[...] = jnp.dot(turn, spread, preferred_element_type=f32).astype(bf16)
     for send in sends:
         send.wait()
 
@@ -190,7 +193,7 @@
     down_far_b = shift(down_right[half:], xs - 1, xs)
 
     bundle, spread = pl.pallas_call(
-        functools.partial(place_kernel, pair),
+        functools.partial(place_kernel, pair, cores),
         out_shape=(
             pltpu.HBM((xs, MEMBERS, pair, CAP, chunk), bf16),
             jax.ShapeDtypeStruct((nodes, ys * CAP), bf16),
@@ -204,7 +207,6 @@
         compiler_params=pltpu.CompilerParams(vmem_limit_bytes=8 << 20),
     )(arrived.transpose(1, 0, 2))
     bundle = bundle.reshape(xs * ys, CAP, chunk)
-    by_core = spread.reshape(nodes // cores, cores, -1).transpose(1, 0, 2).reshape(spread.shape)
     target = small(target_kernel, jax.ShapeDtypeStruct((TOP, token_count), i32), expert_ids.T)
     rows = exchange(bundle, LOCAL).reshape(xs * ys * CAP, chunk)
 
@@ -235,7 +237,7 @@
     )(x_arg, share, *held((down,)), down_left, down_right, down_far_a, down_far_b)
     returned = exchange(partial_out.reshape(ys, CAP, width), "y").reshape(ys * CAP, width)
 
-    results = jnp.dot(by_core, returned, preferred_element_type=f32).astype(bf16)
+    results = jnp.dot(spread, returned, preferred_element_type=f32).astype(bf16)
     results = exchange(results.reshape(cores, nodes // cores, xs, chunk), "core")
     results = results.transpose(1, 0, 2, 3)
     terms = small(mix_kernel, jax.ShapeDtypeStruct((nodes, 2 * token_count), bf16), target, weights)

time: 196 us -> 195 us (level)
  blocking collectives: 43.2 us -> 75.9 us
  waiting for transfers between devices: 85.6 us -> 59.5 us
  starting transfers between devices: 50.4 us -> 43.6 us
    all_to_all x2 -> x3, blocking collectives: 43.2 us -> 75.9 us  [exchange(): return lax.all_to_all(value, axes, split_axis=0, concat_axis=0, tiled=True)]
    all_to_all x4 -> x3, waiting for transfers between devices: 43.8 us -> 17.7 us  [exchange(): return lax.all_to_all(value, axes, split_axis=0, concat_axis=0, tiled=True)]
    all_to_all x4 -> x3, starting transfers between devices: 28.3 us -> 21.5 us  [exchange(): return lax.all_to_all(value, axes, split_axis=0, concat_axis=0, tiled=True)]
  transfers between devices with their start and end apart: 11 -> 10, of which waited for: 7 -> 6; matrix products, arithmetic and copies ran while one was open for 0% -> 0% of each run, Pallas kernels for 2% -> 2%
where the time goes in v6:
time: 195 us; the launch traced here: 194 us
  blocking collectives  75.9 us (39%)
  waiting for transfers between devices  59.5 us (31%)
  starting transfers between devices  43.6 us (22%)
  Pallas kernels  8 us (4%)
  local copies, waits for them, and re-layouts  4.56 us (2%)
    all_to_all x3, blocking collectives, exchange(): return lax.all_to_all(value, axes, split_axis=0, concat_axis=0, tiled=True)  75.9 us
    ppermute x7, waiting for transfers between devices, shift(): lax.ppermute(value, 'x', [(i, (i + by) % count) for i in range(count)])  41.8 us
    ppermute x7, starting transfers between devices, shift(): lax.ppermute(value, 'x', [(i, (i + by) % count) for i in range(count)])  22.2 us
    all_to_all x3, starting transfers between devices, exchange(): return lax.all_to_all(value, axes, split_axis=0, concat_axis=0, tiled=True)  21.5 us
    all_to_all x3, waiting for transfers between devices, exchange(): return lax.all_to_all(value, axes, split_axis=0, concat_axis=0, tiled=True)  17.7 us
  transfers between devices with their start and end apart: 10, of which 6 were waited for; matrix products, arithmetic and copies ran while one was open for 0% of the time, Pallas kernels for 2%

profile of v6, /device:TPU:66, one launch (start us, length us, event | category | flops | bytes accessed | tf_op | source)
XLA Modules:
  0.0 194.4 jit_solution(12400637130415140733)
XLA Ops:
  0.0 0.7 add_select_fusion.1
  0.7 0.1 fusion.4
  0.8 0.1 select_reduce_fusion
  0.9 0.3 convolution_convert_fusion.1
  1.2 0.1 reshape.29
  1.2 0.1 broadcast_in_dim.26
  1.3 0.1 pad_maximum_fusion
  1.5 39.3 %all_to_all.30 = bf16[32,4,1024]{2,1,0:T(4,128)(2,1)S(1)} all-to-all(bf16[32,4,1024]{2,1,0:T(4,128)(2,1)S(1)} %pad_maximum_fusion), channel_id=1, replica_groups=mesh['z'=16,'core'=2,'y'=8,'x'=4] {'z','core'}, dimensions={0} | all-to-all | bytes 524288 | tf_op jit(solution)/shard_map/all_to_all | solution.py:25
  40.8 0.1 copy.25
  40.9 0.0 copy-start.5
  40.9 0.0 copy-start.6
  40.9 1.4 shard_map.67
  42.3 10.3 %all-to-all-start.1 = ((bf16[32,16,896]{2,1,0:T(8,128)(2,1)}), bf16[32,16,896]{2,1,0:T(8,128)(2,1)S(1)}, u32[]{:S(2)}, u32[]{:S(2)}) async-start(bf16[32,16,896]{2,1,0:T(8,128)(2,1)} %bitcast.32), calls=%async_computation.1 | async-start | bytes 1835008 | tf_op jit(solution)/shard_map/all_to_all | solution.py:25
  52.6 0.2 fusion
  52.8 3.4 %collective-permute-start = (bf16[896,256]{1,0:T(8,128)(2,1)S(1)}, bf16[896,256]{1,0:T(8,128)(2,1)S(1)}, u32[]{:S(2)}, u32[]{:S(2)}) collective-permute-start(bf16[896,256]{1,0:T(8,128)(2,1)S(1)} %get-tuple-element.10), channel_id=1, source_target_pairs={{0,1},{1,2},{2,3},{3,0},{4,5},{5,6},{6,7},{7,4},{8,9},{9,10},{10,1... | collective-permute-start | bytes 1376264 | tf_op jit(solution)/shard_map/ppermute | solution.py:29
  56.1 2.7 %collective-permute-start.1 = (bf16[896,256]{1,0:T(8,128)(2,1)S(1)}, bf16[896,256]{1,0:T(8,128)(2,1)S(1)}, u32[]{:S(2)}, u32[]{:S(2)}) collective-permute-start(bf16[896,256]{1,0:T(8,128)(2,1)S(1)} %get-tuple-element.11), channel_id=1, source_target_pairs={{0,2},{1,3},{2,0},{3,1},{4,6},{5,7},{6,4},{7,5},{8,10},{9,11},{10,... | collective-permute-start | bytes 1376264 | tf_op jit(solution)/shard_map/ppermute | solution.py:29
  58.9 4.3 %collective-permute-start.2 = (bf16[896,256]{1,0:T(8,128)(2,1)S(1)}, bf16[896,256]{1,0:T(8,128)(2,1)}, u32[]{:S(2)}, u32[]{:S(2)}) collective-permute-start(bf16[896,256]{1,0:T(8,128)(2,1)S(1)} %get-tuple-element.9), channel_id=1, source_target_pairs={{0,3},{1,0},{2,1},{3,2},{4,7},{5,4},{6,5},{7,6},{8,11},{9,8},{10,9... | collective-permute-start | bytes 1376264 | tf_op jit(solution)/shard_map/ppermute | solution.py:29
  63.2 1.9 collective-permute-start.3
  65.2 3.9 %collective-permute-start.4 = (bf16[128,3584]{1,0:T(8,128)(2,1)}, bf16[128,3584]{1,0:T(8,128)(2,1)S(1)}, u32[]{:S(2)}, u32[]{:S(2)}) collective-permute-start(bf16[128,3584]{1,0:T(8,128)(2,1)} %bitcast.9.w0_ref), channel_id=1, source_target_pairs={{0,3},{1,0},{2,1},{3,2},{4,7},{5,4},{6,5},{7,6},{8,11},{9,8},{10,9... | collective-permute-start | bytes 2752520 | tf_op jit(solution)/shard_map/ppermute | solution.py:29
  69.1 14.4 %collective-permute-done.refs_0_ = bf16[896,256]{1,0:T(8,128)(2,1)S(1)} collective-permute-done((bf16[896,256]{1,0:T(8,128)(2,1)S(1)}, bf16[896,256]{1,0:T(8,128)(2,1)S(1)}, u32[]{:S(2)}, u32[]{:S(2)}) %collective-permute-start) | collective-permute-done | bytes 458784 | tf_op jit(solution)/shard_map/ppermute | solution.py:29
  83.5 0.0 collective-permute-done.1.refs_1_
  83.5 0.8 copy-done.7
  84.3 0.8 copy-done.8
  85.1 2.0 %collective-permute-done.2.refs_2_ = bf16[896,256]{1,0:T(8,128)(2,1)} collective-permute-done((bf16[896,256]{1,0:T(8,128)(2,1)S(1)}, bf16[896,256]{1,0:T(8,128)(2,1)}, u32[]{:S(2)}, u32[]{:S(2)}) %collective-permute-start.2) | collective-permute-done | bytes 458784 | tf_op jit(solution)/shard_map/ppermute | solution.py:29
  87.1 0.0 all-to-all-done.1
  87.1 3.9 %shard_map.68 = bf16[512,1024]{1,0:T(8,128)(2,1)} custom-call(s32[1]{0:T(128)} %bitcast.3.x_ref, bf16[512,896]{1,0:T(8,128)(2,1)S(1)} %bitcast.26, bf16[1,3584,128]{2,1,0:T(8,128)(2,1)} %gate_ref.1, bf16[1,3584,128]{2,1,0:T(8,128)(2,1)} %up_ref.1, bf16[896,256]{1,0:T(8,128)(2,1)} %copy-done.7, bf16[896,256]{1,0:T(8,128)(2,1)} %copy-done.8, ...), custom_call_target="tpu_custom_call" | custom-call | flops 2147483648 | bytes 4194304 | tf_op jit(solution)/shard_map/pallas_call | solution.py:214
  91.0 5.3 %all-to-all-start.2 = ((bf16[4,128,1024]{2,1,0:T(8,128)(2,1)}), bf16[4,128,1024]{2,1,0:T(8,128)(2,1)S(1)}, u32[]{:S(2)}, u32[]{:S(2)}) async-start(bf16[4,128,1024]{2,1,0:T(8,128)(2,1)} %bitcast.30), calls=%async_computation.2 | async-start | bytes 2097152 | tf_op jit(solution)/shard_map/all_to_all | solution.py:25
  96.3 8.4 %collective-permute-done.3.w1_ref = bf16[128,3584]{1,0:T(8,128)(2,1)S(1)} collective-permute-done((bf16[128,3584]{1,0:T(8,128)(2,1)}, bf16[128,3584]{1,0:T(8,128)(2,1)S(1)}, u32[]{:S(2)}, u32[]{:S(2)}) %collective-permute-start.3) | collective-permute-done | bytes 917536 | tf_op jit(solution)/shard_map/ppermute | solution.py:29
  104.7 3.4 %collective-permute-start.5 = (bf16[64,3584]{1,0:T(8,128)(2,1)S(1)}, bf16[64,3584]{1,0:T(8,128)(2,1)S(1)}, u32[]{:S(2)}, u32[]{:S(2)}) collective-permute-start(bf16[64,3584]{1,0:T(8,128)(2,1)S(1)} %slice.16), channel_id=1, source_target_pairs={{0,1},{1,2},{2,3},{3,0},{4,5},{5,6},{6,7},{7,4},{8,9},{9,10},{10,1... | collective-permute-start | bytes 1376264 | tf_op jit(solution)/shard_map/ppermute | solution.py:29
  108.1 0.0 collective-permute-done.4.w3_ref
  108.2 2.5 %collective-permute-start.6 = (bf16[64,3584]{1,0:T(8,128)(2,1)S(1)}, bf16[64,3584]{1,0:T(8,128)(2,1)S(1)}, u32[]{:S(2)}, u32[]{:S(2)}) collective-permute-start(bf16[64,3584]{1,0:T(8,128)(2,1)S(1)} %slice.17), channel_id=1, source_target_pairs={{0,3},{1,0},{2,1},{3,2},{4,7},{5,4},{6,5},{7,6},{8,11},{9,8},{10,9... | collective-permute-start | bytes 1376264 | tf_op jit(solution)/shard_map/ppermute | solution.py:29
  110.6 13.5 %collective-permute-done.5.w2a_ref = bf16[64,3584]{1,0:T(8,128)(2,1)S(1)} collective-permute-done((bf16[64,3584]{1,0:T(8,128)(2,1)S(1)}, bf16[64,3584]{1,0:T(8,128)(2,1)S(1)}, u32[]{:S(2)}, u32[]{:S(2)}) %collective-permute-start.5) | collective-permute-done | bytes 458784 | tf_op jit(solution)/shard_map/ppermute | solution.py:29
  124.1 3.5 %collective-permute-done.6.w2b_ref = bf16[64,3584]{1,0:T(8,128)(2,1)S(1)} collective-permute-done((bf16[64,3584]{1,0:T(8,128)(2,1)S(1)}, bf16[64,3584]{1,0:T(8,128)(2,1)S(1)}, u32[]{:S(2)}, u32[]{:S(2)}) %collective-permute-start.6) | collective-permute-done | bytes 458784 | tf_op jit(solution)/shard_map/ppermute | solution.py:29
  127.6 0.8 copy-done.1
  128.4 1.0 copy-done.2
  129.5 2.6 %shard_map.69 = bf16[128,3584]{1,0:T(8,128)(2,1)S(1)} custom-call(s32[1]{0:T(128)} %bitcast.3.x_ref, bf16[4,128,1024]{2,1,0:T(8,128)(2,1)S(1)} %all-to-all-done.2.share_ref, bf16[128,3584]{1,0:T(8,128)(2,1)} %bitcast.9.w0_ref, bf16[128,3584]{1,0:T(8,128)(2,1)S(1)} %collective-permute-done.3.w1_ref, bf16[128,3584]{1,0:T(8,128)(2,1)S(1)} %collective-permute-done.4.w3_ref, ...), custom_call_target="tpu_custom_call" | custom-call | flops 1073741824 | bytes 6291456 | tf_op jit(solution)/shard_map/pallas_call | solution.py:229
  132.1 32.7 %all_to_all.31 = bf16[8,16,3584]{2,1,0:T(8,128)(2,1)S(1)} all-to-all(bf16[8,16,3584]{2,1,0:T(8,128)(2,1)S(1)} %bitcast.24), channel_id=1, replica_groups=mesh['z'=16,'core'=2,'y'=8,'x'=4] {'y'}, dimensions={0} | all-to-all | bytes 1835008 | tf_op jit(solution)/shard_map/all_to_all | solution.py:25
  164.8 0.2 convolution_convert_fusion
  165.0 0.0 copy-start.3
  165.0 0.0 copy-start.4
  165.1 0.1 reshape.35
  165.1 3.9 %all_to_all.32 = bf16[2,16,4,896]{3,2,1,0:T(4,128)(2,1)S(1)} all-to-all(bf16[2,16,4,896]{3,2,1,0:T(4,128)(2,1)S(1)} %reshape.35), channel_id=1, replica_groups=mesh['z'=16,'core'=2,'y'=8,'x'=4] {'core'}, dimensions={0} | all-to-all | bytes 458752 | tf_op jit(solution)/shard_map/all_to_all | solution.py:25
  169.0 0.8 copy.22
  169.8 5.9 %all-to-all-start.5 = ((bf16[16,2,4,896]{3,2,1,0:T(4,128)(2,1)}), bf16[16,2,4,896]{3,2,1,0:T(4,128)(2,1)S(1)}, u32[]{:S(2)}, u32[]{:S(2)}) async-start(bf16[16,2,4,896]{3,2,1,0:T(4,128)(2,1)} %copy.22), calls=%async_computation.5 | async-start | bytes 458752 | tf_op jit(solution)/shard_map/all_to_all | solution.py:25
  175.8 0.1 shard_map.66
  175.8 17.7 %all-to-all-done.5 = bf16[16,2,4,896]{3,2,1,0:T(4,128)(2,1)S(1)} async-done(((bf16[16,2,4,896]{3,2,1,0:T(4,128)(2,1)}), bf16[16,2,4,896]{3,2,1,0:T(4,128)(2,1)S(1)}, u32[]{:S(2)}, u32[]{:S(2)}) %all-to-all-start.5) | async-done | bytes 229408 | tf_op jit(solution)/shard_map/all_to_all | solution.py:25
  193.6 0.2 fusion.6
  193.8 0.6 fusion.3
  (17 shorter events, 0.1 us)
Async XLA Ops:
  0.0 0.9 copy-start
  40.9 11.7 %copy-start.5 = (bf16[1,3584,128]{2,1,0:T(8,128)(2,1)S(1)}, bf16[1,3584,128]{2,1,0:T(8,128)(2,1)}, u32[]{:S(2)}) copy-start(bf16[1,3584,128]{2,1,0:T(8,128)(2,1)} %gate_ref.1) | copy-start | bytes 2752516
  40.9 11.7 %copy-start.6 = (bf16[1,3584,128]{2,1,0:T(8,128)(2,1)S(1)}, bf16[1,3584,128]{2,1,0:T(8,128)(2,1)}, u32[]{:S(2)}) copy-start(bf16[1,3584,128]{2,1,0:T(8,128)(2,1)} %up_ref.1) | copy-start | bytes 2752516
  42.3 44.9 %all-to-all-start.1 = ((bf16[32,16,896]{2,1,0:T(8,128)(2,1)}), bf16[32,16,896]{2,1,0:T(8,128)(2,1)S(1)}, u32[]{:S(2)}, u32[]{:S(2)}) async-start(bf16[32,16,896]{2,1,0:T(8,128)(2,1)} %bitcast.32), calls=%async_computation.1 | async-start | bytes 1835008 | tf_op jit(solution)/shard_map/all_to_all | solution.py:25
  52.8 30.8 %collective-permute-start = (bf16[896,256]{1,0:T(8,128)(2,1)S(1)}, bf16[896,256]{1,0:T(8,128)(2,1)S(1)}, u32[]{:S(2)}, u32[]{:S(2)}) collective-permute-start(bf16[896,256]{1,0:T(8,128)(2,1)S(1)} %get-tuple-element.10), channel_id=1, source_target_pairs={{0,1},{1,2},{2,3},{3,0},{4,5},{5,6},{6,7},{7,4},{8,9},{9,10},{10,1... | collective-permute-start | bytes 1376264 | tf_op jit(solution)/shard_map/ppermute | solution.py:29
  56.1 27.4 %collective-permute-start.1 = (bf16[896,256]{1,0:T(8,128)(2,1)S(1)}, bf16[896,256]{1,0:T(8,128)(2,1)S(1)}, u32[]{:S(2)}, u32[]{:S(2)}) collective-permute-start(bf16[896,256]{1,0:T(8,128)(2,1)S(1)} %get-tuple-element.11), channel_id=1, source_target_pairs={{0,2},{1,3},{2,0},{3,1},{4,6},{5,7},{6,4},{7,5},{8,10},{9,11},{10,... | collective-permute-start | bytes 1376264 | tf_op jit(solution)/shard_map/ppermute | solution.py:29
  58.9 28.2 %collective-permute-start.2 = (bf16[896,256]{1,0:T(8,128)(2,1)S(1)}, bf16[896,256]{1,0:T(8,128)(2,1)}, u32[]{:S(2)}, u32[]{:S(2)}) collective-permute-start(bf16[896,256]{1,0:T(8,128)(2,1)S(1)} %get-tuple-element.9), channel_id=1, source_target_pairs={{0,3},{1,0},{2,1},{3,2},{4,7},{5,4},{6,5},{7,6},{8,11},{9,8},{10,9... | collective-permute-start | bytes 1376264 | tf_op jit(solution)/shard_map/ppermute | solution.py:29
  63.2 41.5 %collective-permute-start.3 = (bf16[128,3584]{1,0:T(8,128)(2,1)}, bf16[128,3584]{1,0:T(8,128)(2,1)S(1)}, u32[]{:S(2)}, u32[]{:S(2)}) collective-permute-start(bf16[128,3584]{1,0:T(8,128)(2,1)} %bitcast.9.w0_ref), channel_id=1, source_target_pairs={{0,1},{1,2},{2,3},{3,0},{4,5},{5,6},{6,7},{7,4},{8,9},{9,10},{10,1... | collective-permute-start | bytes 2752520 | tf_op jit(solution)/shard_map/ppermute | solution.py:29
  65.2 42.9 %collective-permute-start.4 = (bf16[128,3584]{1,0:T(8,128)(2,1)}, bf16[128,3584]{1,0:T(8,128)(2,1)S(1)}, u32[]{:S(2)}, u32[]{:S(2)}) collective-permute-start(bf16[128,3584]{1,0:T(8,128)(2,1)} %bitcast.9.w0_ref), channel_id=1, source_target_pairs={{0,3},{1,0},{2,1},{3,2},{4,7},{5,4},{6,5},{7,6},{8,11},{9,8},{10,9... | collective-permute-start | bytes 2752520 | tf_op jit(solution)/shard_map/ppermute | solution.py:29
  83.5 0.8 copy-start.7
  84.3 0.8 copy-start.8
  91.0 37.4 %all-to-all-start.2 = ((bf16[4,128,1024]{2,1,0:T(8,128)(2,1)}), bf16[4,128,1024]{2,1,0:T(8,128)(2,1)S(1)}, u32[]{:S(2)}, u32[]{:S(2)}) async-start(bf16[4,128,1024]{2,1,0:T(8,128)(2,1)} %bitcast.30), calls=%async_computation.2 | async-start | bytes 2097152 | tf_op jit(solution)/shard_map/all_to_all | solution.py:25
  104.7 19.4 %collective-permute-start.5 = (bf16[64,3584]{1,0:T(8,128)(2,1)S(1)}, bf16[64,3584]{1,0:T(8,128)(2,1)S(1)}, u32[]{:S(2)}, u32[]{:S(2)}) collective-permute-start(bf16[64,3584]{1,0:T(8,128)(2,1)S(1)} %slice.16), channel_id=1, source_target_pairs={{0,1},{1,2},{2,3},{3,0},{4,5},{5,6},{6,7},{7,4},{8,9},{9,10},{10,1... | collective-permute-start | bytes 1376264 | tf_op jit(solution)/shard_map/ppermute | solution.py:29
  108.2 19.5 %collective-permute-start.6 = (bf16[64,3584]{1,0:T(8,128)(2,1)S(1)}, bf16[64,3584]{1,0:T(8,128)(2,1)S(1)}, u32[]{:S(2)}, u32[]{:S(2)}) collective-permute-start(bf16[64,3584]{1,0:T(8,128)(2,1)S(1)} %slice.17), channel_id=1, source_target_pairs={{0,3},{1,0},{2,1},{3,2},{4,7},{5,4},{6,5},{7,6},{8,11},{9,8},{10,9... | collective-permute-start | bytes 1376264 | tf_op jit(solution)/shard_map/ppermute | solution.py:29
  127.6 0.8 copy-start.1
  128.4 1.0 copy-start.2
  165.0 10.7 %copy-start.3 = (s32[8,4]{0,1:T(4,128)S(1)}, s32[8,4]{0,1:T(4,128)}, u32[]{:S(2)}) copy-start(s32[8,4]{0,1:T(4,128)} %param.7) | copy-start | bytes 388
  165.0 10.7 %copy-start.4 = (s32[8,4]{0,1:T(4,128)S(1)}, s32[8,4]{0,1:T(4,128)}, u32[]{:S(2)}) copy-start(s32[8,4]{0,1:T(4,128)} %param.8) | copy-start | bytes 388
  169.8 23.7 %all-to-all-start.5 = ((bf16[16,2,4,896]{3,2,1,0:T(4,128)(2,1)}), bf16[16,2,4,896]{3,2,1,0:T(4,128)(2,1)S(1)}, u32[]{:S(2)}, u32[]{:S(2)}) async-start(bf16[16,2,4,896]{3,2,1,0:T(4,128)(2,1)} %copy.22), calls=%async_computation.5 | async-start | bytes 458752 | tf_op jit(solution)/shard_map/all_to_all | solution.py:25

commit v7 on v6

--- a/solution.py
+++ b/solution.py
@@ -77,6 +77,35 @@
     by_core = row % (nodes // cores) * cores + row // (nodes // cores)
     turn = jnp.where(column == by_core, 1.0, 0.0).astype(bf16)
     spread_ref[...] = jnp.dot(turn, spread, preferred_element_type=f32).astype(bf16)
+    for send in sends:
+        send.wait()
+
+
+def block_kernel(xs, x_ref, gate_ref, up_ref, *refs):
+    outs, (buffer, load_sem, send_sem) = refs[: xs - 1], refs[xs - 1 :]
+    x = x_ref[0]
+    depth = buffer.shape[1]
+    loads = []
+    for k in range(1, xs):
+        rows = pl.ds(pl.multiple_of(lax.rem(x + k, xs) * depth, depth), depth)
+        loads.append(
+            [
+                pltpu.make_async_copy(
+                    ref.at[0, rows], buffer.at[k - 1, :, i * LANES : (i + 1) * LANES], load_sem.at[k - 1, i]
+                )
+                for i, ref in enumerate((gate_ref, up_ref))
+            ]
+        )
+    for load in loads:
+        for copy in load:
+            copy.start()
+    sends = []
+    for k, load in enumerate(loads):
+        for copy in load:
+            copy.wait()
+        send = pltpu.make_async_copy(buffer.at[k], outs[k], send_sem.at[k])
+        send.start()
+        sends.append(send)
     for send in sends:
         send.wait()
 
@@ -180,11 +209,22 @@
     arrived = exchange(outgoing, NODE)
     weights = small(weight_kernel, jax.ShapeDtypeStruct((TOP, token_count), f32), combine_codes.T)
 
-    joined = jnp.concatenate([gate_weight[0], up_weight[0]], axis=1)
+    quarters = pl.pallas_call(
+        functools.partial(block_kernel, xs),
+        out_shape=[pltpu.HBM((chunk, 2 * units), bf16)] * (xs - 1),
+        in_specs=[SMEM, HBM, HBM],
+        out_specs=[HBM] * (xs - 1),
+        scratch_shapes=[
+            pltpu.VMEM((xs - 1, chunk, 2 * units), bf16),
+            pltpu.SemaphoreType.DMA((xs - 1, 2)),
+            pltpu.SemaphoreType.DMA((xs - 1,)),
+        ],
+        compiler_params=pltpu.CompilerParams(vmem_limit_bytes=8 << 20),
+        cost_estimate=pl.CostEstimate(flops=1 << 20, bytes_accessed=3 << 20, transcendentals=0),
+    )(x_arg, *held((gate_weight, up_weight)))
     blocks = []
     for k in range(1, xs):
-        block = lax.dynamic_slice_in_dim(joined, lax.rem(x + k, xs) * chunk, chunk, 0)
-        blocks.append(shift(block, k, xs))
+        blocks.append(shift(quarters[k - 1], k, xs))
     down = down_weight[0]
     down_left = shift(down, 1, xs)
     down_right = shift(down, xs - 1, xs)

time: 195 us -> 196 us (level)
  Pallas kernels: 8 us -> 10.2 us
    pallas_call x0 -> x1, Pallas kernels: none -> 2.32 us  [body(): pl.pallas_call(functools.partial(block_kernel, xs), out_shape=[pltpu.HBM(...]
  transfers between devices with their start and end apart: 10 -> 10, of which waited for: 6 -> 6; matrix products, arithmetic and copies ran while one was open for 0% -> 0% of each run, Pallas kernels for 2% -> 3%
where the time goes in v7:
time: 196 us; the launch traced here: 195 us
  blocking collectives  75.2 us (38%)
  waiting for transfers between devices  58.5 us (30%)
  starting transfers between devices  44.5 us (23%)
  Pallas kernels  10.2 us (5%)
  local copies, waits for them, and re-layouts  4.49 us (2%)
    all_to_all x3, blocking collectives, exchange(): return lax.all_to_all(value, axes, split_axis=0, concat_axis=0, tiled=True)  75.2 us
    ppermute x7, waiting for transfers between devices, shift(): lax.ppermute(value, 'x', [(i, (i + by) % count) for i in range(count)])  41.4 us
    ppermute x7, starting transfers between devices, shift(): lax.ppermute(value, 'x', [(i, (i + by) % count) for i in range(count)])  22.3 us
    all_to_all x3, starting transfers between devices, exchange(): return lax.all_to_all(value, axes, split_axis=0, concat_axis=0, tiled=True)  22.2 us
    all_to_all x3, waiting for transfers between devices, exchange(): return lax.all_to_all(value, axes, split_axis=0, concat_axis=0, tiled=True)  17 us
  transfers between devices with their start and end apart: 10, of which 6 were waited for; matrix products, arithmetic and copies ran while one was open for 0% of the time, Pallas kernels for 3%

profile of v7, /device:TPU:66, one launch (start us, length us, event | category | flops | bytes accessed | tf_op | source)
XLA Modules:
  0.0 195.4 jit_solution(11739485431874969262)
XLA Ops:
  0.0 0.0 copy-start
  0.0 0.7 add_select_fusion.1
  0.7 0.1 fusion.1
  0.8 0.1 select_reduce_fusion
  0.9 0.0 copy-done
  0.9 0.3 convolution_convert_fusion.1
  1.2 0.1 reshape.29
  1.2 0.1 broadcast_in_dim.26
  1.3 0.1 pad_maximum_fusion
  1.5 39.3 %all_to_all.30 = bf16[32,4,1024]{2,1,0:T(4,128)(2,1)S(1)} all-to-all(bf16[32,4,1024]{2,1,0:T(4,128)(2,1)S(1)} %pad_maximum_fusion), channel_id=1, replica_groups=mesh['z'=16,'core'=2,'y'=8,'x'=4] {'z','core'}, dimensions={0} | all-to-all | bytes 524288 | tf_op jit(solution)/shard_map/all_to_all | solution.py:25
  40.8 0.1 copy.25
  40.9 1.3 shard_map.67
  42.2 10.3 %all-to-all-start.1 = ((bf16[32,16,896]{2,1,0:T(8,128)(2,1)}), bf16[32,16,896]{2,1,0:T(8,128)(2,1)S(1)}, u32[]{:S(2)}, u32[]{:S(2)}) async-start(bf16[32,16,896]{2,1,0:T(8,128)(2,1)} %bitcast.30), calls=%async_computation.1 | async-start | bytes 1835008 | tf_op jit(solution)/shard_map/all_to_all | solution.py:25
  52.5 2.3 %shard_map.68 = (bf16[896,256]{1,0:T(8,128)(2,1)}, bf16[896,256]{1,0:T(8,128)(2,1)}, bf16[896,256]{1,0:T(8,128)(2,1)}) custom-call(s32[1]{0:T(128)} %bitcast.3.x_ref, bf16[1,3584,128]{2,1,0:T(8,128)(2,1)} %gate_ref.3, bf16[1,3584,128]{2,1,0:T(8,128)(2,1)} %up_ref.3), custom_call_target="tpu_custom_call" | custom-call | flops 1048576 | bytes 3145728 | tf_op jit(solution)/shard_map/pallas_call | solution.py:212
  54.8 3.4 %collective-permute-start = (bf16[896,256]{1,0:T(8,128)(2,1)}, bf16[896,256]{1,0:T(8,128)(2,1)S(1)}, u32[]{:S(2)}, u32[]{:S(2)}) collective-permute-start(bf16[896,256]{1,0:T(8,128)(2,1)} %get-tuple-element.12), channel_id=1, source_target_pairs={{0,1},{1,2},{2,3},{3,0},{4,5},{5,6},{6,7},{7,4},{8,9},{9,10},{10,1... | collective-permute-start | bytes 1376264 | tf_op jit(solution)/shard_map/ppermute | solution.py:29
  58.2 2.7 %collective-permute-start.1 = (bf16[896,256]{1,0:T(8,128)(2,1)}, bf16[896,256]{1,0:T(8,128)(2,1)S(1)}, u32[]{:S(2)}, u32[]{:S(2)}) collective-permute-start(bf16[896,256]{1,0:T(8,128)(2,1)} %get-tuple-element.13), channel_id=1, source_target_pairs={{0,2},{1,3},{2,0},{3,1},{4,6},{5,7},{6,4},{7,5},{8,10},{9,11},{10,... | collective-permute-start | bytes 1376264 | tf_op jit(solution)/shard_map/ppermute | solution.py:29
  61.0 4.3 %collective-permute-start.2 = (bf16[896,256]{1,0:T(8,128)(2,1)}, bf16[896,256]{1,0:T(8,128)(2,1)}, u32[]{:S(2)}, u32[]{:S(2)}) collective-permute-start(bf16[896,256]{1,0:T(8,128)(2,1)} %get-tuple-element.14), channel_id=1, source_target_pairs={{0,3},{1,0},{2,1},{3,2},{4,7},{5,4},{6,5},{7,6},{8,11},{9,8},{10,9... | collective-permute-start | bytes 1376264 | tf_op jit(solution)/shard_map/ppermute | solution.py:29
  65.3 1.9 collective-permute-start.3
  67.3 3.9 %collective-permute-start.4 = (bf16[128,3584]{1,0:T(8,128)(2,1)}, bf16[128,3584]{1,0:T(8,128)(2,1)S(1)}, u32[]{:S(2)}, u32[]{:S(2)}) collective-permute-start(bf16[128,3584]{1,0:T(8,128)(2,1)} %bitcast.7.w0_ref), channel_id=1, source_target_pairs={{0,3},{1,0},{2,1},{3,2},{4,7},{5,4},{6,5},{7,6},{8,11},{9,8},{10,9... | collective-permute-start | bytes 2752520 | tf_op jit(solution)/shard_map/ppermute | solution.py:29
  71.2 13.7 %collective-permute-done.refs_0_ = bf16[896,256]{1,0:T(8,128)(2,1)S(1)} collective-permute-done((bf16[896,256]{1,0:T(8,128)(2,1)}, bf16[896,256]{1,0:T(8,128)(2,1)S(1)}, u32[]{:S(2)}, u32[]{:S(2)}) %collective-permute-start) | collective-permute-done | bytes 458784 | tf_op jit(solution)/shard_map/ppermute | solution.py:29
  84.9 0.0 collective-permute-done.1.refs_1_
  84.9 0.8 copy-done.6
  85.7 2.7 %collective-permute-done.2.refs_2_ = bf16[896,256]{1,0:T(8,128)(2,1)} collective-permute-done((bf16[896,256]{1,0:T(8,128)(2,1)}, bf16[896,256]{1,0:T(8,128)(2,1)}, u32[]{:S(2)}, u32[]{:S(2)}) %collective-permute-start.2) | collective-permute-done | bytes 458784 | tf_op jit(solution)/shard_map/ppermute | solution.py:29
  88.4 0.0 all-to-all-done.1
  88.4 3.8 %shard_map.69 = bf16[512,1024]{1,0:T(8,128)(2,1)} custom-call(s32[1]{0:T(128)} %bitcast.3.x_ref, bf16[512,896]{1,0:T(8,128)(2,1)S(1)} %bitcast.24, bf16[1,3584,128]{2,1,0:T(8,128)(2,1)} %gate_ref.3, bf16[1,3584,128]{2,1,0:T(8,128)(2,1)} %up_ref.3, bf16[896,256]{1,0:T(8,128)(2,1)} %copy-done.5, bf16[896,256]{1,0:T(8,128)(2,1)} %copy-done.6, ...), custom_call_target="tpu_custom_call" | custom-call | flops 2147483648 | bytes 4194304 | tf_op jit(solution)/shard_map/pallas_call | solution.py:254
  92.2 5.6 %all-to-all-start.2 = ((bf16[4,128,1024]{2,1,0:T(8,128)(2,1)}), bf16[4,128,1024]{2,1,0:T(8,128)(2,1)S(1)}, u32[]{:S(2)}, u32[]{:S(2)}) async-start(bf16[4,128,1024]{2,1,0:T(8,128)(2,1)} %bitcast.28), calls=%async_computation.2 | async-start | bytes 2097152 | tf_op jit(solution)/shard_map/all_to_all | solution.py:25
  97.7 8.2 %collective-permute-done.3.w1_ref = bf16[128,3584]{1,0:T(8,128)(2,1)S(1)} collective-permute-done((bf16[128,3584]{1,0:T(8,128)(2,1)}, bf16[128,3584]{1,0:T(8,128)(2,1)S(1)}, u32[]{:S(2)}, u32[]{:S(2)}) %collective-permute-start.3) | collective-permute-done | bytes 917536 | tf_op jit(solution)/shard_map/ppermute | solution.py:29
  106.0 3.4 %collective-permute-start.5 = (bf16[64,3584]{1,0:T(8,128)(2,1)S(1)}, bf16[64,3584]{1,0:T(8,128)(2,1)S(1)}, u32[]{:S(2)}, u32[]{:S(2)}) collective-permute-start(bf16[64,3584]{1,0:T(8,128)(2,1)S(1)} %slice.16), channel_id=1, source_target_pairs={{0,1},{1,2},{2,3},{3,0},{4,5},{5,6},{6,7},{7,4},{8,9},{9,10},{10,1... | collective-permute-start | bytes 1376264 | tf_op jit(solution)/shard_map/ppermute | solution.py:29
  109.4 0.0 collective-permute-done.4.w3_ref
  109.4 2.6 %collective-permute-start.6 = (bf16[64,3584]{1,0:T(8,128)(2,1)S(1)}, bf16[64,3584]{1,0:T(8,128)(2,1)S(1)}, u32[]{:S(2)}, u32[]{:S(2)}) collective-permute-start(bf16[64,3584]{1,0:T(8,128)(2,1)S(1)} %slice.17), channel_id=1, source_target_pairs={{0,3},{1,0},{2,1},{3,2},{4,7},{5,4},{6,5},{7,6},{8,11},{9,8},{10,9... | collective-permute-start | bytes 1376264 | tf_op jit(solution)/shard_map/ppermute | solution.py:29
  112.0 13.7 %collective-permute-done.5.w2a_ref = bf16[64,3584]{1,0:T(8,128)(2,1)S(1)} collective-permute-done((bf16[64,3584]{1,0:T(8,128)(2,1)S(1)}, bf16[64,3584]{1,0:T(8,128)(2,1)S(1)}, u32[]{:S(2)}, u32[]{:S(2)}) %collective-permute-start.5) | collective-permute-done | bytes 458784 | tf_op jit(solution)/shard_map/ppermute | solution.py:29
  125.8 3.1 %collective-permute-done.6.w2b_ref = bf16[64,3584]{1,0:T(8,128)(2,1)S(1)} collective-permute-done((bf16[64,3584]{1,0:T(8,128)(2,1)S(1)}, bf16[64,3584]{1,0:T(8,128)(2,1)S(1)}, u32[]{:S(2)}, u32[]{:S(2)}) %collective-permute-start.6) | collective-permute-done | bytes 458784 | tf_op jit(solution)/shard_map/ppermute | solution.py:29
  128.9 0.8 copy-done.1
  129.7 0.0 all-to-all-done.2.share_ref
  129.7 1.0 copy-done.2
  130.7 2.6 %shard_map.70 = bf16[128,3584]{1,0:T(8,128)(2,1)S(1)} custom-call(s32[1]{0:T(128)} %bitcast.3.x_ref, bf16[4,128,1024]{2,1,0:T(8,128)(2,1)S(1)} %all-to-all-done.2.share_ref, bf16[128,3584]{1,0:T(8,128)(2,1)} %bitcast.7.w0_ref, bf16[128,3584]{1,0:T(8,128)(2,1)S(1)} %collective-permute-done.3.w1_ref, bf16[128,3584]{1,0:T(8,128)(2,1)S(1)} %collective-permute-done.4.w3_ref, ...), custom_call_target="tpu_custom_call" | custom-call | flops 1073741824 | bytes 6291456 | tf_op jit(solution)/shard_map/pallas_call | solution.py:269
  133.4 32.0 %all_to_all.31 = bf16[8,16,3584]{2,1,0:T(8,128)(2,1)S(1)} all-to-all(bf16[8,16,3584]{2,1,0:T(8,128)(2,1)S(1)} %bitcast.22), channel_id=1, replica_groups=mesh['z'=16,'core'=2,'y'=8,'x'=4] {'y'}, dimensions={0} | all-to-all | bytes 1835008 | tf_op jit(solution)/shard_map/all_to_all | solution.py:25
  165.4 0.3 convolution_convert_fusion
  165.6 0.1 reshape.35
  165.7 3.9 %all_to_all.32 = bf16[2,16,4,896]{3,2,1,0:T(4,128)(2,1)S(1)} all-to-all(bf16[2,16,4,896]{3,2,1,0:T(4,128)(2,1)S(1)} %reshape.35), channel_id=1, replica_groups=mesh['z'=16,'core'=2,'y'=8,'x'=4] {'core'}, dimensions={0} | all-to-all | bytes 458752 | tf_op jit(solution)/shard_map/all_to_all | solution.py:25
  169.6 0.8 copy.22
  170.4 6.3 %all-to-all-start.5 = ((bf16[16,2,4,896]{3,2,1,0:T(4,128)(2,1)}), bf16[16,2,4,896]{3,2,1,0:T(4,128)(2,1)S(1)}, u32[]{:S(2)}, u32[]{:S(2)}) async-start(bf16[16,2,4,896]{3,2,1,0:T(4,128)(2,1)} %copy.22), calls=%async_computation.5 | async-start | bytes 458752 | tf_op jit(solution)/shard_map/all_to_all | solution.py:25
  176.7 0.0 copy-start.4
  176.8 0.7 copy-done.4
  177.4 0.1 shard_map.66
  177.5 17.0 %all-to-all-done.5 = bf16[16,2,4,896]{3,2,1,0:T(4,128)(2,1)S(1)} async-done(((bf16[16,2,4,896]{3,2,1,0:T(4,128)(2,1)}), bf16[16,2,4,896]{3,2,1,0:T(4,128)(2,1)S(1)}, u32[]{:S(2)}, u32[]{:S(2)}) %all-to-all-start.5) | async-done | bytes 229408 | tf_op jit(solution)/shard_map/all_to_all | solution.py:25
  194.6 0.2 fusion.3
  194.8 0.6 fusion
  (13 shorter events, 0.1 us)
Async XLA Ops:
  0.0 0.9 copy-start
  42.2 46.2 %all-to-all-start.1 = ((bf16[32,16,896]{2,1,0:T(8,128)(2,1)}), bf16[32,16,896]{2,1,0:T(8,128)(2,1)S(1)}, u32[]{:S(2)}, u32[]{:S(2)}) async-start(bf16[32,16,896]{2,1,0:T(8,128)(2,1)} %bitcast.30), calls=%async_computation.1 | async-start | bytes 1835008 | tf_op jit(solution)/shard_map/all_to_all | solution.py:25
  54.8 30.0 %collective-permute-start = (bf16[896,256]{1,0:T(8,128)(2,1)}, bf16[896,256]{1,0:T(8,128)(2,1)S(1)}, u32[]{:S(2)}, u32[]{:S(2)}) collective-permute-start(bf16[896,256]{1,0:T(8,128)(2,1)} %get-tuple-element.12), channel_id=1, source_target_pairs={{0,1},{1,2},{2,3},{3,0},{4,5},{5,6},{6,7},{7,4},{8,9},{9,10},{10,1... | collective-permute-start | bytes 1376264 | tf_op jit(solution)/shard_map/ppermute | solution.py:29
  58.2 26.7 %collective-permute-start.1 = (bf16[896,256]{1,0:T(8,128)(2,1)}, bf16[896,256]{1,0:T(8,128)(2,1)S(1)}, u32[]{:S(2)}, u32[]{:S(2)}) collective-permute-start(bf16[896,256]{1,0:T(8,128)(2,1)} %get-tuple-element.13), channel_id=1, source_target_pairs={{0,2},{1,3},{2,0},{3,1},{4,6},{5,7},{6,4},{7,5},{8,10},{9,11},{10,... | collective-permute-start | bytes 1376264 | tf_op jit(solution)/shard_map/ppermute | solution.py:29
  61.0 27.4 %collective-permute-start.2 = (bf16[896,256]{1,0:T(8,128)(2,1)}, bf16[896,256]{1,0:T(8,128)(2,1)}, u32[]{:S(2)}, u32[]{:S(2)}) collective-permute-start(bf16[896,256]{1,0:T(8,128)(2,1)} %get-tuple-element.14), channel_id=1, source_target_pairs={{0,3},{1,0},{2,1},{3,2},{4,7},{5,4},{6,5},{7,6},{8,11},{9,8},{10,9... | collective-permute-start | bytes 1376264 | tf_op jit(solution)/shard_map/ppermute | solution.py:29
  65.3 40.6 %collective-permute-start.3 = (bf16[128,3584]{1,0:T(8,128)(2,1)}, bf16[128,3584]{1,0:T(8,128)(2,1)S(1)}, u32[]{:S(2)}, u32[]{:S(2)}) collective-permute-start(bf16[128,3584]{1,0:T(8,128)(2,1)} %bitcast.7.w0_ref), channel_id=1, source_target_pairs={{0,1},{1,2},{2,3},{3,0},{4,5},{5,6},{6,7},{7,4},{8,9},{9,10},{10,1... | collective-permute-start | bytes 2752520 | tf_op jit(solution)/shard_map/ppermute | solution.py:29
  67.3 42.1 %collective-permute-start.4 = (bf16[128,3584]{1,0:T(8,128)(2,1)}, bf16[128,3584]{1,0:T(8,128)(2,1)S(1)}, u32[]{:S(2)}, u32[]{:S(2)}) collective-permute-start(bf16[128,3584]{1,0:T(8,128)(2,1)} %bitcast.7.w0_ref), channel_id=1, source_target_pairs={{0,3},{1,0},{2,1},{3,2},{4,7},{5,4},{6,5},{7,6},{8,11},{9,8},{10,9... | collective-permute-start | bytes 2752520 | tf_op jit(solution)/shard_map/ppermute | solution.py:29
  84.9 3.5 %copy-start.5 = (bf16[896,256]{1,0:T(8,128)(2,1)}, bf16[896,256]{1,0:T(8,128)(2,1)S(1)}, u32[]{:S(2)}) copy-start(bf16[896,256]{1,0:T(8,128)(2,1)S(1)} %collective-permute-done.refs_0_) | copy-start | bytes 1376260
  84.9 0.8 copy-start.6
  92.2 37.5 %all-to-all-start.2 = ((bf16[4,128,1024]{2,1,0:T(8,128)(2,1)}), bf16[4,128,1024]{2,1,0:T(8,128)(2,1)S(1)}, u32[]{:S(2)}, u32[]{:S(2)}) async-start(bf16[4,128,1024]{2,1,0:T(8,128)(2,1)} %bitcast.28), calls=%async_computation.2 | async-start | bytes 2097152 | tf_op jit(solution)/shard_map/all_to_all | solution.py:25
  106.0 19.8 %collective-permute-start.5 = (bf16[64,3584]{1,0:T(8,128)(2,1)S(1)}, bf16[64,3584]{1,0:T(8,128)(2,1)S(1)}, u32[]{:S(2)}, u32[]{:S(2)}) collective-permute-start(bf16[64,3584]{1,0:T(8,128)(2,1)S(1)} %slice.16), channel_id=1, source_target_pairs={{0,1},{1,2},{2,3},{3,0},{4,5},{5,6},{6,7},{7,4},{8,9},{9,10},{10,1... | collective-permute-start | bytes 1376264 | tf_op jit(solution)/shard_map/ppermute | solution.py:29
  109.4 19.5 %collective-permute-start.6 = (bf16[64,3584]{1,0:T(8,128)(2,1)S(1)}, bf16[64,3584]{1,0:T(8,128)(2,1)S(1)}, u32[]{:S(2)}, u32[]{:S(2)}) collective-permute-start(bf16[64,3584]{1,0:T(8,128)(2,1)S(1)} %slice.17), channel_id=1, source_target_pairs={{0,3},{1,0},{2,1},{3,2},{4,7},{5,4},{6,5},{7,6},{8,11},{9,8},{10,9... | collective-permute-start | bytes 1376264 | tf_op jit(solution)/shard_map/ppermute | solution.py:29
  128.9 0.8 copy-start.1
  129.7 1.0 copy-start.2
  170.4 6.3 %copy-start.3 = (s32[8,4]{0,1:T(4,128)S(1)}, s32[8,4]{0,1:T(4,128)}, u32[]{:S(2)}) copy-start(s32[8,4]{0,1:T(4,128)} %param.7) | copy-start | bytes 388
  170.4 24.2 %all-to-all-start.5 = ((bf16[16,2,4,896]{3,2,1,0:T(4,128)(2,1)}), bf16[16,2,4,896]{3,2,1,0:T(4,128)(2,1)S(1)}, u32[]{:S(2)}, u32[]{:S(2)}) async-start(bf16[16,2,4,896]{3,2,1,0:T(4,128)(2,1)} %copy.22), calls=%async_computation.5 | async-start | bytes 458752 | tf_op jit(solution)/shard_map/all_to_all | solution.py:25
  176.7 0.7 copy-start.4
